TPU v7x, 32 devices: a whole 2x2x4 slice. The times are simulated.
32 devices in a mesh: row: 4 (over z), col: 4 (over x, core), ch: 2 (over y).
Axes of the slice: x: 2, y: 2, z: 4, core: 2. Of those that a mesh axis runs over, the one named last changes fastest.
Arguments:
- image_tokens: bfloat16 [64, 1024, 128], P(('row', 'ch'), 'col'), may hold values from -61 to 61
- labels: int32 [64, 1024], P(('row', 'ch'), 'col'), may hold values from 0 to 2
- rel_index: int32 [64, 64], replicated, may hold values from 0 to 224
- norm_gain: float32 [2, 2, 128], replicated, may hold values from 0.25 to 1.75
- norm_shift: float32 [2, 2, 128], replicated, may hold values from -1.5 to 1.5
- qkv_weight: bfloat16 [2, 3, 128, 128], P(None, None, None, 'ch'), may hold values from -5 to 5
- qkv_bias: float32 [2, 3, 128], P(None, None, 'ch'), may hold values from -1.5 to 1.5
- bias_table: float32 [2, 225, 4], P(None, None, 'ch'), may hold values from -4 to 4
- proj_weight: bfloat16 [2, 128, 128], P(None, 'ch'), may hold values from -0.5 to 0.5
- proj_bias: float32 [2, 128], replicated, may hold values from -1.5 to 1.5
- fc1_weight: bfloat16 [2, 128, 512], P(None, None, 'ch'), may hold values from -0.5 to 0.5
- fc1_bias: float32 [2, 512], P(None, 'ch'), may hold values from -2.5 to 2.5
- fc2_weight: bfloat16 [2, 512, 128], P(None, 'ch'), may hold values from -0.25 to 0.25
- fc2_bias: float32 [2, 128], replicated, may hold values from -1.5 to 1.5
Outputs:
- encoded: bfloat16 [64, 1024, 128], P(('row', 'ch'), 'col')
All inputs are finite; a program needn't handle non-finite values.
Results may differ from a plain program's by a relative error of at most 0.014.
Values may be sent and summed in bfloat16 or wider, within the bound.
No kernel may reach another device: no remote copies, remote signals or barrier semaphores. Data moves between devices by JAX's collectives and lax.ppermute only.
A program may use at most 128 MiB of HBM per device.

v0:
```python
import math

import jax
import jax.numpy as jnp
from jax import lax
from jax.experimental import pallas as pl
from jax.experimental.pallas import tpu as pltpu
from jax.sharding import PartitionSpec as P

WIN = 8
SHIFT = 4
EPS = 1e-05
NEG = -1e30
LOG2E = math.log2(math.e)
BF = jnp.bfloat16
F32 = jnp.float32


def dot_nt(a, b):
    return lax.dot_general(a, b, (((1,), (1,)), ((), ())), preferred_element_type=F32)


def dot_nn(a, b):
    return lax.dot_general(a, b, (((1,), (0,)), ((), ())), preferred_element_type=F32)


def layer_norm(x, gain, shift):
    center = x - jnp.mean(x, axis=-1, keepdims=True)
    spread = jnp.mean(center * center, axis=-1, keepdims=True)
    return (center * lax.rsqrt(spread + EPS) * gain + shift).astype(BF)


def gelu(v):
    half = 0.5 * v
    return half + half * lax.erf(v * math.sqrt(0.5))


def head_masks(heads, depth, width):
    lane = lax.broadcasted_iota(jnp.int32, (WIN * WIN, width), 1)
    return [(lane // depth == h).astype(F32).astype(BF) for h in range(heads)]


def stack_heads(rows, masks):
    return jnp.concatenate([rows * mask for mask in masks], axis=0)


def attend(q, k, v, bias, allowed, masks, ones):
    scores = dot_nt(q, stack_heads(k, masks)) + bias
    if allowed is not None:
        scores = jnp.where(allowed, scores, NEG)
    lanes = 128
    first = lax.broadcasted_iota(jnp.int32, (q.shape[0], lanes), 1) < WIN * WIN
    parts = []
    for start in range(0, scores.shape[1], lanes):
        s = scores[:, start : start + lanes]
        low = jnp.max(jnp.where(first, s, NEG), axis=-1, keepdims=True)
        high = jnp.max(jnp.where(first, NEG, s), axis=-1, keepdims=True)
        parts.append(jnp.exp2(s - jnp.where(first, low, high)).astype(BF))
    weights = jnp.concatenate(parts, axis=1)
    rhs = jnp.concatenate([stack_heads(v, masks), ones], axis=1)
    summed = dot_nn(weights, rhs)
    width = v.shape[1]
    return summed[:, :width] / summed[:, width:]


def pick(table, index):
    rows = index.shape[0]
    wide = jnp.concatenate([index, index], axis=1)
    low_index = jnp.minimum(wide, 127)
    high_index = jnp.maximum(wide - 128, 0)
    in_low = wide < 128
    first = lax.broadcasted_iota(jnp.int32, wide.shape, 1) < index.shape[1]

    def of_head(h):
        low = jnp.broadcast_to(table[h : h + 1, :128], (rows, 128))
        high = jnp.broadcast_to(table[h : h + 1, 128:], (rows, 128))
        return jnp.where(
            in_low,
            jnp.take_along_axis(low, low_index, axis=1),
            jnp.take_along_axis(high, high_index, axis=1),
        )

    return jnp.concatenate(
        [jnp.where(first, of_head(h), of_head(h + 1)) for h in range(0, table.shape[0], 2)], axis=1
    )


def mlp(middle, gain, shift, fc1, fc1_bias, fc2, fc2_bias):
    normed = layer_norm(middle, gain, shift)
    hidden = gelu(dot_nt(normed, fc1) + fc1_bias).astype(BF)
    return middle + dot_nn(hidden, fc2) + fc2_bias


def split_qkv(normed, wqkv, qkv_bias, scale):
    c = normed.shape[1]
    product = dot_nt(normed, wqkv) + qkv_bias
    if product.shape[1] == 3 * c:
        return (
            (product[:, :c] * scale).astype(BF),
            product[:, c : 2 * c].astype(BF),
            product[:, 2 * c :].astype(BF),
        )
    return product[:, :c].astype(BF), product[:, c:].astype(BF)


def regular_kernel(
    x_ref, left_ref, right_ref, rel_ref, table_ref, wqkv_ref, proj_ref, fc1_ref, fc2_ref,
    gain_ref, shift_ref, qkvb_ref, projb_ref, fc1b_ref, fc2b_ref, top_ref, bottom_ref, bias_ref,
):
    c = x_ref.shape[2]
    heads = table_ref.shape[0]
    depth = c // heads
    tokens = WIN * WIN
    scale = depth ** (-0.5) * LOG2E
    masks = head_masks(heads, depth, c)
    ones = jnp.concatenate(masks, axis=0)
    bias_ref[...] = pick(table_ref[...] * LOG2E, rel_ref[...])

    def run(x):
        q, k, v = split_qkv(
            layer_norm(x, gain_ref[0:1], shift_ref[0:1]), wqkv_ref[...], qkvb_ref[...], scale
        )
        outs = []
        for w in range(x.shape[0] // tokens):
            at = slice(w * tokens, (w + 1) * tokens)
            outs.append(attend(q[at], k[at], v[at], bias_ref[...], None, masks, ones))
        attended = jnp.concatenate(outs, axis=0).astype(BF)
        middle = x + dot_nn(attended, proj_ref[...]) + projb_ref[...]
        middle = middle.astype(BF).astype(F32)
        return mlp(
            middle, gain_ref[1:2], shift_ref[1:2], fc1_ref[...], fc1b_ref[...], fc2_ref[...], fc2b_ref[...]
        )

    group = 4

    def step(i, carry):
        start = pl.multiple_of(i * group * WIN, group * WIN)
        block = x_ref[:, pl.ds(start, group * WIN), :].astype(F32)
        x = jnp.concatenate(
            [block[r, w * WIN : (w + 1) * WIN] for w in range(group) for r in range(WIN)], axis=0
        )
        out = run(x)
        for r in range(WIN):
            row = jnp.concatenate(
                [out[w * tokens + r * WIN : w * tokens + (r + 1) * WIN] for w in range(group)], axis=0
            ).astype(BF)
            target = top_ref if r < SHIFT else bottom_ref
            target[r % SHIFT, pl.ds(start, group * WIN), :] = row
        return carry

    lax.fori_loop(0, x_ref.shape[1] // (group * WIN), step, 0)
    left = left_ref[...].astype(F32).reshape(tokens, c)
    right = right_ref[...].astype(F32).reshape(tokens, c)
    out = run(jnp.concatenate([left, right], axis=0))
    first = lax.broadcasted_iota(jnp.int32, (tokens, c), 0) % WIN < SHIFT
    edge = jnp.where(first, out[tokens:], out[:tokens])
    cols = x_ref.shape[1]
    for r in range(WIN):
        target = top_ref if r < SHIFT else bottom_ref
        target[r % SHIFT, cols : cols + WIN, :] = edge[r * WIN : (r + 1) * WIN].astype(BF)


def shifted_kernel(
    top_ref, bottom_ref, above_ref, below_ref, region_ref, rel_ref, table_ref, wqkv_ref, proj_ref,
    fc1_ref, fc2_ref, gain_ref, shift_ref, qkvb_ref, projb_ref, fc1b_ref, fc2b_ref, out_ref,
    bias_ref, own_ref, halo_ref, res_ref, *, group,
):
    c = top_ref.shape[2]
    cols = out_ref.shape[1]
    heads = table_ref.shape[0]
    depth = c // heads
    half = SHIFT * WIN
    tokens = WIN * WIN
    scale = depth ** (-0.5) * LOG2E
    masks = head_masks(heads, depth, c)
    ones = jnp.concatenate(masks, axis=0)
    bias_ref[...] = pick(table_ref[...] * LOG2E, rel_ref[...])
    for dst, srcs in ((own_ref, (top_ref, bottom_ref)), (halo_ref, (above_ref, below_ref))):
        for s, src in enumerate(srcs):
            value = src[...].astype(F32)
            edge = value[:, cols:]
            dst[s * SHIFT : (s + 1) * SHIFT, 0:WIN, :] = edge
            dst[s * SHIFT : (s + 1) * SHIFT, WIN : WIN + cols, :] = value[:, :cols]
            dst[s * SHIFT : (s + 1) * SHIFT, WIN + cols :, :] = edge
    first = lax.broadcasted_iota(jnp.int32, (WIN, group * WIN, c), 1) % WIN < SHIFT

    def step(i, carry):
        start = pl.multiple_of(i * group * WIN, WIN)

        def gather(ref):
            before = ref[:, pl.ds(start, group * WIN), :]
            after = ref[:, pl.ds(start + WIN, group * WIN), :]
            both = jnp.where(first, after, before)
            return jnp.concatenate(
                [
                    both[s * SHIFT + r, w * WIN : (w + 1) * WIN]
                    for w in range(group) for s in range(2) for r in range(SHIFT)
                ],
                axis=0,
            )

        x = gather(own_ref)
        gain, shift = gain_ref[0:1], shift_ref[0:1]
        q, k_own, v_own = split_qkv(layer_norm(x, gain, shift), wqkv_ref[...], qkvb_ref[...], scale)
        k_halo, v_halo = split_qkv(
            layer_norm(gather(halo_ref), gain, shift), wqkv_ref[c:], qkvb_ref[:, c:], scale
        )
        outs = []
        for w in range(group):
            ids = region_ref[i * group + w]
            key_ids = ids[:, :tokens * 2]
            for s in range(2):
                at = slice((w * 2 + s) * half, (w * 2 + s + 1) * half)
                k = jnp.concatenate([k_own[at], k_halo[at]], axis=0)
                v = jnp.concatenate([v_own[at], v_halo[at]], axis=0)
                row = ids[s : s + 1, :]
                keys = jnp.concatenate([row, row], axis=1)
                square = jnp.broadcast_to(row, (2 * tokens, 2 * tokens)).T[:half]
                allowed = jnp.concatenate([square, square], axis=1) == keys
                outs.append(
                    attend(q[at], k, v, bias_ref[s * half : (s + 1) * half], allowed, masks, ones)
                )
        attended = jnp.concatenate(outs, axis=0).astype(BF)
        middle = x + dot_nn(attended, proj_ref[...]) + projb_ref[...]
        middle = middle.astype(BF).astype(F32)
        out = mlp(
            middle, gain_ref[1:2], shift_ref[1:2], fc1_ref[...], fc1b_ref[...], fc2_ref[...], fc2b_ref[...]
        )
        for r in range(WIN):
            s, a = r // SHIFT, r % SHIFT
            res_ref[r, pl.ds(start, group * WIN), :] = jnp.concatenate(
                [
                    out[(w * 2 + s) * half + a * WIN : (w * 2 + s) * half + (a + 1) * WIN]
                    for w in range(group)
                ],
                axis=0,
            )
        return carry

    lax.fori_loop(0, (cols + WIN) // (group * WIN), step, 0)
    low = lax.broadcasted_iota(jnp.int32, (WIN, cols, c), 1) % WIN < SHIFT
    out_ref[...] = jnp.where(low, res_ref[:, 0:cols, :], res_ref[:, WIN : WIN + cols, :]).astype(BF)


def call(kernel, out_shapes, scratch, *args):
    return pl.pallas_call(
        kernel,
        out_shape=out_shapes,
        scratch_shapes=scratch,
        compiler_params=pltpu.CompilerParams(vmem_limit_bytes=48 * 1024 * 1024),
    )(*args)


def neighbours(axis, by):
    size = lax.axis_size(axis)
    return [(i, i + by) for i in range(size) if 0 <= i + by < size]


def padded(shard, sides, width):
    for axis, dim in sides:
        length = shard.shape[dim]
        last = lax.slice_in_dim(shard, length - width, length, axis=dim)
        leading = lax.slice_in_dim(shard, 0, width, axis=dim)
        before = lax.ppermute(last, axis, neighbours(axis, 1))
        after = lax.ppermute(leading, axis, neighbours(axis, -1))
        shard = jnp.concatenate([before, shard, after], axis=dim)
    return shard


def on_device(
    image_tokens, labels, rel_index, norm_gain, norm_shift, qkv_weight, qkv_bias, bias_table,
    proj_weight, proj_bias, fc1_weight, fc1_bias, fc2_weight, fc2_bias,
):
    own_rows, tile_cols, c = image_tokens.shape
    groups = lax.axis_size("ch")
    swap = [(i, (i + 1) % groups) for i in range(groups)]
    blocks, _, _, part = qkv_weight.shape
    hidden = fc1_weight.shape[2]
    entries = bias_table.shape[1]
    own_heads = bias_table.shape[2]

    def others(value):
        found = [value]
        for _ in range(groups - 1):
            found.append(lax.ppermute(found[-1], "ch", swap))
        return found

    weights = []
    for b in range(blocks):
        packed = jnp.concatenate(
            [
                qkv_weight[b].transpose(0, 2, 1).reshape(3 * part, c),
                proj_weight[b],
                fc1_weight[b].T,
                fc2_weight[b],
            ],
            axis=0,
        )
        weights.append(others(packed))
    tables = jnp.pad(bias_table.transpose(0, 2, 1), ((0, 0), (0, 0), (0, 256 - entries)))
    flat = jnp.concatenate([qkv_bias.reshape(-1), fc1_bias.reshape(-1), tables.reshape(-1)])
    small = [v.reshape(-1) for v in others(flat.reshape(-1, 128))]

    def full(b):
        got = weights[b]
        at = 0

        def take(rows):
            nonlocal at
            out = [g[at : at + rows] for g in got]
            at += rows
            return out

        qkv = jnp.concatenate([g.reshape(3, part, c) for g in take(3 * part)], axis=1).reshape(-1, c)
        proj = jnp.concatenate(take(part), axis=0)
        fc1 = jnp.concatenate(take(hidden), axis=0)
        fc2 = jnp.concatenate(take(hidden), axis=0)
        nq, nf = qkv_bias.size, fc1_bias.size
        qkvb = jnp.concatenate([s[:nq].reshape(blocks, 3, part)[b] for s in small], axis=1)
        fc1b = jnp.concatenate([s[nq : nq + nf].reshape(blocks, hidden)[b] for s in small], axis=0)
        table = jnp.concatenate(
            [s[nq + nf :].reshape(blocks, own_heads, 256)[b] for s in small], axis=0
        )
        return (
            table, qkv, proj, fc1, fc2, norm_gain[b], norm_shift[b], qkvb.reshape(1, -1),
            proj_bias[b][None], fc1b[None], fc2_bias[b][None],
        )

    left = lax.ppermute(image_tokens[:, tile_cols - WIN :], "col", neighbours("col", 1))
    right = lax.ppermute(image_tokens[:, :WIN], "col", neighbours("col", -1))

    margin = padded(labels, (("col", 1), (("row", "ch"), 0)), SHIFT)
    first_row = (lax.axis_index("row") * groups + lax.axis_index("ch")) * own_rows
    image_rows = own_rows * groups * lax.axis_size("row")
    image_cols = tile_cols * lax.axis_size("col")
    grid_rows = jnp.mod(first_row - SHIFT + jnp.arange(own_rows + 2 * SHIFT), image_rows)
    grid_cols = jnp.mod(
        lax.axis_index("col") * tile_cols - SHIFT + jnp.arange(tile_cols + 2 * SHIFT), image_cols
    )
    region = margin * 4 + (grid_rows < SHIFT)[:, None] * 2 + (grid_cols < SHIFT)[None, :]
    wins = tile_cols // WIN + 1
    half = SHIFT * WIN
    cells = region.reshape(4, SHIFT, wins, 2, SHIFT)[:, :, :, ::-1, :]
    cells = cells.transpose(2, 0, 1, 3, 4).reshape(wins, 4, half)
    order = jnp.stack(
        [
            jnp.concatenate([cells[:, 1], cells[:, 0]], axis=1),
            jnp.concatenate([cells[:, 2], cells[:, 3]], axis=1),
        ],
        axis=1,
    )
    order = jnp.concatenate([order, order], axis=2).astype(F32)

    rel = rel_index.reshape(2, SHIFT, 2, SHIFT, 2, SHIFT, 2, SHIFT)[:, :, ::-1, :, :, :, ::-1, :]
    rel = rel.reshape(2, half, 2, half)
    rel_shifted = jnp.concatenate(
        [
            jnp.concatenate([rel[1, :, 1], rel[1, :, 0]], axis=1),
            jnp.concatenate([rel[0, :, 0], rel[0, :, 1]], axis=1),
        ],
        axis=0,
    )

    strip = jax.ShapeDtypeStruct((SHIFT, tile_cols + WIN, c), BF)
    tokens = WIN * WIN
    heads = own_heads * groups
    bias_scratch = pltpu.VMEM((tokens, heads * tokens), F32)
    top, bottom = call(
        regular_kernel, (strip, strip), [bias_scratch], image_tokens, left, right, rel_index, *full(0)
    )
    above = lax.ppermute(bottom, ("row", "ch"), neighbours(("row", "ch"), 1))
    below = lax.ppermute(top, ("row", "ch"), neighbours(("row", "ch"), -1))
    group = max(g for g in range(1, 5) if wins % g == 0)
    wide = pltpu.VMEM((WIN, tile_cols + 2 * WIN, c), F32)
    return call(
        lambda *refs: shifted_kernel(*refs, group=group),
        jax.ShapeDtypeStruct(image_tokens.shape, BF),
        [bias_scratch, wide, wide, pltpu.VMEM((WIN, tile_cols + WIN, c), F32)],
        top, bottom, above, below, order, rel_shifted, *full(1),
    )


def solution(mesh):
    in_specs = (
        P(("row", "ch"), "col", None),
        P(("row", "ch"), "col"),
        P(),
        P(),
        P(),
        P(None, None, None, "ch"),
        P(None, None, "ch"),
        P(None, None, "ch"),
        P(None, "ch", None),
        P(),
        P(None, None, "ch"),
        P(None, "ch"),
        P(None, "ch", None),
        P(),
    )
    out_specs = P(("row", "ch"), "col", None)
    return jax.shard_map(
        on_device, mesh=mesh, in_specs=in_specs, out_specs=out_specs, check_vma=False
    )
```

profile of v0, /device:TPU:9, one launch (start us, length us, event | category | flops | bytes accessed | tf_op | source)
XLA Modules:
  0.0 88.9 jit_solution(6609717927529001532)
XLA Ops:
  0.0 0.8 fusion.6
  0.8 3.7 %collective-permute-start = (bf16[8,8,128]{2,1,0:T(8,128)(2,1)S(1)}, bf16[8,8,128]{2,1,0:T(8,128)(2,1)S(1)}, u32[]{:S(2)}, u32[]{:S(2)}) collective-permute-start(bf16[8,8,128]{2,1,0:T(8,128)(2,1)S(1)} %get-tuple-element.10), channel_id=1, source_target_pairs={{0,2},{2,4},{4,6},{1,3},{3,5},{5,7},{8,10},{10,12},{12,14},{9,11},... | collective-permute-start | bytes 49160 | tf_op jit(solution)/shard_map/ppermute | solution.py:329
  4.5 1.9 %collective-permute-start.1 = (bf16[8,8,128]{2,1,0:T(8,128)(2,1)S(1)}, bf16[8,8,128]{2,1,0:T(8,128)(2,1)S(1)}, u32[]{:S(2)}, u32[]{:S(2)}) collective-permute-start(bf16[8,8,128]{2,1,0:T(8,128)(2,1)S(1)} %get-tuple-element.9), channel_id=1, source_target_pairs={{2,0},{4,2},{6,4},{3,1},{5,3},{7,5},{10,8},{12,10},{14,12},{11,9},... | collective-permute-start | bytes 49160 | tf_op jit(solution)/shard_map/ppermute | solution.py:330
  6.4 0.7 pad_bitcast_fusion
  7.1 0.7 copy.38
  7.8 0.7 copy.21
  8.4 0.1 reshape.118
  8.5 1.3 %collective-permute-start.2 = (f32[15,128]{1,0:T(8,128)S(1)}, f32[15,128]{1,0:T(8,128)S(1)}, u32[]{:S(2)}, u32[]{:S(2)}) collective-permute-start(f32[15,128]{1,0:T(8,128)S(1)} %maximum_bitcast_fusion), channel_id=1, source_target_pairs={{0,1},{1,0},{2,3},{3,2},{4,5},{5,4},{6,7},{7,6},{8,9},{9,8},{10,11... | collective-permute-start | bytes 23048 | tf_op jit(solution)/shard_map/ppermute | solution.py:285
  9.8 0.8 fusion.13
  10.6 1.9 %collective-permute-start.7 = (s32[8,4]{1,0:T(8,128)S(1)}, s32[8,4]{1,0:T(8,128)S(1)}, u32[]{:S(2)}, u32[]{:S(2)}) collective-permute-start(s32[8,4]{1,0:T(8,128)S(1)} %get-tuple-element.40), channel_id=1, source_target_pairs={{2,0},{4,2},{6,4},{3,1},{5,3},{7,5},{10,8},{12,10},{14,12},{11,9},... | collective-permute-start | bytes 392 | tf_op jit(solution)/shard_map/ppermute | solution.py:265
  12.5 3.9 %collective-permute-start.6 = (s32[8,4]{1,0:T(8,128)S(1)}, s32[8,4]{1,0:T(8,128)S(1)}, u32[]{:S(2)}, u32[]{:S(2)}) collective-permute-start(s32[8,4]{1,0:T(8,128)S(1)} %get-tuple-element.39), channel_id=1, source_target_pairs={{0,2},{2,4},{4,6},{1,3},{3,5},{5,7},{8,10},{10,12},{12,14},{9,11},... | collective-permute-start | bytes 392 | tf_op jit(solution)/shard_map/ppermute | solution.py:264
  16.5 0.0 copy-start.9
  16.5 0.7 copy-done.9
  17.2 0.9 copy-done.4
  18.1 0.0 copy-start.7
  18.1 0.0 copy-start.5
  18.1 0.1 copy.32
  18.2 0.6 copy-done.7
  18.9 0.1 copy-done.5
  19.1 0.1 compare_convert_fusion
  19.1 0.7 copy-done.1
  19.8 0.8 reshape.128
  20.6 0.1 copy.29
  20.7 1.4 %rev.7 = s32[2,4,2,4,2,4,2,4]{7,6,5,3,2,1,4,0:T(2,128)S(1)} reverse(s32[2,4,2,4,2,4,2,4]{7,6,5,3,2,1,4,0:T(2,128)S(1)} %copy.29), dimensions={2,6} | reverse | bytes 32768 | tf_op jit(solution)/shard_map/rev | solution.py:354
  22.1 0.7 reshape.129
  22.8 0.0 copy-start.12
  22.8 0.1 copy.37
  22.9 0.5 copy-done.11
  23.4 0.0 copy-done.12
  23.5 0.7 copy-done.13
  24.1 0.0 copy-done.14
  24.2 0.1 add_add_fusion.1.refs_5_
  24.3 0.7 copy-done.6
  25.0 0.1 pad_add_fusion.2
  25.0 2.2 %collective-permute-start.9 = (s32[4,264]{1,0:T(4,128)S(1)}, s32[4,264]{1,0:T(4,128)S(1)}, u32[]{:S(2)}, u32[]{:S(2)}) collective-permute-start(s32[4,264]{1,0:T(4,128)S(1)} %get-tuple-element.34), channel_id=1, source_target_pairs={{1,0},{8,1},{9,8},{16,9},{17,16},{24,17},{25,24},{3,2},{10,3},{11,... | collective-permute-start | bytes 12680 | tf_op jit(solution)/shard_map/ppermute | solution.py:265
  27.2 3.3 %collective-permute-start.8 = (s32[4,264]{1,0:T(4,128)S(1)}, s32[4,264]{1,0:T(4,128)S(1)}, u32[]{:S(2)}, u32[]{:S(2)}) collective-permute-start(s32[4,264]{1,0:T(4,128)S(1)} %get-tuple-element.33), channel_id=1, source_target_pairs={{0,1},{1,8},{8,9},{9,16},{16,17},{17,24},{24,25},{2,3},{3,10},{10,... | collective-permute-start | bytes 12680 | tf_op jit(solution)/shard_map/ppermute | solution.py:264
  30.5 1.2 %collective-permute-start.3 = (bf16[768,128]{1,0:T(8,128)(2,1)S(1)}, bf16[768,128]{1,0:T(8,128)(2,1)S(1)}, u32[]{:S(2)}, u32[]{:S(2)}) collective-permute-start(bf16[768,128]{1,0:T(8,128)(2,1)S(1)} %pad_maximum_fusion), channel_id=1, source_target_pairs={{0,1},{1,0},{2,3},{3,2},{4,5},{5,4},{6,7},{7,6},{8,9},{9,8},{10,11... | collective-permute-start | bytes 589832 | tf_op jit(solution)/shard_map/ppermute | solution.py:285
  31.7 0.8 collective-permute-done.8
  32.5 0.5 collective-permute-start.10
  32.9 0.1 add_multiply_fusion
  33.0 0.4 mul.24
  33.4 0.3 add_add_fusion
  33.7 1.9 %rev.6 = s32[4,4,33,2,4]{4,3,2,1,0:T(2,128)S(1)} reverse(s32[4,4,33,2,4]{4,3,2,1,0:T(2,128)S(1)} %add_add_fusion), dimensions={3} | reverse | bytes 33792 | tf_op jit(solution)/shard_map/rev | solution.py:343
  35.5 0.3 copy.24
  35.9 0.1 copy.36
  35.9 0.1 copy.35
  36.0 0.1 pad_add_fusion.1
  36.1 0.1 copy.34
  36.2 0.1 copy.33
  36.3 0.1 pad_add_fusion
  36.4 0.1 add_convert_fusion.refs_4_
  36.6 0.1 reshape.125
  36.7 0.1 maximum_bitcast_fusion.1
  36.8 0.1 maximum_bitcast_fusion.2
  36.9 0.6 collective-permute-done.3
  37.5 0.0 copy-start
  37.6 0.6 copy-done.2
  38.2 0.7 slice-done
  39.0 13.2 %shard_map.136 = (bf16[4,264,128]{2,1,0:T(8,128)(2,1)S(1)}, bf16[4,264,128]{2,1,0:T(8,128)(2,1)S(1)}) custom-call(bf16[8,256,128]{2,1,0:T(8,128)(2,1)S(1)} %copy-done, bf16[8,8,128]{2,1,0:T(8,128)(2,1)S(1)} %collective-permute-done.left_ref, bf16[8,8,128]{2,1,0:T(8,128)(2,1)S(1)} %collective-permute-done.1.right_ref, s32[64,64]{1,0:T(8,128)S(1)} %copy-done.1, ...), custom_call_target="tpu_custom_call" | custom-call | tf_op jit(solution)/shard_map/pallas_call | solution.py:246
  52.2 3.0 %collective-permute-start.4 = (bf16[4,264,128]{2,1,0:T(8,128)(2,1)S(1)}, bf16[4,264,128]{2,1,0:T(8,128)(2,1)S(1)}, u32[]{:S(2)}, u32[]{:S(2)}) collective-permute-start(bf16[4,264,128]{2,1,0:T(8,128)(2,1)S(1)} %get-tuple-element.8.refs_1_), channel_id=1, source_target_pairs={{0,1},{1,8},{8,9},{9,16},{16,17},{17,24},{24,25},{2,3},{3,10},{10,... | collective-permute-start | bytes 811016 | tf_op jit(solution)/shard_map/ppermute | solution.py:371
  55.3 3.1 %collective-permute-start.5 = (bf16[4,264,128]{2,1,0:T(8,128)(2,1)S(1)}, bf16[4,264,128]{2,1,0:T(8,128)(2,1)S(1)}, u32[]{:S(2)}, u32[]{:S(2)}) collective-permute-start(bf16[4,264,128]{2,1,0:T(8,128)(2,1)S(1)} %get-tuple-element.7.refs_0_), channel_id=1, source_target_pairs={{1,0},{8,1},{9,8},{16,9},{17,16},{24,17},{25,24},{3,2},{10,3},{11,... | collective-permute-start | bytes 811016 | tf_op jit(solution)/shard_map/ppermute | solution.py:372
  58.5 8.8 %collective-permute-done.4.refs_2_ = bf16[4,264,128]{2,1,0:T(8,128)(2,1)S(1)} collective-permute-done((bf16[4,264,128]{2,1,0:T(8,128)(2,1)S(1)}, bf16[4,264,128]{2,1,0:T(8,128)(2,1)S(1)}, u32[]{:S(2)}, u32[]{:S(2)}) %collective-permute-start.4) | collective-permute-done | bytes 270368 | tf_op jit(solution)/shard_map/ppermute | solution.py:371
  67.3 1.9 %collective-permute-done.5.refs_3_ = bf16[4,264,128]{2,1,0:T(8,128)(2,1)S(1)} collective-permute-done((bf16[4,264,128]{2,1,0:T(8,128)(2,1)S(1)}, bf16[4,264,128]{2,1,0:T(8,128)(2,1)S(1)}, u32[]{:S(2)}, u32[]{:S(2)}) %collective-permute-start.5) | collective-permute-done | bytes 270368 | tf_op jit(solution)/shard_map/ppermute | solution.py:372
  69.3 19.7 %shard_map.137 = bf16[8,256,128]{2,1,0:T(8,128)(2,1)} custom-call(bf16[4,264,128]{2,1,0:T(8,128)(2,1)S(1)} %get-tuple-element.7.refs_0_, bf16[4,264,128]{2,1,0:T(8,128)(2,1)S(1)} %get-tuple-element.8.refs_1_, bf16[4,264,128]{2,1,0:T(8,128)(2,1)S(1)} %collective-permute-done.4.refs_2_, bf16[4,264,128]{2,1,0:T(8,128)(2,1)S(1)} %collective-permute-done.5.refs_3_, ...), custom_call_target="tpu_custom_call" | custom-call | tf_op jit(solution)/shard_map/pallas_call | solution.py:246
  (68 shorter events, 0.4 us)
Async XLA Ops:
  0.0 17.2 %copy-start.3 = (bf16[2,256,128]{2,1,0:T(8,128)(2,1)S(1)}, bf16[2,256,128]{2,1,0:T(8,128)(2,1)}, u32[]{:S(2)}) copy-start(bf16[2,256,128]{2,1,0:T(8,128)(2,1)} %param.26) | copy-start | bytes 393220
  0.8 38.2 %collective-permute-start = (bf16[8,8,128]{2,1,0:T(8,128)(2,1)S(1)}, bf16[8,8,128]{2,1,0:T(8,128)(2,1)S(1)}, u32[]{:S(2)}, u32[]{:S(2)}) collective-permute-start(bf16[8,8,128]{2,1,0:T(8,128)(2,1)S(1)} %get-tuple-element.10), channel_id=1, source_target_pairs={{0,2},{2,4},{4,6},{1,3},{3,5},{5,7},{8,10},{10,12},{12,14},{9,11},... | collective-permute-start | bytes 49160 | tf_op jit(solution)/shard_map/ppermute | solution.py:329
  4.5 34.5 %collective-permute-start.1 = (bf16[8,8,128]{2,1,0:T(8,128)(2,1)S(1)}, bf16[8,8,128]{2,1,0:T(8,128)(2,1)S(1)}, u32[]{:S(2)}, u32[]{:S(2)}) collective-permute-start(bf16[8,8,128]{2,1,0:T(8,128)(2,1)S(1)} %get-tuple-element.9), channel_id=1, source_target_pairs={{2,0},{4,2},{6,4},{3,1},{5,3},{7,5},{10,8},{12,10},{14,12},{11,9},... | collective-permute-start | bytes 49160 | tf_op jit(solution)/shard_map/ppermute | solution.py:330
  8.5 28.0 %collective-permute-start.2 = (f32[15,128]{1,0:T(8,128)S(1)}, f32[15,128]{1,0:T(8,128)S(1)}, u32[]{:S(2)}, u32[]{:S(2)}) collective-permute-start(f32[15,128]{1,0:T(8,128)S(1)} %maximum_bitcast_fusion), channel_id=1, source_target_pairs={{0,1},{1,0},{2,3},{3,2},{4,5},{5,4},{6,7},{7,6},{8,9},{9,8},{10,11... | collective-permute-start | bytes 23048 | tf_op jit(solution)/shard_map/ppermute | solution.py:285
  9.8 6.6 %copy-start.8 = (f32[2,225,2]{1,2,0:T(2,128)S(1)}, f32[2,225,2]{1,2,0:T(2,128)}, u32[]{:S(2)}) copy-start(f32[2,225,2]{1,2,0:T(2,128)} %param.21) | copy-start | bytes 10804
  10.6 13.7 %collective-permute-start.7 = (s32[8,4]{1,0:T(8,128)S(1)}, s32[8,4]{1,0:T(8,128)S(1)}, u32[]{:S(2)}, u32[]{:S(2)}) collective-permute-start(s32[8,4]{1,0:T(8,128)S(1)} %get-tuple-element.40), channel_id=1, source_target_pairs={{2,0},{4,2},{6,4},{3,1},{5,3},{7,5},{10,8},{12,10},{14,12},{11,9},... | collective-permute-start | bytes 392 | tf_op jit(solution)/shard_map/ppermute | solution.py:265
  12.5 11.8 %collective-permute-start.6 = (s32[8,4]{1,0:T(8,128)S(1)}, s32[8,4]{1,0:T(8,128)S(1)}, u32[]{:S(2)}, u32[]{:S(2)}) collective-permute-start(s32[8,4]{1,0:T(8,128)S(1)} %get-tuple-element.39), channel_id=1, source_target_pairs={{0,2},{2,4},{4,6},{1,3},{3,5},{5,7},{8,10},{10,12},{12,14},{9,11},... | collective-permute-start | bytes 392 | tf_op jit(solution)/shard_map/ppermute | solution.py:264
  16.5 0.7 copy-start.9
  17.2 0.9 %copy-start.4 = (bf16[2,128,256]{2,1,0:T(8,128)(2,1)S(1)}, bf16[2,128,256]{2,1,0:T(8,128)(2,1)}, u32[]{:S(2)}) copy-start(bf16[2,128,256]{2,1,0:T(8,128)(2,1)} %param.24) | copy-start | bytes 393220
  18.1 0.8 copy-start.7
  18.1 0.9 %copy-start.5 = (bf16[2,3,128,64]{2,3,1,0:T(8,128)(2,1)S(1)}, bf16[2,3,128,64]{2,3,1,0:T(8,128)(2,1)}, u32[]{:S(2)}) copy-start(bf16[2,3,128,64]{2,3,1,0:T(8,128)(2,1)} %param.19) | copy-start | bytes 294916
  19.0 0.8 copy-start.1
  22.8 0.7 copy-start.11
  22.8 0.7 copy-start.12
  23.5 0.7 copy-start.13
  23.5 0.7 copy-start.14
  24.2 0.7 copy-start.6
  25.0 5.5 %copy-start.10 = (f32[2,3,64]{2,0,1:T(2,128)S(1)}, f32[2,3,64]{2,0,1:T(2,128)}, u32[]{:S(2)}) copy-start(f32[2,3,64]{2,0,1:T(2,128)} %param.20) | copy-start | bytes 4612
  25.0 5.5 %collective-permute-start.9 = (s32[4,264]{1,0:T(4,128)S(1)}, s32[4,264]{1,0:T(4,128)S(1)}, u32[]{:S(2)}, u32[]{:S(2)}) collective-permute-start(s32[4,264]{1,0:T(4,128)S(1)} %get-tuple-element.34), channel_id=1, source_target_pairs={{1,0},{8,1},{9,8},{16,9},{17,16},{24,17},{25,24},{3,2},{10,3},{11,... | collective-permute-start | bytes 12680 | tf_op jit(solution)/shard_map/ppermute | solution.py:265
  27.2 5.3 %collective-permute-start.8 = (s32[4,264]{1,0:T(4,128)S(1)}, s32[4,264]{1,0:T(4,128)S(1)}, u32[]{:S(2)}, u32[]{:S(2)}) collective-permute-start(s32[4,264]{1,0:T(4,128)S(1)} %get-tuple-element.33), channel_id=1, source_target_pairs={{0,1},{1,8},{8,9},{9,16},{16,17},{17,24},{24,25},{2,3},{3,10},{10,... | collective-permute-start | bytes 12680 | tf_op jit(solution)/shard_map/ppermute | solution.py:264
  30.5 7.0 %collective-permute-start.3 = (bf16[768,128]{1,0:T(8,128)(2,1)S(1)}, bf16[768,128]{1,0:T(8,128)(2,1)S(1)}, u32[]{:S(2)}, u32[]{:S(2)}) collective-permute-start(bf16[768,128]{1,0:T(8,128)(2,1)S(1)} %pad_maximum_fusion), channel_id=1, source_target_pairs={{0,1},{1,0},{2,3},{3,2},{4,5},{5,4},{6,7},{7,6},{8,9},{9,8},{10,11... | collective-permute-start | bytes 589832 | tf_op jit(solution)/shard_map/ppermute | solution.py:285
  32.5 25.9 %collective-permute-start.10 = (bf16[768,128]{1,0:T(8,128)(2,1)S(1)}, bf16[768,128]{1,0:T(8,128)(2,1)S(1)}, u32[]{:S(2)}, u32[]{:S(2)}) collective-permute-start(bf16[768,128]{1,0:T(8,128)(2,1)S(1)} %pad_maximum_fusion.1), channel_id=1, source_target_pairs={{0,1},{1,0},{2,3},{3,2},{4,5},{5,4},{6,7},{7,6},{8,9},{9,8},{10,11... | collective-permute-start | bytes 589832 | tf_op jit(solution)/shard_map/ppermute | solution.py:285
  37.5 0.7 copy-start.2
  37.5 1.4 %copy-start = (bf16[8,256,128]{2,1,0:T(8,128)(2,1)S(1)}, bf16[8,256,128]{2,1,0:T(8,128)(2,1)}, u32[]{:S(2)}) copy-start(bf16[8,256,128]{2,1,0:T(8,128)(2,1)} %x_ref.1) | copy-start | bytes 1572868
  38.2 0.8 slice-start
  52.2 15.1 %collective-permute-start.4 = (bf16[4,264,128]{2,1,0:T(8,128)(2,1)S(1)}, bf16[4,264,128]{2,1,0:T(8,128)(2,1)S(1)}, u32[]{:S(2)}, u32[]{:S(2)}) collective-permute-start(bf16[4,264,128]{2,1,0:T(8,128)(2,1)S(1)} %get-tuple-element.8.refs_1_), channel_id=1, source_target_pairs={{0,1},{1,8},{8,9},{9,16},{16,17},{17,24},{24,25},{2,3},{3,10},{10,... | collective-permute-start | bytes 811016 | tf_op jit(solution)/shard_map/ppermute | solution.py:371
  55.3 14.0 %collective-permute-start.5 = (bf16[4,264,128]{2,1,0:T(8,128)(2,1)S(1)}, bf16[4,264,128]{2,1,0:T(8,128)(2,1)S(1)}, u32[]{:S(2)}, u32[]{:S(2)}) collective-permute-start(bf16[4,264,128]{2,1,0:T(8,128)(2,1)S(1)} %get-tuple-element.7.refs_0_), channel_id=1, source_target_pairs={{1,0},{8,1},{9,8},{16,9},{17,16},{24,17},{25,24},{3,2},{10,3},{11,... | collective-permute-start | bytes 811016 | tf_op jit(solution)/shard_map/ppermute | solution.py:372
where the time goes:
time: 89.6 us; the launch traced here: 88.9 us
  Pallas kernels  32.9 us (37%)
  starting transfers between devices  25.9 us (29%)
  local copies, waits for them, and re-layouts  16.3 us (18%)
  waiting for transfers between devices  12.1 us (14%)
  other arithmetic  1.17 us (1%)
    pallas_call x2, Pallas kernels, call(): pl.pallas_call(kernel, out_shape=out_shapes, scratch_shapes=scratch, comp...  32.9 us
    ppermute x1, waiting for transfers between devices, on_device(): above = lax.ppermute(bottom, ('row', 'ch'), neighbours(('row', 'ch'), 1))  8.8 us
    unnamed x43, local copies, waits for them, and re-layouts  8.16 us
    ppermute x2, starting transfers between devices, padded(): before = lax.ppermute(last, axis, neighbours(axis, 1))  7.18 us
    ppermute x2, starting transfers between devices, padded(): after = lax.ppermute(leading, axis, neighbours(axis, -1))  4.06 us
    ppermute x1, starting transfers between devices, on_device(): lax.ppermute(image_tokens[:, tile_cols - WIN:], 'col', neighbours('col', 1))  3.67 us
    ppermute x1, starting transfers between devices, on_device(): below = lax.ppermute(top, ('row', 'ch'), neighbours(('row', 'ch'), -1))  3.14 us
    ppermute x1, starting transfers between devices, on_device(): above = lax.ppermute(bottom, ('row', 'ch'), neighbours(('row', 'ch'), 1))  3.04 us
  transfers between devices with their start and end apart: 11, of which 4 were waited for; matrix products, arithmetic and copies ran while one was open for 12% of the time, Pallas kernels for 15%

commit v1 on v0

v1 whole, which is shorter than its diff:
```python
import math

import jax
import jax.numpy as jnp
from jax import lax
from jax.experimental import pallas as pl
from jax.experimental.pallas import tpu as pltpu
from jax.sharding import PartitionSpec as P

WIN = 8
SHIFT = 4
EPS = 1e-05
NEG = -1e30
LOG2E = math.log2(math.e)
BF = jnp.bfloat16
F32 = jnp.float32


def dot_nt(a, b):
    return lax.dot_general(a, b, (((1,), (1,)), ((), ())), preferred_element_type=F32)


def dot_nn(a, b):
    return lax.dot_general(a, b, (((1,), (0,)), ((), ())), preferred_element_type=F32)


def layer_norm(x, gain, shift):
    center = x - jnp.mean(x, axis=-1, keepdims=True)
    spread = jnp.mean(center * center, axis=-1, keepdims=True)
    return (center * lax.rsqrt(spread + EPS) * gain + shift).astype(BF)


def gelu(v):
    half = 0.5 * v
    return half + half * lax.erf(v * math.sqrt(0.5))


def head_masks(heads, depth, width):
    lane = lax.broadcasted_iota(jnp.int32, (WIN * WIN, width), 1)
    return [(lane // depth == h).astype(F32).astype(BF) for h in range(heads)]


def stack_heads(rows, masks):
    return jnp.concatenate([rows * mask for mask in masks], axis=0)


def attend(q, k, v, bias, allowed, masks, ones):
    scores = dot_nt(q, stack_heads(k, masks)) + bias
    if allowed is not None:
        scores = jnp.where(allowed, scores, NEG)
    lanes = 128
    first = lax.broadcasted_iota(jnp.int32, (q.shape[0], lanes), 1) < WIN * WIN
    parts = []
    for start in range(0, scores.shape[1], lanes):
        s = scores[:, start : start + lanes]
        low = jnp.max(jnp.where(first, s, NEG), axis=-1, keepdims=True)
        high = jnp.max(jnp.where(first, NEG, s), axis=-1, keepdims=True)
        parts.append(jnp.exp2(s - jnp.where(first, low, high)).astype(BF))
    weights = jnp.concatenate(parts, axis=1)
    rhs = jnp.concatenate([stack_heads(v, masks), ones], axis=1)
    summed = dot_nn(weights, rhs)
    width = v.shape[1]
    return summed[:, :width] / summed[:, width:]


def pick(low_rows, high_rows, skip, wide):
    rows = wide.shape[0]
    in_low = wide < 128
    low_index = jnp.minimum(wide, 127)
    high_index = jnp.maximum(wide - skip, 0)
    first = lax.broadcasted_iota(jnp.int32, wide.shape, 1) < WIN * WIN

    def of_head(h):
        low = jnp.broadcast_to(low_rows[h] * LOG2E, (rows, 128))
        high = jnp.broadcast_to(high_rows[h] * LOG2E, (rows, 128))
        return jnp.where(
            in_low,
            jnp.take_along_axis(low, low_index, axis=1),
            jnp.take_along_axis(high, high_index, axis=1),
        )

    return jnp.concatenate(
        [jnp.where(first, of_head(h), of_head(h + 1)) for h in range(0, len(low_rows), 2)], axis=1
    )


def split3(value):
    high = value.astype(BF)
    rest = value - high.astype(F32)
    middle = rest.astype(BF)
    return [high, middle, (rest - middle.astype(F32)).astype(BF)]


QKVB, FC1B, TABLE = 0, 3, 5
GAIN, SHIFTS, PROJB, FC2B = 9, 11, 13, 14
SMALL = 16


def pack_kernel(*refs, count):
    hbm, refs = refs[:count], refs[count:]
    (w0_ref, w1_ref, left_ref, right_ref, rel2_ref), refs = refs[:5], refs[5:]
    staged, small_ref, sems = refs[:count], refs[count], refs[count + 1]
    cols = hbm[0].shape[1]
    edge = 2 * WIN
    copies = [
        pltpu.make_async_copy(hbm[0].at[:, 0:edge], staged[0].at[0], sems.at[0]),
        pltpu.make_async_copy(hbm[0].at[:, cols - edge : cols], staged[0].at[1], sems.at[count]),
    ]
    copies += [pltpu.make_async_copy(hbm[k], staged[k], sems.at[k]) for k in range(1, count)]
    for copy in copies:
        copy.start()
    for copy in copies:
        copy.wait()
    (x, labels, rel, gain, shift, qkv, qkvb, table, proj, projb, fc1, fc1b, fc2, fc2b) = staged
    c = x.shape[3]
    part = qkv.shape[3]
    hidden = fc1.shape[2]
    entries = table.shape[1]
    for b, out in enumerate((w0_ref, w1_ref)):
        at = 0
        for m in range(3):
            out[at : at + part, :] = qkv[b, m].astype(F32).T.astype(BF)
            at += part
        out[at : at + part, :] = proj[b]
        at += part
        for start in range(0, hidden, 128):
            out[at : at + c, :] = fc1[b, :, start : start + 128]
            at += c
        out[at : at + hidden, :] = fc2[b]
        at += hidden
        small_ref[...] = jnp.zeros_like(small_ref)
        small_ref[QKVB : QKVB + 3, 0:part] = qkvb[b]
        for k in range(hidden // 128):
            small_ref[FC1B + k : FC1B + k + 1, :] = fc1b[b : b + 1, k * 128 : (k + 1) * 128]
        k = TABLE
        for h in range(table.shape[2]):
            for first in (0, entries - 128):
                column = table[b, first : first + 128, h : h + 1]
                small_ref[k : k + 1, :] = jnp.broadcast_to(column, (128, 128)).T[0:1]
                k += 1
        small_ref[GAIN : GAIN + 2, :] = gain[b]
        small_ref[SHIFTS : SHIFTS + 2, :] = shift[b]
        small_ref[PROJB : PROJB + 1, :] = projb[b : b + 1, :]
        small_ref[FC2B : FC2B + 1, :] = fc2b[b : b + 1, :]
        for piece in split3(small_ref[...]):
            out[at : at + SMALL, :] = piece
            at += SMALL
    ids = (labels[...] + 1).astype(F32).astype(BF)
    for r in range(WIN):
        left_ref[r] = x[0, r, 0:WIN]
        right_ref[r] = x[1, r, WIN:]
    left_ref[WIN] = ids[:, 0:128]
    right_ref[WIN] = ids[:, cols - 128 : cols]
    rel2_ref[...] = jnp.concatenate([rel[...], rel[...]], axis=1)


class Weights:

    def __init__(self, packs, scratch, c, part, hidden):
        self.qkv, self.proj, self.fc1, self.fc2 = scratch
        self.c = c
        self.packs = packs
        self.part, self.hidden = part, hidden
        self.start_small = 4 * part + (hidden // 128) * c + hidden

    def small(self, row, rows=1, width=128):
        out = []
        for p in self.packs:
            at = self.start_small
            value = sum(
                p[at + k * SMALL : at + (k + 1) * SMALL, :].astype(F32) for k in range(3)
            )
            out.append(value[row : row + rows, :width])
        return out

    def load(self):
        c, part, hidden = self.c, self.part, self.hidden
        for m in range(3):
            rows = jnp.concatenate([p[m * part : (m + 1) * part, :] for p in self.packs], axis=0)
            self.qkv[:, m * c : (m + 1) * c] = rows.astype(F32).T.astype(BF)
        for g, p in enumerate(self.packs):
            at = 3 * part
            self.proj[g * part : (g + 1) * part, :] = p[at : at + part, :]
            at += part
            for k in range(hidden // 128):
                lane = g * hidden + k * 128
                self.fc1[:, lane : lane + 128] = p[at : at + c, :]
                at += c
            self.fc2[g * hidden : (g + 1) * hidden, :] = p[at : at + hidden, :]
        self.gain = [self.small(GAIN + k)[0] for k in range(2)]
        self.shift = [self.small(SHIFTS + k)[0] for k in range(2)]
        self.proj_bias = self.small(PROJB)[0]
        self.fc2_bias = self.small(FC2B)[0]
        self.qkv_bias = jnp.concatenate(
            [v for m in range(3) for v in self.small(QKVB + m, width=part)], axis=1
        )
        rows = [self.small(FC1B + k) for k in range(hidden // 128)]
        self.fc1_bias = jnp.concatenate(
            [row[g] for g in range(len(self.packs)) for row in rows], axis=1
        )

    def bias(self, own_heads, skip, wide):
        rows = [self.small(TABLE + k) for k in range(2 * own_heads)]
        low = [rows[2 * h][g] for g in range(len(self.packs)) for h in range(own_heads)]
        high = [rows[2 * h + 1][g] for g in range(len(self.packs)) for h in range(own_heads)]
        return pick(low, high, skip, wide)

    def queries(self, x, scale):
        c = self.c
        product = dot_nn(layer_norm(x, self.gain[0], self.shift[0]), self.qkv[...]) + self.qkv_bias
        return (
            (product[:, :c] * scale).astype(BF),
            product[:, c : 2 * c].astype(BF),
            product[:, 2 * c :].astype(BF),
        )

    def keys(self, x):
        c = self.c
        normed = layer_norm(x, self.gain[0], self.shift[0])
        product = dot_nn(normed, self.qkv[:, c:]) + self.qkv_bias[:, c:]
        return product[:, :c].astype(BF), product[:, c:].astype(BF)

    def finish(self, x, attended):
        middle = x + dot_nn(attended, self.proj[...]) + self.proj_bias
        middle = middle.astype(BF).astype(F32)
        normed = layer_norm(middle, self.gain[1], self.shift[1])
        hidden = gelu(dot_nn(normed, self.fc1[...]) + self.fc1_bias).astype(BF)
        return middle + dot_nn(hidden, self.fc2[...]) + self.fc2_bias


def regular_kernel(
    x_ref, left_ref, right_ref, labels_ref, rel_ref, *refs, groups, own_heads, entries, part, hidden
):
    packs, refs = refs[:groups], refs[groups:]
    (top_ref, bottom_ref, bias_ref), scratch = refs[:3], refs[3:]
    c = x_ref.shape[2]
    cols = x_ref.shape[1]
    heads = own_heads * groups
    depth = c // heads
    tokens = WIN * WIN
    scale = depth ** (-0.5) * LOG2E
    w = Weights(packs, scratch, c, part, hidden)
    w.load()
    masks = head_masks(heads, depth, c)
    ones = jnp.concatenate(masks, axis=0)
    bias_ref[...] = w.bias(own_heads, entries - 128, rel_ref[...])

    lanes = jnp.concatenate(
        [
            left_ref[WIN].astype(F32),
            (labels_ref[...] + 1).astype(F32),
            right_ref[WIN].astype(F32),
        ],
        axis=1,
    )
    span = lanes.shape[1]
    lane = lax.broadcasted_iota(jnp.int32, (WIN, span), 1)
    match = lane % WIN == lax.broadcasted_iota(jnp.int32, (WIN, span), 0)
    spread = jnp.concatenate(
        [jnp.where(match, lanes[r : r + 1], 0.0) for r in range(WIN)], axis=0
    ).astype(BF)
    source = lax.broadcasted_iota(jnp.int32, (span, 128), 0)
    window = lax.broadcasted_iota(jnp.int32, (span, 128), 1)
    chosen = ((source - 128 + SHIFT) // WIN == window) & (source >= 128 - SHIFT)
    ids = dot_nn(spread, chosen.astype(F32).astype(BF))
    for r in range(WIN):
        target = top_ref if r < SHIFT else bottom_ref
        target[r % SHIFT, cols + WIN :, :] = ids[r * WIN : (r + 1) * WIN].astype(BF)

    def run(x):
        q, k, v = w.queries(x, scale)
        outs = []
        for n in range(x.shape[0] // tokens):
            at = slice(n * tokens, (n + 1) * tokens)
            outs.append(attend(q[at], k[at], v[at], bias_ref[...], None, masks, ones))
        return w.finish(x, jnp.concatenate(outs, axis=0).astype(BF))

    group = 4

    def step(i, carry):
        start = pl.multiple_of(i * group * WIN, group * WIN)
        block = x_ref[:, pl.ds(start, group * WIN), :].astype(F32)
        x = jnp.concatenate(
            [block[r, n * WIN : (n + 1) * WIN] for n in range(group) for r in range(WIN)], axis=0
        )
        out = run(x)
        for r in range(WIN):
            row = jnp.concatenate(
                [out[n * tokens + r * WIN : n * tokens + (r + 1) * WIN] for n in range(group)], axis=0
            ).astype(BF)
            target = top_ref if r < SHIFT else bottom_ref
            target[r % SHIFT, pl.ds(start, group * WIN), :] = row
        return carry

    lax.fori_loop(0, cols // (group * WIN), step, 0)
    left = left_ref[0:WIN].astype(F32).reshape(tokens, c)
    right = right_ref[0:WIN].astype(F32).reshape(tokens, c)
    out = run(jnp.concatenate([left, right], axis=0))
    first = lax.broadcasted_iota(jnp.int32, (tokens, c), 0) % WIN < SHIFT
    edge = jnp.where(first, out[tokens:], out[:tokens])
    for r in range(WIN):
        target = top_ref if r < SHIFT else bottom_ref
        target[r % SHIFT, cols : cols + WIN, :] = edge[r * WIN : (r + 1) * WIN].astype(BF)


def shifted_kernel(
    top_ref, bottom_ref, above_ref, below_ref, rel_ref, *refs,
    group, groups, own_heads, entries, part, hidden,
):
    packs, refs = refs[:groups], refs[groups:]
    (out_ref, bias_ref, own_ref, halo_ref, res_ref, qid_ref, kid_ref), scratch = refs[:7], refs[7:]
    c = top_ref.shape[2]
    cols = out_ref.shape[1]
    heads = own_heads * groups
    depth = c // heads
    half = SHIFT * WIN
    tokens = WIN * WIN
    scale = depth ** (-0.5) * LOG2E
    w = Weights(packs, scratch, c, part, hidden)
    w.load()
    masks = head_masks(heads, depth, c)
    ones = jnp.concatenate(masks, axis=0)

    rel = rel_ref[...]
    rel = jnp.concatenate(
        [
            jnp.concatenate([rel[a + SHIFT : a + WIN], rel[a : a + SHIFT]], axis=0)
            for a in range(0, tokens, WIN)
        ],
        axis=0,
    )
    lane = lax.broadcasted_iota(jnp.int32, rel.shape, 1)
    rel = jnp.where(lane % WIN < SHIFT, pltpu.roll(rel, 128 - SHIFT, 1), pltpu.roll(rel, SHIFT, 1))
    rel = jnp.concatenate([pltpu.roll(rel[half:], half, 1), rel[:half]], axis=0)
    bias_ref[...] = w.bias(own_heads, entries - 128, rel)

    for s, (own, halo) in enumerate(((top_ref, above_ref), (bottom_ref, below_ref))):
        parts = []
        for dst, src in ((own_ref, own), (halo_ref, halo)):
            value = src[...].astype(F32)
            edge = value[:, cols : cols + WIN]
            dst[s * SHIFT : (s + 1) * SHIFT, 0:WIN, :] = edge
            dst[s * SHIFT : (s + 1) * SHIFT, WIN : WIN + cols, :] = value[:, :cols]
            dst[s * SHIFT : (s + 1) * SHIFT, WIN + cols :, :] = edge
            parts.append(value[:, cols + WIN :].reshape(half, 128))
        qid_ref[s] = parts[0]
        both = jnp.concatenate(parts + parts, axis=0)
        kid_ref[s] = both.T
    first = lax.broadcasted_iota(jnp.int32, (WIN, group * WIN, c), 1) % WIN < SHIFT

    def step(i, carry):
        start = pl.multiple_of(i * group * WIN, WIN)

        def gather(ref):
            before = ref[:, pl.ds(start, group * WIN), :]
            after = ref[:, pl.ds(start + WIN, group * WIN), :]
            both = jnp.where(first, after, before)
            return jnp.concatenate(
                [
                    both[s * SHIFT + r, n * WIN : (n + 1) * WIN]
                    for n in range(group) for s in range(2) for r in range(SHIFT)
                ],
                axis=0,
            )

        x = gather(own_ref)
        q, k_own, v_own = w.queries(x, scale)
        k_halo, v_halo = w.keys(gather(halo_ref))
        outs = []
        for n in range(group):
            j = i * group + n
            for s in range(2):
                at = slice((n * 2 + s) * half, (n * 2 + s + 1) * half)
                k = jnp.concatenate([k_own[at], k_halo[at]], axis=0)
                v = jnp.concatenate([v_own[at], v_halo[at]], axis=0)
                keys = kid_ref[s, pl.ds(j, 1), :]
                queries = jnp.take_along_axis(qid_ref[s], jnp.full((half, 128), j, jnp.int32), axis=1)
                allowed = jnp.concatenate([queries, queries], axis=1) == jnp.concatenate(
                    [keys, keys], axis=1
                )
                outs.append(
                    attend(q[at], k, v, bias_ref[s * half : (s + 1) * half], allowed, masks, ones)
                )
        out = w.finish(x, jnp.concatenate(outs, axis=0).astype(BF))
        for r in range(WIN):
            s, a = r // SHIFT, r % SHIFT
            res_ref[r, pl.ds(start, group * WIN), :] = jnp.concatenate(
                [
                    out[(n * 2 + s) * half + a * WIN : (n * 2 + s) * half + (a + 1) * WIN]
                    for n in range(group)
                ],
                axis=0,
            )
        return carry

    lax.fori_loop(0, (cols + WIN) // (group * WIN), step, 0)
    low = lax.broadcasted_iota(jnp.int32, (WIN, cols, c), 1) % WIN < SHIFT
    out_ref[...] = jnp.where(low, res_ref[:, 0:cols, :], res_ref[:, WIN : WIN + cols, :]).astype(BF)


def call(kernel, out_shapes, scratch, *args, in_specs=None):
    specs = {} if in_specs is None else {"in_specs": in_specs}
    return pl.pallas_call(
        kernel,
        out_shape=out_shapes,
        scratch_shapes=scratch,
        compiler_params=pltpu.CompilerParams(vmem_limit_bytes=48 * 1024 * 1024),
        **specs,
    )(*args)


def neighbours(axis, by):
    size = lax.axis_size(axis)
    return [(i, i + by) for i in range(size) if 0 <= i + by < size]


def on_device(*args):
    image_tokens, labels, rel_index = args[:3]
    qkv_weight, bias_table, fc1_weight = args[5], args[7], args[10]
    tile_cols, c = image_tokens.shape[1:]
    groups = lax.axis_size("ch")
    swap = [(i, (i + 1) % groups) for i in range(groups)]
    part = qkv_weight.shape[3]
    hidden = fc1_weight.shape[2]
    entries = bias_table.shape[1]
    own_heads = bias_table.shape[2]
    tokens = WIN * WIN

    def others(value):
        found = [value]
        for _ in range(groups - 1):
            found.append(lax.ppermute(found[-1], "ch", swap))
        return found

    rows = 4 * part + (hidden // 128) * c + hidden + 3 * SMALL
    pack = jax.ShapeDtypeStruct((rows, 128), BF)
    edge = jax.ShapeDtypeStruct((WIN + 1, WIN, c), BF)
    staged = [pltpu.VMEM((2, WIN, 2 * WIN, c), BF)] + [pltpu.VMEM(a.shape, a.dtype) for a in args[1:]]
    own0, own1, left_edge, right_edge, rel2 = call(
        lambda *refs: pack_kernel(*refs, count=len(args)),
        (pack, pack, edge, edge, jax.ShapeDtypeStruct((tokens, 2 * tokens), jnp.int32)),
        staged + [pltpu.VMEM((SMALL, 128), F32), pltpu.SemaphoreType.DMA((len(args) + 1,))],
        *args,
        in_specs=[pl.BlockSpec(memory_space=pl.ANY)] * len(args),
    )
    packs0 = others(own0)
    left = lax.ppermute(right_edge, "col", neighbours("col", 1))
    right = lax.ppermute(left_edge, "col", neighbours("col", -1))
    packs1 = others(own1)

    sizes = dict(groups=groups, own_heads=own_heads, entries=entries, part=part, hidden=hidden)
    weights_scratch = [
        pltpu.VMEM((c, 3 * c), BF),
        pltpu.VMEM((c, c), BF),
        pltpu.VMEM((c, groups * hidden), BF),
        pltpu.VMEM((groups * hidden, c), BF),
    ]
    strip = jax.ShapeDtypeStruct((SHIFT, tile_cols + 2 * WIN, c), BF)
    bias_scratch = pltpu.VMEM((tokens, own_heads * groups * tokens), F32)
    top, bottom = call(
        lambda *refs: regular_kernel(*refs, **sizes),
        (strip, strip),
        [bias_scratch] + weights_scratch,
        image_tokens, left, right, labels, rel2, *packs0,
    )
    above = lax.ppermute(bottom, ("row", "ch"), neighbours(("row", "ch"), 1))
    below = lax.ppermute(top, ("row", "ch"), neighbours(("row", "ch"), -1))
    wins = tile_cols // WIN + 1
    group = max(g for g in range(1, 5) if wins % g == 0)
    wide = pltpu.VMEM((WIN, tile_cols + 2 * WIN, c), F32)
    return call(
        lambda *refs: shifted_kernel(*refs, group=group, **sizes),
        jax.ShapeDtypeStruct(image_tokens.shape, BF),
        [
            bias_scratch, wide, wide, pltpu.VMEM((WIN, tile_cols + WIN, c), F32),
            pltpu.VMEM((2, SHIFT * WIN, 128), F32), pltpu.VMEM((2, 128, 128), F32),
        ] + weights_scratch,
        top, bottom, above, below, rel2, *packs1,
    )


def solution(mesh):
    in_specs = (
        P(("row", "ch"), "col", None),
        P(("row", "ch"), "col"),
        P(),
        P(),
        P(),
        P(None, None, None, "ch"),
        P(None, None, "ch"),
        P(None, None, "ch"),
        P(None, "ch", None),
        P(),
        P(None, None, "ch"),
        P(None, "ch"),
        P(None, "ch", None),
        P(),
    )
    out_specs = P(("row", "ch"), "col", None)
    return jax.shard_map(
        on_device, mesh=mesh, in_specs=in_specs, out_specs=out_specs, check_vma=False
    )
```

time: 89.6 us -> 69.8 us (0.78)
  starting transfers between devices: 25.9 us -> 13.6 us
  local copies, waits for them, and re-layouts: 16.3 us -> 6 us
  waiting for transfers between devices: 12.1 us -> 15.9 us
  other arithmetic: 1.17 us -> 0 us
    ppermute x3 -> x2, waiting for transfers between devices: 0.57 us -> 12.8 us  [others(): found.append(lax.ppermute(found[-1], 'ch', swap))]
    ppermute x6 -> x2, starting transfers between devices: 16.8 us -> 5.87 us  [the longest x1 3.95 us: on_device(): left = lax.ppermute(right_edge, 'col', neighbours('col', 1))]
    ppermute x1, waiting for transfers between devices: 8.8 us -> 0.01 us  [on_device(): above = lax.ppermute(bottom, ('row', 'ch'), neighbours(('row', 'ch'), 1))]
    rev x2 -> x0, local copies, waits for them, and re-layouts: 3.26 us -> none  [the longest x1 1.86 us: on_device(): cells = region.reshape(4, SHIFT, wins, 2, SHIFT)[:, :, :, ::-1, :]]
    ppermute x6 -> x2, waiting for transfers between devices: 0.76 us -> 3.14 us  [the longest x1 3.14 us: on_device(): right = lax.ppermute(left_edge, 'col', neighbours('col', -1))]
    slice x17 -> x0, local copies, waits for them, and re-layouts: 2.38 us -> none  [the longest x2 0.79 us: padded(): last = lax.slice_in_dim(shard, length - width, length, axis=dim)]
    unnamed x43 -> x25, local copies, waits for them, and re-layouts: 8.16 us -> 6 us
    ppermute x1, waiting for transfers between devices: 1.95 us -> 0.01 us  [on_device(): below = lax.ppermute(top, ('row', 'ch'), neighbours(('row', 'ch'), -1))]
  transfers between devices with their start and end apart: 11 -> 6, of which waited for: 4 -> 2; matrix products, arithmetic and copies ran while one was open for 12% -> 0% of each run, Pallas kernels for 15% -> 0%
where the time goes in v1:
time: 69.8 us; the launch traced here: 68.8 us
  Pallas kernels  33.1 us (47%)
  waiting for transfers between devices  15.9 us (23%)
  starting transfers between devices  13.6 us (19%)
  local copies, waits for them, and re-layouts  6 us (9%)
    pallas_call x3, Pallas kernels, call(): pl.pallas_call(kernel, out_shape=out_shapes, scratch_shapes=scratch, comp...  33.1 us
    ppermute x2, waiting for transfers between devices, others(): found.append(lax.ppermute(found[-1], 'ch', swap))  12.8 us
    unnamed x25, local copies, waits for them, and re-layouts  6 us
    ppermute x1, starting transfers between devices, on_device(): left = lax.ppermute(right_edge, 'col', neighbours('col', 1))  3.95 us
    ppermute x1, starting transfers between devices, on_device(): above = lax.ppermute(bottom, ('row', 'ch'), neighbours(('row', 'ch'), 1))  3.26 us
    ppermute x1, waiting for transfers between devices, on_device(): right = lax.ppermute(left_edge, 'col', neighbours('col', -1))  3.14 us
    ppermute x2, starting transfers between devices, others(): found.append(lax.ppermute(found[-1], 'ch', swap))  2.43 us
    ppermute x1, starting transfers between devices, on_device(): below = lax.ppermute(top, ('row', 'ch'), neighbours(('row', 'ch'), -1))  2.02 us
  transfers between devices with their start and end apart: 6, of which 2 were waited for; matrix products, arithmetic and copies ran while one was open for 0% of the time, Pallas kernels for 0%

profile of v1, /device:TPU:9, one launch (start us, length us, event | category | flops | bytes accessed | tf_op | source)
XLA Modules:
  0.0 68.8 jit_solution(12430755138948037635)
XLA Ops:
  0.0 0.0 copy-start
  0.0 0.7 %copy.16.refs_6_ = f32[2,3,64]{2,1,0:T(4,128)S(1)} copy(f32[2,3,64]{2,0,1:T(2,128)} %param.20) | data formatting | bytes 3072 | tf_op args[6]
  0.7 1.1 %copy.15.refs_5_ = bf16[2,3,128,64]{3,2,1,0:T(8,128)(2,1)S(1)} copy(bf16[2,3,128,64]{2,3,1,0:T(8,128)(2,1)} %param.19) | data formatting | bytes 196608 | tf_op args[5]
  1.8 0.0 copy-start.3
  1.8 0.0 copy-start.6
  1.8 0.0 copy-start.7
  1.8 0.0 copy-start.8
  1.9 0.0 copy-start.9
  1.9 0.0 copy-start.10
  1.9 0.8 %copy.17.refs_7_ = f32[2,225,2]{2,1,0:T(8,128)S(1)} copy(f32[2,225,2]{1,2,0:T(2,128)} %param.21) | data formatting | bytes 7200 | tf_op args[7]
  2.7 0.0 copy-done
  2.7 0.0 copy-done.3
  2.7 0.0 copy-done.6
  2.8 0.0 copy-done.7
  2.8 0.0 copy-done.8
  2.8 0.0 copy-done.9
  2.8 0.0 copy-done.10
  2.8 0.0 copy-start.1
  2.8 0.9 %copy-done.1 = bf16[2,128,256]{2,1,0:T(8,128)(2,1)S(1)} copy-done((bf16[2,128,256]{2,1,0:T(8,128)(2,1)S(1)}, bf16[2,128,256]{2,1,0:T(8,128)(2,1)}, u32[]{:S(2)}) %copy-start.1) | copy-done | bytes 131096
  3.7 0.0 copy-start.2
  3.7 0.9 %copy-done.2 = bf16[2,256,128]{2,1,0:T(8,128)(2,1)S(1)} copy-done((bf16[2,256,128]{2,1,0:T(8,128)(2,1)S(1)}, bf16[2,256,128]{2,1,0:T(8,128)(2,1)}, u32[]{:S(2)}) %copy-start.2) | copy-done | bytes 131096
  4.6 0.0 copy-start.4
  4.6 0.8 %copy-done.4 = s32[64,64]{1,0:T(8,128)S(1)} copy-done((s32[64,64]{1,0:T(8,128)S(1)}, s32[64,64]{1,0:T(8,128)}, u32[]{:S(2)}) %copy-start.4) | copy-done | bytes 16408
  5.4 0.0 copy-start.5
  5.4 0.8 %copy-done.5 = bf16[2,64,128]{2,1,0:T(8,128)(2,1)S(1)} copy-done((bf16[2,64,128]{2,1,0:T(8,128)(2,1)S(1)}, bf16[2,64,128]{2,1,0:T(8,128)(2,1)}, u32[]{:S(2)}) %copy-start.5) | copy-done | bytes 32792
  6.1 1.5 %shard_map.136 = (bf16[816,128]{1,0:T(8,128)(2,1)S(1)}, bf16[816,128]{1,0:T(8,128)(2,1)S(1)}, bf16[9,8,128]{2,1,0:T(8,128)(2,1)S(1)}, bf16[9,8,128]{2,1,0:T(8,128)(2,1)S(1)}, s32[64,128]{1,0:T(8,128)S(1)}) custom-call(bf16[8,256,128]{2,1,0:T(8,128)(2,1)S(1)} %copy-done, s32[8,256]{1,0:T(8,128)S(1)} %copy-done.3, s32[64,64]{1,0:T(8,128)S(1)} %copy-done.4, ...), custom_call_target="tpu_custom_call" | custom-call | tf_op jit(solution)/shard_map/pallas_call | solution.py:403
  7.6 1.3 %collective-permute-start.2 = (bf16[816,128]{1,0:T(8,128)(2,1)S(1)}, bf16[816,128]{1,0:T(8,128)(2,1)S(1)}, u32[]{:S(2)}, u32[]{:S(2)}) collective-permute-start(bf16[816,128]{1,0:T(8,128)(2,1)S(1)} %get-tuple-element.15.refs_5_), channel_id=1, source_target_pairs={{0,1},{1,0},{2,3},{3,2},{4,5},{5,4},{6,7},{7,6},{8,9},{9,8},{10,11... | collective-permute-start | bytes 626696 | tf_op jit(solution)/shard_map/ppermute | solution.py:432
  8.9 3.9 %collective-permute-start = (bf16[9,8,128]{2,1,0:T(8,128)(2,1)S(1)}, bf16[9,8,128]{2,1,0:T(8,128)(2,1)S(1)}, u32[]{:S(2)}, u32[]{:S(2)}) collective-permute-start(bf16[9,8,128]{2,1,0:T(8,128)(2,1)S(1)} %get-tuple-element.12), channel_id=1, source_target_pairs={{0,2},{2,4},{4,6},{1,3},{3,5},{5,7},{8,10},{10,12},{12,14},{9,11},... | collective-permute-start | bytes 55304 | tf_op jit(solution)/shard_map/ppermute | solution.py:447
  12.9 1.9 %collective-permute-start.1 = (bf16[9,8,128]{2,1,0:T(8,128)(2,1)S(1)}, bf16[9,8,128]{2,1,0:T(8,128)(2,1)S(1)}, u32[]{:S(2)}, u32[]{:S(2)}) collective-permute-start(bf16[9,8,128]{2,1,0:T(8,128)(2,1)S(1)} %get-tuple-element.13), channel_id=1, source_target_pairs={{2,0},{4,2},{6,4},{3,1},{5,3},{7,5},{10,8},{12,10},{14,12},{11,9},... | collective-permute-start | bytes 55304 | tf_op jit(solution)/shard_map/ppermute | solution.py:448
  14.8 0.0 collective-permute-done.refs_1_
  14.8 3.1 %collective-permute-done.1.refs_2_ = bf16[9,8,128]{2,1,0:T(8,128)(2,1)S(1)} collective-permute-done((bf16[9,8,128]{2,1,0:T(8,128)(2,1)S(1)}, bf16[9,8,128]{2,1,0:T(8,128)(2,1)S(1)}, u32[]{:S(2)}, u32[]{:S(2)}) %collective-permute-start.1) | collective-permute-done | bytes 18464 | tf_op jit(solution)/shard_map/ppermute | solution.py:448
  17.9 0.0 collective-permute-done.2.refs_6_
  18.0 13.3 %shard_map.137 = (bf16[4,272,128]{2,1,0:T(8,128)(2,1)S(1)}, bf16[4,272,128]{2,1,0:T(8,128)(2,1)S(1)}) custom-call(bf16[8,256,128]{2,1,0:T(8,128)(2,1)S(1)} %copy-done, bf16[9,8,128]{2,1,0:T(8,128)(2,1)S(1)} %collective-permute-done.refs_1_, bf16[9,8,128]{2,1,0:T(8,128)(2,1)S(1)} %collective-permute-done.1.refs_2_, s32[8,256]{1,0:T(8,128)S(1)} %copy-done.3, ...), custom_call_target="tpu_custom_call" | custom-call | tf_op jit(solution)/shard_map/pallas_call | solution.py:403
  31.3 2.0 %collective-permute-start.4 = (bf16[4,272,128]{2,1,0:T(8,128)(2,1)S(1)}, bf16[4,272,128]{2,1,0:T(8,128)(2,1)S(1)}, u32[]{:S(2)}, u32[]{:S(2)}) collective-permute-start(bf16[4,272,128]{2,1,0:T(8,128)(2,1)S(1)} %get-tuple-element.16.refs_0_), channel_id=1, source_target_pairs={{1,0},{8,1},{9,8},{16,9},{17,16},{24,17},{25,24},{3,2},{10,3},{11,... | collective-permute-start | bytes 835592 | tf_op jit(solution)/shard_map/ppermute | solution.py:467
  33.3 3.3 %collective-permute-start.3 = (bf16[4,272,128]{2,1,0:T(8,128)(2,1)S(1)}, bf16[4,272,128]{2,1,0:T(8,128)(2,1)S(1)}, u32[]{:S(2)}, u32[]{:S(2)}) collective-permute-start(bf16[4,272,128]{2,1,0:T(8,128)(2,1)S(1)} %get-tuple-element.17.refs_1_), channel_id=1, source_target_pairs={{0,1},{1,8},{8,9},{9,16},{16,17},{17,24},{24,25},{2,3},{3,10},{10,... | collective-permute-start | bytes 835592 | tf_op jit(solution)/shard_map/ppermute | solution.py:466
  36.6 1.1 %collective-permute-start.5 = (bf16[816,128]{1,0:T(8,128)(2,1)S(1)}, bf16[816,128]{1,0:T(8,128)(2,1)S(1)}, u32[]{:S(2)}, u32[]{:S(2)}) collective-permute-start(bf16[816,128]{1,0:T(8,128)(2,1)S(1)} %get-tuple-element.18.refs_5_), channel_id=1, source_target_pairs={{0,1},{1,0},{2,3},{3,2},{4,5},{5,4},{6,7},{7,6},{8,9},{9,8},{10,11... | collective-permute-start | bytes 626696 | tf_op jit(solution)/shard_map/ppermute | solution.py:432
  37.7 12.8 %collective-permute-done.5.refs_6_ = bf16[816,128]{1,0:T(8,128)(2,1)S(1)} collective-permute-done((bf16[816,128]{1,0:T(8,128)(2,1)S(1)}, bf16[816,128]{1,0:T(8,128)(2,1)S(1)}, u32[]{:S(2)}, u32[]{:S(2)}) %collective-permute-start.5) | collective-permute-done | bytes 208928 | tf_op jit(solution)/shard_map/ppermute | solution.py:432
  50.5 0.0 collective-permute-done.4.refs_3_
  50.5 0.0 collective-permute-done.3.refs_2_
  50.5 18.3 %shard_map.138 = bf16[8,256,128]{2,1,0:T(8,128)(2,1)} custom-call(bf16[4,272,128]{2,1,0:T(8,128)(2,1)S(1)} %get-tuple-element.16.refs_0_, bf16[4,272,128]{2,1,0:T(8,128)(2,1)S(1)} %get-tuple-element.17.refs_1_, bf16[4,272,128]{2,1,0:T(8,128)(2,1)S(1)} %collective-permute-done.3.refs_2_, bf16[4,272,128]{2,1,0:T(8,128)(2,1)S(1)} %collective-permute-done.4.refs_3_, ...), custom_call_target="tpu_custom_call" | custom-call | tf_op jit(solution)/shard_map/pallas_call | solution.py:403
Async XLA Ops:
  0.0 2.7 %copy-start = (bf16[8,256,128]{2,1,0:T(8,128)(2,1)S(1)}, bf16[8,256,128]{2,1,0:T(8,128)(2,1)}, u32[]{:S(2)}) copy-start(bf16[8,256,128]{2,1,0:T(8,128)(2,1)} %refs_0_.3) | copy-start | bytes 1572868
  1.8 0.9 %copy-start.3 = (s32[8,256]{1,0:T(8,128)S(1)}, s32[8,256]{1,0:T(8,128)}, u32[]{:S(2)}) copy-start(s32[8,256]{1,0:T(8,128)} %refs_3_.3) | copy-start | bytes 24580
  1.8 0.9 %copy-start.6 = (f32[2,2,128]{2,1,0:T(2,128)S(1)}, f32[2,2,128]{2,1,0:T(2,128)}, u32[]{:S(2)}) copy-start(f32[2,2,128]{2,1,0:T(2,128)} %refs_3_.2) | copy-start | bytes 6148
  1.8 0.9 %copy-start.7 = (f32[2,2,128]{2,1,0:T(2,128)S(1)}, f32[2,2,128]{2,1,0:T(2,128)}, u32[]{:S(2)}) copy-start(f32[2,2,128]{2,1,0:T(2,128)} %refs_4_.1) | copy-start | bytes 6148
  1.8 0.9 %copy-start.8 = (f32[2,256]{1,0:T(2,128)S(1)}, f32[2,256]{1,0:T(2,128)}, u32[]{:S(2)}) copy-start(f32[2,256]{1,0:T(2,128)} %refs_11_.1) | copy-start | bytes 6148
  1.9 0.9 %copy-start.9 = (f32[2,128]{1,0:T(2,128)S(1)}, f32[2,128]{1,0:T(2,128)}, u32[]{:S(2)}) copy-start(f32[2,128]{1,0:T(2,128)} %refs_9_.1) | copy-start | bytes 3076
  1.9 0.9 %copy-start.10 = (f32[2,128]{1,0:T(2,128)S(1)}, f32[2,128]{1,0:T(2,128)}, u32[]{:S(2)}) copy-start(f32[2,128]{1,0:T(2,128)} %refs_13_.1) | copy-start | bytes 3076
  2.8 0.9 %copy-start.1 = (bf16[2,128,256]{2,1,0:T(8,128)(2,1)S(1)}, bf16[2,128,256]{2,1,0:T(8,128)(2,1)}, u32[]{:S(2)}) copy-start(bf16[2,128,256]{2,1,0:T(8,128)(2,1)} %refs_10_.1) | copy-start | bytes 393220
  3.7 0.9 %copy-start.2 = (bf16[2,256,128]{2,1,0:T(8,128)(2,1)S(1)}, bf16[2,256,128]{2,1,0:T(8,128)(2,1)}, u32[]{:S(2)}) copy-start(bf16[2,256,128]{2,1,0:T(8,128)(2,1)} %refs_12_.1) | copy-start | bytes 393220
  4.6 0.8 %copy-start.4 = (s32[64,64]{1,0:T(8,128)S(1)}, s32[64,64]{1,0:T(8,128)}, u32[]{:S(2)}) copy-start(s32[64,64]{1,0:T(8,128)} %refs_2_.1) | copy-start | bytes 49156
  5.4 0.8 %copy-start.5 = (bf16[2,64,128]{2,1,0:T(8,128)(2,1)S(1)}, bf16[2,64,128]{2,1,0:T(8,128)(2,1)}, u32[]{:S(2)}) copy-start(bf16[2,64,128]{2,1,0:T(8,128)(2,1)} %refs_8_.1) | copy-start | bytes 98308
  7.6 10.3 %collective-permute-start.2 = (bf16[816,128]{1,0:T(8,128)(2,1)S(1)}, bf16[816,128]{1,0:T(8,128)(2,1)S(1)}, u32[]{:S(2)}, u32[]{:S(2)}) collective-permute-start(bf16[816,128]{1,0:T(8,128)(2,1)S(1)} %get-tuple-element.15.refs_5_), channel_id=1, source_target_pairs={{0,1},{1,0},{2,3},{3,2},{4,5},{5,4},{6,7},{7,6},{8,9},{9,8},{10,11... | collective-permute-start | bytes 626696 | tf_op jit(solution)/shard_map/ppermute | solution.py:432
  8.9 5.9 %collective-permute-start = (bf16[9,8,128]{2,1,0:T(8,128)(2,1)S(1)}, bf16[9,8,128]{2,1,0:T(8,128)(2,1)S(1)}, u32[]{:S(2)}, u32[]{:S(2)}) collective-permute-start(bf16[9,8,128]{2,1,0:T(8,128)(2,1)S(1)} %get-tuple-element.12), channel_id=1, source_target_pairs={{0,2},{2,4},{4,6},{1,3},{3,5},{5,7},{8,10},{10,12},{12,14},{9,11},... | collective-permute-start | bytes 55304 | tf_op jit(solution)/shard_map/ppermute | solution.py:447
  12.9 5.1 %collective-permute-start.1 = (bf16[9,8,128]{2,1,0:T(8,128)(2,1)S(1)}, bf16[9,8,128]{2,1,0:T(8,128)(2,1)S(1)}, u32[]{:S(2)}, u32[]{:S(2)}) collective-permute-start(bf16[9,8,128]{2,1,0:T(8,128)(2,1)S(1)} %get-tuple-element.13), channel_id=1, source_target_pairs={{2,0},{4,2},{6,4},{3,1},{5,3},{7,5},{10,8},{12,10},{14,12},{11,9},... | collective-permute-start | bytes 55304 | tf_op jit(solution)/shard_map/ppermute | solution.py:448
  31.3 19.2 %collective-permute-start.4 = (bf16[4,272,128]{2,1,0:T(8,128)(2,1)S(1)}, bf16[4,272,128]{2,1,0:T(8,128)(2,1)S(1)}, u32[]{:S(2)}, u32[]{:S(2)}) collective-permute-start(bf16[4,272,128]{2,1,0:T(8,128)(2,1)S(1)} %get-tuple-element.16.refs_0_), channel_id=1, source_target_pairs={{1,0},{8,1},{9,8},{16,9},{17,16},{24,17},{25,24},{3,2},{10,3},{11,... | collective-permute-start | bytes 835592 | tf_op jit(solution)/shard_map/ppermute | solution.py:467
  33.3 17.2 %collective-permute-start.3 = (bf16[4,272,128]{2,1,0:T(8,128)(2,1)S(1)}, bf16[4,272,128]{2,1,0:T(8,128)(2,1)S(1)}, u32[]{:S(2)}, u32[]{:S(2)}) collective-permute-start(bf16[4,272,128]{2,1,0:T(8,128)(2,1)S(1)} %get-tuple-element.17.refs_1_), channel_id=1, source_target_pairs={{0,1},{1,8},{8,9},{9,16},{16,17},{17,24},{24,25},{2,3},{3,10},{10,... | collective-permute-start | bytes 835592 | tf_op jit(solution)/shard_map/ppermute | solution.py:466
  36.6 13.9 %collective-permute-start.5 = (bf16[816,128]{1,0:T(8,128)(2,1)S(1)}, bf16[816,128]{1,0:T(8,128)(2,1)S(1)}, u32[]{:S(2)}, u32[]{:S(2)}) collective-permute-start(bf16[816,128]{1,0:T(8,128)(2,1)S(1)} %get-tuple-element.18.refs_5_), channel_id=1, source_target_pairs={{0,1},{1,0},{2,3},{3,2},{4,5},{5,4},{6,7},{7,6},{8,9},{9,8},{10,11... | collective-permute-start | bytes 626696 | tf_op jit(solution)/shard_map/ppermute | solution.py:432

commit v2 on v1

--- a/solution.py
+++ b/solution.py
@@ -6,6 +6,7 @@
 from jax.experimental import pallas as pl
 from jax.experimental.pallas import tpu as pltpu
 from jax.sharding import PartitionSpec as P
+
 
 WIN = 8
 SHIFT = 4
@@ -113,13 +114,13 @@
         copy.wait()
     (x, labels, rel, gain, shift, qkv, qkvb, table, proj, projb, fc1, fc1b, fc2, fc2b) = staged
     c = x.shape[3]
-    part = qkv.shape[3]
+    part = qkv.shape[2]
     hidden = fc1.shape[2]
-    entries = table.shape[1]
+    entries = table.shape[2]
     for b, out in enumerate((w0_ref, w1_ref)):
         at = 0
         for m in range(3):
-            out[at : at + part, :] = qkv[b, m].astype(F32).T.astype(BF)
+            out[at : at + part, :] = qkv[b, m]
             at += part
         out[at : at + part, :] = proj[b]
         at += part
@@ -129,14 +130,14 @@
         out[at : at + hidden, :] = fc2[b]
         at += hidden
         small_ref[...] = jnp.zeros_like(small_ref)
-        small_ref[QKVB : QKVB + 3, 0:part] = qkvb[b]
+        for m in range(3):
+            small_ref[QKVB + m : QKVB + m + 1, 0:part] = qkvb[m, b : b + 1]
         for k in range(hidden // 128):
             small_ref[FC1B + k : FC1B + k + 1, :] = fc1b[b : b + 1, k * 128 : (k + 1) * 128]
         k = TABLE
-        for h in range(table.shape[2]):
+        for h in range(table.shape[1]):
             for first in (0, entries - 128):
-                column = table[b, first : first + 128, h : h + 1]
-                small_ref[k : k + 1, :] = jnp.broadcast_to(column, (128, 128)).T[0:1]
+                small_ref[k : k + 1, :] = table[b, h : h + 1, first : first + 128]
                 k += 1
         small_ref[GAIN : GAIN + 2, :] = gain[b]
         small_ref[SHIFTS : SHIFTS + 2, :] = shift[b]
@@ -229,10 +230,14 @@
 
 
 def regular_kernel(
-    x_ref, left_ref, right_ref, labels_ref, rel_ref, *refs, groups, own_heads, entries, part, hidden
+    x_hbm, labels_hbm, left_ref, right_ref, rel_ref, *refs, groups, own_heads, entries, part, hidden
 ):
     packs, refs = refs[:groups], refs[groups:]
-    (top_ref, bottom_ref, bias_ref), scratch = refs[:3], refs[3:]
+    (top_ref, bottom_ref, bias_ref, x_ref, labels_ref, sems), scratch = refs[:6], refs[6:]
+    x_copy = pltpu.make_async_copy(x_hbm, x_ref, sems.at[0])
+    labels_copy = pltpu.make_async_copy(labels_hbm, labels_ref, sems.at[1])
+    x_copy.start()
+    labels_copy.start()
     c = x_ref.shape[2]
     cols = x_ref.shape[1]
     heads = own_heads * groups
@@ -245,6 +250,7 @@
     ones = jnp.concatenate(masks, axis=0)
     bias_ref[...] = w.bias(own_heads, entries - 128, rel_ref[...])
 
+    labels_copy.wait()
     lanes = jnp.concatenate(
         [
             left_ref[WIN].astype(F32),
@@ -292,6 +298,7 @@
             target[r % SHIFT, pl.ds(start, group * WIN), :] = row
         return carry
 
+    x_copy.wait()
     lax.fori_loop(0, cols // (group * WIN), step, 0)
     left = left_ref[0:WIN].astype(F32).reshape(tokens, c)
     right = right_ref[0:WIN].astype(F32).reshape(tokens, c)
@@ -409,13 +416,17 @@
     )(*args)
 
 
+def in_hbm(value):
+    return pltpu.with_memory_space_constraint(value, pltpu.HBM)
+
+
 def neighbours(axis, by):
     size = lax.axis_size(axis)
     return [(i, i + by) for i in range(size) if 0 <= i + by < size]
 
 
-def on_device(*args):
-    image_tokens, labels, rel_index = args[:3]
+def both_blocks(*args):
+    image_tokens, labels, _ = args[:3]
     qkv_weight, bias_table, fc1_weight = args[5], args[7], args[10]
     tile_cols, c = image_tokens.shape[1:]
     groups = lax.axis_size("ch")
@@ -435,13 +446,17 @@
     rows = 4 * part + (hidden // 128) * c + hidden + 3 * SMALL
     pack = jax.ShapeDtypeStruct((rows, 128), BF)
     edge = jax.ShapeDtypeStruct((WIN + 1, WIN, c), BF)
+    args = list(args)
+    args[5] = qkv_weight.transpose(0, 1, 3, 2)
+    args[6] = args[6].transpose(1, 0, 2)
+    args[7] = bias_table.transpose(0, 2, 1)
     staged = [pltpu.VMEM((2, WIN, 2 * WIN, c), BF)] + [pltpu.VMEM(a.shape, a.dtype) for a in args[1:]]
     own0, own1, left_edge, right_edge, rel2 = call(
         lambda *refs: pack_kernel(*refs, count=len(args)),
         (pack, pack, edge, edge, jax.ShapeDtypeStruct((tokens, 2 * tokens), jnp.int32)),
         staged + [pltpu.VMEM((SMALL, 128), F32), pltpu.SemaphoreType.DMA((len(args) + 1,))],
-        *args,
-        in_specs=[pl.BlockSpec(memory_space=pl.ANY)] * len(args),
+        *(in_hbm(a) for a in args),
+        in_specs=[pl.BlockSpec(memory_space=pltpu.HBM)] * len(args),
     )
     packs0 = others(own0)
     left = lax.ppermute(right_edge, "col", neighbours("col", 1))
@@ -460,8 +475,13 @@
     top, bottom = call(
         lambda *refs: regular_kernel(*refs, **sizes),
         (strip, strip),
-        [bias_scratch] + weights_scratch,
-        image_tokens, left, right, labels, rel2, *packs0,
+        [
+            bias_scratch, pltpu.VMEM(image_tokens.shape, BF), pltpu.VMEM(labels.shape, jnp.int32),
+            pltpu.SemaphoreType.DMA((2,)),
+        ] + weights_scratch,
+        in_hbm(image_tokens), in_hbm(labels), left, right, rel2, *packs0,
+        in_specs=[pl.BlockSpec(memory_space=pltpu.HBM)] * 2
+        + [pl.BlockSpec(memory_space=pltpu.VMEM)] * (3 + groups),
     )
     above = lax.ppermute(bottom, ("row", "ch"), neighbours(("row", "ch"), 1))
     below = lax.ppermute(top, ("row", "ch"), neighbours(("row", "ch"), -1))
@@ -498,5 +518,5 @@
     )
     out_specs = P(("row", "ch"), "col", None)
     return jax.shard_map(
-        on_device, mesh=mesh, in_specs=in_specs, out_specs=out_specs, check_vma=False
-    )
+        both_blocks, mesh=mesh, in_specs=in_specs, out_specs=out_specs, check_vma=False
+    )

time: 69.8 us -> 64.2 us (0.920)
  local copies, waits for them, and re-layouts: 6 us -> 0 us
  Pallas kernels: 33.1 us -> 33.8 us
    unnamed x25 -> x0, local copies, waits for them, and re-layouts: 6 us -> none
    pallas_call x3, Pallas kernels: 33.1 us -> 33.8 us  [call(): pl.pallas_call(kernel, out_shape=out_shapes, scratch_shapes=scratch, comp...]
where the time goes in v2:
time: 64.2 us; the launch traced here: 63.4 us
  Pallas kernels  33.8 us (53%)
  waiting for transfers between devices  15.9 us (25%)
  starting transfers between devices  13.6 us (21%)
    pallas_call x3, Pallas kernels, call(): pl.pallas_call(kernel, out_shape=out_shapes, scratch_shapes=scratch, comp...  33.8 us
    ppermute x2, waiting for transfers between devices, others(): found.append(lax.ppermute(found[-1], 'ch', swap))  12.7 us
    ppermute x1, starting transfers between devices, both_blocks(): left = lax.ppermute(right_edge, 'col', neighbours('col', 1))  3.95 us
    ppermute x1, starting transfers between devices, both_blocks(): above = lax.ppermute(bottom, ('row', 'ch'), neighbours(('row', 'ch'), 1))  3.26 us
    ppermute x1, waiting for transfers between devices, both_blocks(): right = lax.ppermute(left_edge, 'col', neighbours('col', -1))  3.14 us
    ppermute x2, starting transfers between devices, others(): found.append(lax.ppermute(found[-1], 'ch', swap))  2.5 us
    ppermute x1, starting transfers between devices, both_blocks(): below = lax.ppermute(top, ('row', 'ch'), neighbours(('row', 'ch'), -1))  2.02 us
    ppermute x1, starting transfers between devices, both_blocks(): right = lax.ppermute(left_edge, 'col', neighbours('col', -1))  1.92 us
  transfers between devices with their start and end apart: 6, of which 2 were waited for; matrix products, arithmetic and copies ran while one was open for 0% of the time, Pallas kernels for 0%

profile of v2, /device:TPU:9, one launch (start us, length us, event | category | flops | bytes accessed | tf_op | source)
XLA Modules:
  0.0 63.4 jit_solution(11626219548957535247)
XLA Ops:
  0.0 1.4 %shard_map.136 = (bf16[816,128]{1,0:T(8,128)(2,1)S(1)}, bf16[816,128]{1,0:T(8,128)(2,1)S(1)}, bf16[9,8,128]{2,1,0:T(8,128)(2,1)S(1)}, bf16[9,8,128]{2,1,0:T(8,128)(2,1)S(1)}, s32[64,128]{1,0:T(8,128)S(1)}) custom-call(bf16[8,256,128]{2,1,0:T(8,128)(2,1)} %refs_0_.3, s32[8,256]{1,0:T(8,128)} %refs_1_.3, s32[64,64]{1,0:T(8,128)} %refs_2_.1, ...), custom_call_target="tpu_custom_call" | custom-call | tf_op jit(solution)/shard_map/pallas_call | solution.py:410
  1.4 1.3 %collective-permute-start.2 = (bf16[816,128]{1,0:T(8,128)(2,1)S(1)}, bf16[816,128]{1,0:T(8,128)(2,1)S(1)}, u32[]{:S(2)}, u32[]{:S(2)}) collective-permute-start(bf16[816,128]{1,0:T(8,128)(2,1)S(1)} %get-tuple-element.15.refs_5_), channel_id=1, source_target_pairs={{0,1},{1,0},{2,3},{3,2},{4,5},{5,4},{6,7},{7,6},{8,9},{9,8},{10,11... | collective-permute-start | bytes 626696 | tf_op jit(solution)/shard_map/ppermute | solution.py:443
  2.7 3.9 %collective-permute-start = (bf16[9,8,128]{2,1,0:T(8,128)(2,1)S(1)}, bf16[9,8,128]{2,1,0:T(8,128)(2,1)S(1)}, u32[]{:S(2)}, u32[]{:S(2)}) collective-permute-start(bf16[9,8,128]{2,1,0:T(8,128)(2,1)S(1)} %get-tuple-element.12), channel_id=1, source_target_pairs={{0,2},{2,4},{4,6},{1,3},{3,5},{5,7},{8,10},{10,12},{12,14},{9,11},... | collective-permute-start | bytes 55304 | tf_op jit(solution)/shard_map/ppermute | solution.py:462
  6.7 1.9 %collective-permute-start.1 = (bf16[9,8,128]{2,1,0:T(8,128)(2,1)S(1)}, bf16[9,8,128]{2,1,0:T(8,128)(2,1)S(1)}, u32[]{:S(2)}, u32[]{:S(2)}) collective-permute-start(bf16[9,8,128]{2,1,0:T(8,128)(2,1)S(1)} %get-tuple-element.13), channel_id=1, source_target_pairs={{2,0},{4,2},{6,4},{3,1},{5,3},{7,5},{10,8},{12,10},{14,12},{11,9},... | collective-permute-start | bytes 55304 | tf_op jit(solution)/shard_map/ppermute | solution.py:463
  8.6 0.0 collective-permute-done.refs_2_
  8.6 3.1 %collective-permute-done.1.refs_3_ = bf16[9,8,128]{2,1,0:T(8,128)(2,1)S(1)} collective-permute-done((bf16[9,8,128]{2,1,0:T(8,128)(2,1)S(1)}, bf16[9,8,128]{2,1,0:T(8,128)(2,1)S(1)}, u32[]{:S(2)}, u32[]{:S(2)}) %collective-permute-start.1) | collective-permute-done | bytes 18464 | tf_op jit(solution)/shard_map/ppermute | solution.py:463
  11.8 0.0 collective-permute-done.2.refs_6_
  11.8 14.1 %shard_map.137 = (bf16[4,272,128]{2,1,0:T(8,128)(2,1)S(1)}, bf16[4,272,128]{2,1,0:T(8,128)(2,1)S(1)}) custom-call(bf16[8,256,128]{2,1,0:T(8,128)(2,1)} %refs_0_.3, s32[8,256]{1,0:T(8,128)} %refs_1_.3, bf16[9,8,128]{2,1,0:T(8,128)(2,1)S(1)} %collective-permute-done.refs_2_, bf16[9,8,128]{2,1,0:T(8,128)(2,1)S(1)} %collective-permute-done.1.refs_3_, ...), custom_call_target="tpu_custom_call" | custom-call | tf_op jit(solution)/shard_map/pallas_call | solution.py:410
  25.9 2.0 %collective-permute-start.4 = (bf16[4,272,128]{2,1,0:T(8,128)(2,1)S(1)}, bf16[4,272,128]{2,1,0:T(8,128)(2,1)S(1)}, u32[]{:S(2)}, u32[]{:S(2)}) collective-permute-start(bf16[4,272,128]{2,1,0:T(8,128)(2,1)S(1)} %get-tuple-element.16.refs_0_), channel_id=1, source_target_pairs={{1,0},{8,1},{9,8},{16,9},{17,16},{24,17},{25,24},{3,2},{10,3},{11,... | collective-permute-start | bytes 835592 | tf_op jit(solution)/shard_map/ppermute | solution.py:487
  27.9 3.3 %collective-permute-start.3 = (bf16[4,272,128]{2,1,0:T(8,128)(2,1)S(1)}, bf16[4,272,128]{2,1,0:T(8,128)(2,1)S(1)}, u32[]{:S(2)}, u32[]{:S(2)}) collective-permute-start(bf16[4,272,128]{2,1,0:T(8,128)(2,1)S(1)} %get-tuple-element.17.refs_1_), channel_id=1, source_target_pairs={{0,1},{1,8},{8,9},{9,16},{16,17},{17,24},{24,25},{2,3},{3,10},{10,... | collective-permute-start | bytes 835592 | tf_op jit(solution)/shard_map/ppermute | solution.py:486
  31.2 1.2 %collective-permute-start.5 = (bf16[816,128]{1,0:T(8,128)(2,1)S(1)}, bf16[816,128]{1,0:T(8,128)(2,1)S(1)}, u32[]{:S(2)}, u32[]{:S(2)}) collective-permute-start(bf16[816,128]{1,0:T(8,128)(2,1)S(1)} %get-tuple-element.18.refs_5_), channel_id=1, source_target_pairs={{0,1},{1,0},{2,3},{3,2},{4,5},{5,4},{6,7},{7,6},{8,9},{9,8},{10,11... | collective-permute-start | bytes 626696 | tf_op jit(solution)/shard_map/ppermute | solution.py:443
  32.4 12.7 %collective-permute-done.5.refs_6_ = bf16[816,128]{1,0:T(8,128)(2,1)S(1)} collective-permute-done((bf16[816,128]{1,0:T(8,128)(2,1)S(1)}, bf16[816,128]{1,0:T(8,128)(2,1)S(1)}, u32[]{:S(2)}, u32[]{:S(2)}) %collective-permute-start.5) | collective-permute-done | bytes 208928 | tf_op jit(solution)/shard_map/ppermute | solution.py:443
  45.1 0.0 collective-permute-done.4.refs_3_
  45.1 0.0 collective-permute-done.3.refs_2_
  45.1 18.3 %shard_map.138 = bf16[8,256,128]{2,1,0:T(8,128)(2,1)} custom-call(bf16[4,272,128]{2,1,0:T(8,128)(2,1)S(1)} %get-tuple-element.16.refs_0_, bf16[4,272,128]{2,1,0:T(8,128)(2,1)S(1)} %get-tuple-element.17.refs_1_, bf16[4,272,128]{2,1,0:T(8,128)(2,1)S(1)} %collective-permute-done.3.refs_2_, bf16[4,272,128]{2,1,0:T(8,128)(2,1)S(1)} %collective-permute-done.4.refs_3_, ...), custom_call_target="tpu_custom_call" | custom-call | tf_op jit(solution)/shard_map/pallas_call | solution.py:410
Async XLA Ops:
  1.4 10.3 %collective-permute-start.2 = (bf16[816,128]{1,0:T(8,128)(2,1)S(1)}, bf16[816,128]{1,0:T(8,128)(2,1)S(1)}, u32[]{:S(2)}, u32[]{:S(2)}) collective-permute-start(bf16[816,128]{1,0:T(8,128)(2,1)S(1)} %get-tuple-element.15.refs_5_), channel_id=1, source_target_pairs={{0,1},{1,0},{2,3},{3,2},{4,5},{5,4},{6,7},{7,6},{8,9},{9,8},{10,11... | collective-permute-start | bytes 626696 | tf_op jit(solution)/shard_map/ppermute | solution.py:443
  2.7 5.9 %collective-permute-start = (bf16[9,8,128]{2,1,0:T(8,128)(2,1)S(1)}, bf16[9,8,128]{2,1,0:T(8,128)(2,1)S(1)}, u32[]{:S(2)}, u32[]{:S(2)}) collective-permute-start(bf16[9,8,128]{2,1,0:T(8,128)(2,1)S(1)} %get-tuple-element.12), channel_id=1, source_target_pairs={{0,2},{2,4},{4,6},{1,3},{3,5},{5,7},{8,10},{10,12},{12,14},{9,11},... | collective-permute-start | bytes 55304 | tf_op jit(solution)/shard_map/ppermute | solution.py:462
  6.7 5.1 %collective-permute-start.1 = (bf16[9,8,128]{2,1,0:T(8,128)(2,1)S(1)}, bf16[9,8,128]{2,1,0:T(8,128)(2,1)S(1)}, u32[]{:S(2)}, u32[]{:S(2)}) collective-permute-start(bf16[9,8,128]{2,1,0:T(8,128)(2,1)S(1)} %get-tuple-element.13), channel_id=1, source_target_pairs={{2,0},{4,2},{6,4},{3,1},{5,3},{7,5},{10,8},{12,10},{14,12},{11,9},... | collective-permute-start | bytes 55304 | tf_op jit(solution)/shard_map/ppermute | solution.py:463
  25.9 19.2 %collective-permute-start.4 = (bf16[4,272,128]{2,1,0:T(8,128)(2,1)S(1)}, bf16[4,272,128]{2,1,0:T(8,128)(2,1)S(1)}, u32[]{:S(2)}, u32[]{:S(2)}) collective-permute-start(bf16[4,272,128]{2,1,0:T(8,128)(2,1)S(1)} %get-tuple-element.16.refs_0_), channel_id=1, source_target_pairs={{1,0},{8,1},{9,8},{16,9},{17,16},{24,17},{25,24},{3,2},{10,3},{11,... | collective-permute-start | bytes 835592 | tf_op jit(solution)/shard_map/ppermute | solution.py:487
  27.9 17.2 %collective-permute-start.3 = (bf16[4,272,128]{2,1,0:T(8,128)(2,1)S(1)}, bf16[4,272,128]{2,1,0:T(8,128)(2,1)S(1)}, u32[]{:S(2)}, u32[]{:S(2)}) collective-permute-start(bf16[4,272,128]{2,1,0:T(8,128)(2,1)S(1)} %get-tuple-element.17.refs_1_), channel_id=1, source_target_pairs={{0,1},{1,8},{8,9},{9,16},{16,17},{17,24},{24,25},{2,3},{3,10},{10,... | collective-permute-start | bytes 835592 | tf_op jit(solution)/shard_map/ppermute | solution.py:486
  31.2 13.9 %collective-permute-start.5 = (bf16[816,128]{1,0:T(8,128)(2,1)S(1)}, bf16[816,128]{1,0:T(8,128)(2,1)S(1)}, u32[]{:S(2)}, u32[]{:S(2)}) collective-permute-start(bf16[816,128]{1,0:T(8,128)(2,1)S(1)} %get-tuple-element.18.refs_5_), channel_id=1, source_target_pairs={{0,1},{1,0},{2,3},{3,2},{4,5},{5,4},{6,7},{7,6},{8,9},{9,8},{10,11... | collective-permute-start | bytes 626696 | tf_op jit(solution)/shard_map/ppermute | solution.py:443

commit v3 on v2

--- a/solution.py
+++ b/solution.py
@@ -158,7 +158,7 @@
 class Weights:
 
     def __init__(self, packs, scratch, c, part, hidden):
-        self.qkv, self.proj, self.fc1, self.fc2 = scratch
+        self.qkv, self.proj, self.fc1, self.fc2, self.rows = scratch
         self.c = c
         self.packs = packs
         self.part, self.hidden = part, hidden
@@ -188,17 +188,21 @@
                 self.fc1[:, lane : lane + 128] = p[at : at + c, :]
                 at += c
             self.fc2[g * hidden : (g + 1) * hidden, :] = p[at : at + hidden, :]
-        self.gain = [self.small(GAIN + k)[0] for k in range(2)]
-        self.shift = [self.small(SHIFTS + k)[0] for k in range(2)]
-        self.proj_bias = self.small(PROJB)[0]
-        self.fc2_bias = self.small(FC2B)[0]
-        self.qkv_bias = jnp.concatenate(
+        vectors = [self.small(GAIN + k)[0] for k in range(2)]
+        vectors += [self.small(SHIFTS + k)[0] for k in range(2)]
+        vectors += [self.small(PROJB)[0], self.small(FC2B)[0]]
+        for k, row in enumerate(vectors):
+            self.rows[k : k + 1, 0:c] = row
+        self.rows[6:7, 0 : 3 * c] = jnp.concatenate(
             [v for m in range(3) for v in self.small(QKVB + m, width=part)], axis=1
         )
         rows = [self.small(FC1B + k) for k in range(hidden // 128)]
-        self.fc1_bias = jnp.concatenate(
+        self.rows[7:8, :] = jnp.concatenate(
             [row[g] for g in range(len(self.packs)) for row in rows], axis=1
         )
+
+    def row(self, k):
+        return self.rows[k : k + 1, 0 : self.c]
 
     def bias(self, own_heads, skip, wide):
         rows = [self.small(TABLE + k) for k in range(2 * own_heads)]
@@ -208,7 +212,7 @@
 
     def queries(self, x, scale):
         c = self.c
-        product = dot_nn(layer_norm(x, self.gain[0], self.shift[0]), self.qkv[...]) + self.qkv_bias
+        product = dot_nn(layer_norm(x, self.row(0), self.row(2)), self.qkv[...]) + self.rows[6:7, 0 : 3 * c]
         return (
             (product[:, :c] * scale).astype(BF),
             product[:, c : 2 * c].astype(BF),
@@ -217,29 +221,41 @@
 
     def keys(self, x):
         c = self.c
-        normed = layer_norm(x, self.gain[0], self.shift[0])
-        product = dot_nn(normed, self.qkv[:, c:]) + self.qkv_bias[:, c:]
+        normed = layer_norm(x, self.row(0), self.row(2))
+        product = dot_nn(normed, self.qkv[:, c:]) + self.rows[6:7, c : 3 * c]
         return product[:, :c].astype(BF), product[:, c:].astype(BF)
 
     def finish(self, x, attended):
-        middle = x + dot_nn(attended, self.proj[...]) + self.proj_bias
+        middle = x + dot_nn(attended, self.proj[...]) + self.row(4)
         middle = middle.astype(BF).astype(F32)
-        normed = layer_norm(middle, self.gain[1], self.shift[1])
-        hidden = gelu(dot_nn(normed, self.fc1[...]) + self.fc1_bias).astype(BF)
-        return middle + dot_nn(hidden, self.fc2[...]) + self.fc2_bias
+        normed = layer_norm(middle, self.row(1), self.row(3))
+        hidden = gelu(dot_nn(normed, self.fc1[...]) + self.rows[7:8, :]).astype(BF)
+        return middle + dot_nn(hidden, self.fc2[...]) + self.row(5)
+
+
+def pipeline(chunks, first, second, third):
+    def trip(i, carry):
+        for u in range(2):
+            t = 2 * i + u
+            third(jnp.clip(t - 2, 0, chunks - 1), u)
+            second(jnp.clip(t - 1, 0, chunks - 1), 1 - u)
+            first(jnp.minimum(t, chunks - 1), u)
+        return carry
+
+    lax.fori_loop(0, (chunks + 3) // 2, trip, 0)
 
 
 def regular_kernel(
     x_hbm, labels_hbm, left_ref, right_ref, rel_ref, *refs, groups, own_heads, entries, part, hidden
 ):
     packs, refs = refs[:groups], refs[groups:]
-    (top_ref, bottom_ref, bias_ref, x_ref, labels_ref, sems), scratch = refs[:6], refs[6:]
-    x_copy = pltpu.make_async_copy(x_hbm, x_ref, sems.at[0])
+    (top_ref, bottom_ref, bias_ref, x_ref, labels_ref, sems, out_ref, qkv_ref, att_ref), scratch = refs[:9], refs[9:]
+    cols = x_hbm.shape[1]
+    x_copy = pltpu.make_async_copy(x_hbm, x_ref.at[:, 0:cols], sems.at[0])
     labels_copy = pltpu.make_async_copy(labels_hbm, labels_ref, sems.at[1])
     x_copy.start()
     labels_copy.start()
     c = x_ref.shape[2]
-    cols = x_ref.shape[1]
     heads = own_heads * groups
     depth = c // heads
     tokens = WIN * WIN
@@ -273,41 +289,44 @@
         target = top_ref if r < SHIFT else bottom_ref
         target[r % SHIFT, cols + WIN :, :] = ids[r * WIN : (r + 1) * WIN].astype(BF)
 
-    def run(x):
-        q, k, v = w.queries(x, scale)
-        outs = []
-        for n in range(x.shape[0] // tokens):
-            at = slice(n * tokens, (n + 1) * tokens)
-            outs.append(attend(q[at], k[at], v[at], bias_ref[...], None, masks, ones))
-        return w.finish(x, jnp.concatenate(outs, axis=0).astype(BF))
-
     group = 4
-
-    def step(i, carry):
-        start = pl.multiple_of(i * group * WIN, group * WIN)
-        block = x_ref[:, pl.ds(start, group * WIN), :].astype(F32)
-        x = jnp.concatenate(
+    span = group * WIN
+
+    def load(i):
+        block = x_ref[:, pl.ds(pl.multiple_of(i * span, span), span), :].astype(F32)
+        return jnp.concatenate(
             [block[r, n * WIN : (n + 1) * WIN] for n in range(group) for r in range(WIN)], axis=0
         )
-        out = run(x)
+
+    def first(i, slot):
+        for m, value in enumerate(w.queries(load(i), scale)):
+            qkv_ref[slot, m] = value
+
+    def second(i, slot):
+        for n in range(group):
+            at = slice(n * tokens, (n + 1) * tokens)
+            q, k, v = (qkv_ref[slot, m, at] for m in range(3))
+            att_ref[slot, at] = attend(q, k, v, bias_ref[...], None, masks, ones).astype(BF)
+
+    def third(i, slot):
+        out = w.finish(load(i), att_ref[slot])
         for r in range(WIN):
-            row = jnp.concatenate(
+            out_ref[r, pl.ds(pl.multiple_of(i * span, span), span), :] = jnp.concatenate(
                 [out[n * tokens + r * WIN : n * tokens + (r + 1) * WIN] for n in range(group)], axis=0
             ).astype(BF)
-            target = top_ref if r < SHIFT else bottom_ref
-            target[r % SHIFT, pl.ds(start, group * WIN), :] = row
-        return carry
-
+
+    for r in range(WIN):
+        x_ref[r, cols : cols + 2 * WIN, :] = jnp.concatenate([left_ref[r], right_ref[r]], axis=0)
+    x_ref[:, cols + 2 * WIN :, :] = jnp.zeros((WIN, x_ref.shape[1] - cols - 2 * WIN, c), BF)
     x_copy.wait()
-    lax.fori_loop(0, cols // (group * WIN), step, 0)
-    left = left_ref[0:WIN].astype(F32).reshape(tokens, c)
-    right = right_ref[0:WIN].astype(F32).reshape(tokens, c)
-    out = run(jnp.concatenate([left, right], axis=0))
-    first = lax.broadcasted_iota(jnp.int32, (tokens, c), 0) % WIN < SHIFT
-    edge = jnp.where(first, out[tokens:], out[:tokens])
+    pipeline(x_ref.shape[1] // span, first, second, third)
+    before = lax.broadcasted_iota(jnp.int32, (WIN, c), 0) < SHIFT
     for r in range(WIN):
         target = top_ref if r < SHIFT else bottom_ref
-        target[r % SHIFT, cols : cols + WIN, :] = edge[r * WIN : (r + 1) * WIN].astype(BF)
+        target[r % SHIFT, 0:cols, :] = out_ref[r, 0:cols, :]
+        edges = out_ref[r, cols : cols + 2 * WIN, :].astype(F32)
+        edge = jnp.where(before, edges[WIN:], edges[:WIN])
+        target[r % SHIFT, cols : cols + WIN, :] = edge.astype(BF)
 
 
 def shifted_kernel(
@@ -315,7 +334,8 @@
     group, groups, own_heads, entries, part, hidden,
 ):
     packs, refs = refs[:groups], refs[groups:]
-    (out_ref, bias_ref, own_ref, halo_ref, res_ref, qid_ref, kid_ref), scratch = refs[:7], refs[7:]
+    (out_ref, bias_ref, own_ref, halo_ref, res_ref, qid_ref, kid_ref), refs = refs[:7], refs[7:]
+    (q_ref, kv_ref, att_ref), scratch = refs[:3], refs[3:]
     c = top_ref.shape[2]
     cols = out_ref.shape[1]
     heads = own_heads * groups
@@ -353,42 +373,50 @@
         qid_ref[s] = parts[0]
         both = jnp.concatenate(parts + parts, axis=0)
         kid_ref[s] = both.T
-    first = lax.broadcasted_iota(jnp.int32, (WIN, group * WIN, c), 1) % WIN < SHIFT
-
-    def step(i, carry):
+    earlier = lax.broadcasted_iota(jnp.int32, (WIN, group * WIN, c), 1) % WIN < SHIFT
+
+    def gather(ref, i):
         start = pl.multiple_of(i * group * WIN, WIN)
-
-        def gather(ref):
-            before = ref[:, pl.ds(start, group * WIN), :]
-            after = ref[:, pl.ds(start + WIN, group * WIN), :]
-            both = jnp.where(first, after, before)
-            return jnp.concatenate(
-                [
-                    both[s * SHIFT + r, n * WIN : (n + 1) * WIN]
-                    for n in range(group) for s in range(2) for r in range(SHIFT)
-                ],
-                axis=0,
-            )
-
-        x = gather(own_ref)
-        q, k_own, v_own = w.queries(x, scale)
-        k_halo, v_halo = w.keys(gather(halo_ref))
-        outs = []
+        before = ref[:, pl.ds(start, group * WIN), :]
+        after = ref[:, pl.ds(start + WIN, group * WIN), :]
+        both = jnp.where(earlier, after, before)
+        return jnp.concatenate(
+            [
+                both[s * SHIFT + r, n * WIN : (n + 1) * WIN]
+                for n in range(group) for s in range(2) for r in range(SHIFT)
+            ],
+            axis=0,
+        )
+
+    def first(i, slot):
+        q, *own = w.queries(gather(own_ref, i), scale)
+        q_ref[slot] = q
+        for m, value in enumerate(own):
+            kv_ref[slot, m, 0] = value
+        for m, value in enumerate(w.keys(gather(halo_ref, i))):
+            kv_ref[slot, m, 1] = value
+
+    def second(i, slot):
         for n in range(group):
             j = i * group + n
             for s in range(2):
                 at = slice((n * 2 + s) * half, (n * 2 + s + 1) * half)
-                k = jnp.concatenate([k_own[at], k_halo[at]], axis=0)
-                v = jnp.concatenate([v_own[at], v_halo[at]], axis=0)
+                k, v = (
+                    jnp.concatenate([kv_ref[slot, m, 0, at], kv_ref[slot, m, 1, at]], axis=0)
+                    for m in range(2)
+                )
                 keys = kid_ref[s, pl.ds(j, 1), :]
                 queries = jnp.take_along_axis(qid_ref[s], jnp.full((half, 128), j, jnp.int32), axis=1)
                 allowed = jnp.concatenate([queries, queries], axis=1) == jnp.concatenate(
                     [keys, keys], axis=1
                 )
-                outs.append(
-                    attend(q[at], k, v, bias_ref[s * half : (s + 1) * half], allowed, masks, ones)
-                )
-        out = w.finish(x, jnp.concatenate(outs, axis=0).astype(BF))
+                att_ref[slot, at] = attend(
+                    q_ref[slot, at], k, v, bias_ref[s * half : (s + 1) * half], allowed, masks, ones
+                ).astype(BF)
+
+    def third(i, slot):
+        out = w.finish(gather(own_ref, i), att_ref[slot])
+        start = pl.multiple_of(i * group * WIN, WIN)
         for r in range(WIN):
             s, a = r // SHIFT, r % SHIFT
             res_ref[r, pl.ds(start, group * WIN), :] = jnp.concatenate(
@@ -398,9 +426,8 @@
                 ],
                 axis=0,
             )
-        return carry
-
-    lax.fori_loop(0, (cols + WIN) // (group * WIN), step, 0)
+
+    pipeline((cols + WIN) // (group * WIN), first, second, third)
     low = lax.broadcasted_iota(jnp.int32, (WIN, cols, c), 1) % WIN < SHIFT
     out_ref[...] = jnp.where(low, res_ref[:, 0:cols, :], res_ref[:, WIN : WIN + cols, :]).astype(BF)
 
@@ -469,15 +496,17 @@
         pltpu.VMEM((c, c), BF),
         pltpu.VMEM((c, groups * hidden), BF),
         pltpu.VMEM((groups * hidden, c), BF),
+        pltpu.VMEM((8, groups * hidden), F32),
     ]
     strip = jax.ShapeDtypeStruct((SHIFT, tile_cols + 2 * WIN, c), BF)
     bias_scratch = pltpu.VMEM((tokens, own_heads * groups * tokens), F32)
+    wide = pltpu.VMEM((WIN, tile_cols + 4 * WIN, c), BF)
     top, bottom = call(
         lambda *refs: regular_kernel(*refs, **sizes),
         (strip, strip),
         [
-            bias_scratch, pltpu.VMEM(image_tokens.shape, BF), pltpu.VMEM(labels.shape, jnp.int32),
-            pltpu.SemaphoreType.DMA((2,)),
+            bias_scratch, wide, pltpu.VMEM(labels.shape, jnp.int32), pltpu.SemaphoreType.DMA((2,)),
+            wide, pltpu.VMEM((2, 3, 4 * tokens, c), BF), pltpu.VMEM((2, 4 * tokens, c), BF),
         ] + weights_scratch,
         in_hbm(image_tokens), in_hbm(labels), left, right, rel2, *packs0,
         in_specs=[pl.BlockSpec(memory_space=pltpu.HBM)] * 2
@@ -494,6 +523,8 @@
         [
             bias_scratch, wide, wide, pltpu.VMEM((WIN, tile_cols + WIN, c), F32),
             pltpu.VMEM((2, SHIFT * WIN, 128), F32), pltpu.VMEM((2, 128, 128), F32),
+            pltpu.VMEM((2, group * tokens, c), BF), pltpu.VMEM((2, 2, 2, group * tokens, c), BF),
+            pltpu.VMEM((2, group * tokens, c), BF),
         ] + weights_scratch,
         top, bottom, above, below, rel2, *packs1,
     )

time: 64.2 us -> 64.1 us (level)
  no operation moved by 1% of the time
where the time goes in v3:
time: 64.1 us; the launch traced here: 63.2 us
  Pallas kernels  33.6 us (52%)
  waiting for transfers between devices  15.9 us (25%)
  starting transfers between devices  13.6 us (21%)
    pallas_call x3, Pallas kernels, call(): pl.pallas_call(kernel, out_shape=out_shapes, scratch_shapes=scratch, comp...  33.6 us
    ppermute x2, waiting for transfers between devices, others(): found.append(lax.ppermute(found[-1], 'ch', swap))  12.7 us
    ppermute x1, starting transfers between devices, both_blocks(): left = lax.ppermute(right_edge, 'col', neighbours('col', 1))  3.95 us
    ppermute x1, starting transfers between devices, both_blocks(): above = lax.ppermute(bottom, ('row', 'ch'), neighbours(('row', 'ch'), 1))  3.26 us
    ppermute x1, waiting for transfers between devices, both_blocks(): right = lax.ppermute(left_edge, 'col', neighbours('col', -1))  3.14 us
    ppermute x2, starting transfers between devices, others(): found.append(lax.ppermute(found[-1], 'ch', swap))  2.5 us
    ppermute x1, starting transfers between devices, both_blocks(): below = lax.ppermute(top, ('row', 'ch'), neighbours(('row', 'ch'), -1))  2.02 us
    ppermute x1, starting transfers between devices, both_blocks(): right = lax.ppermute(left_edge, 'col', neighbours('col', -1))  1.92 us
  transfers between devices with their start and end apart: 6, of which 2 were waited for; matrix products, arithmetic and copies ran while one was open for 0% of the time, Pallas kernels for 0%

profile of v3, /device:TPU:9, one launch (start us, length us, event | category | flops | bytes accessed | tf_op | source)
XLA Modules:
  0.0 63.2 jit_solution(9389038892494279653)
XLA Ops:
  0.0 1.4 %shard_map.136 = (bf16[816,128]{1,0:T(8,128)(2,1)S(1)}, bf16[816,128]{1,0:T(8,128)(2,1)S(1)}, bf16[9,8,128]{2,1,0:T(8,128)(2,1)S(1)}, bf16[9,8,128]{2,1,0:T(8,128)(2,1)S(1)}, s32[64,128]{1,0:T(8,128)S(1)}) custom-call(bf16[8,256,128]{2,1,0:T(8,128)(2,1)} %refs_0_.3, s32[8,256]{1,0:T(8,128)} %refs_1_.3, s32[64,64]{1,0:T(8,128)} %refs_2_.1, ...), custom_call_target="tpu_custom_call" | custom-call | tf_op jit(solution)/shard_map/pallas_call | solution.py:437
  1.4 1.3 %collective-permute-start.2 = (bf16[816,128]{1,0:T(8,128)(2,1)S(1)}, bf16[816,128]{1,0:T(8,128)(2,1)S(1)}, u32[]{:S(2)}, u32[]{:S(2)}) collective-permute-start(bf16[816,128]{1,0:T(8,128)(2,1)S(1)} %get-tuple-element.15.refs_5_), channel_id=1, source_target_pairs={{0,1},{1,0},{2,3},{3,2},{4,5},{5,4},{6,7},{7,6},{8,9},{9,8},{10,11... | collective-permute-start | bytes 626696 | tf_op jit(solution)/shard_map/ppermute | solution.py:470
  2.7 3.9 %collective-permute-start = (bf16[9,8,128]{2,1,0:T(8,128)(2,1)S(1)}, bf16[9,8,128]{2,1,0:T(8,128)(2,1)S(1)}, u32[]{:S(2)}, u32[]{:S(2)}) collective-permute-start(bf16[9,8,128]{2,1,0:T(8,128)(2,1)S(1)} %get-tuple-element.12), channel_id=1, source_target_pairs={{0,2},{2,4},{4,6},{1,3},{3,5},{5,7},{8,10},{10,12},{12,14},{9,11},... | collective-permute-start | bytes 55304 | tf_op jit(solution)/shard_map/ppermute | solution.py:489
  6.7 1.9 %collective-permute-start.1 = (bf16[9,8,128]{2,1,0:T(8,128)(2,1)S(1)}, bf16[9,8,128]{2,1,0:T(8,128)(2,1)S(1)}, u32[]{:S(2)}, u32[]{:S(2)}) collective-permute-start(bf16[9,8,128]{2,1,0:T(8,128)(2,1)S(1)} %get-tuple-element.13), channel_id=1, source_target_pairs={{2,0},{4,2},{6,4},{3,1},{5,3},{7,5},{10,8},{12,10},{14,12},{11,9},... | collective-permute-start | bytes 55304 | tf_op jit(solution)/shard_map/ppermute | solution.py:490
  8.6 0.0 collective-permute-done.refs_2_
  8.6 3.1 %collective-permute-done.1.refs_3_ = bf16[9,8,128]{2,1,0:T(8,128)(2,1)S(1)} collective-permute-done((bf16[9,8,128]{2,1,0:T(8,128)(2,1)S(1)}, bf16[9,8,128]{2,1,0:T(8,128)(2,1)S(1)}, u32[]{:S(2)}, u32[]{:S(2)}) %collective-permute-start.1) | collective-permute-done | bytes 18464 | tf_op jit(solution)/shard_map/ppermute | solution.py:490
  11.8 0.0 collective-permute-done.2.refs_6_
  11.8 14.4 %shard_map.137 = (bf16[4,272,128]{2,1,0:T(8,128)(2,1)S(1)}, bf16[4,272,128]{2,1,0:T(8,128)(2,1)S(1)}) custom-call(bf16[8,256,128]{2,1,0:T(8,128)(2,1)} %refs_0_.3, s32[8,256]{1,0:T(8,128)} %refs_1_.3, bf16[9,8,128]{2,1,0:T(8,128)(2,1)S(1)} %collective-permute-done.refs_2_, bf16[9,8,128]{2,1,0:T(8,128)(2,1)S(1)} %collective-permute-done.1.refs_3_, ...), custom_call_target="tpu_custom_call" | custom-call | tf_op jit(solution)/shard_map/pallas_call | solution.py:437
  26.2 2.0 %collective-permute-start.4 = (bf16[4,272,128]{2,1,0:T(8,128)(2,1)S(1)}, bf16[4,272,128]{2,1,0:T(8,128)(2,1)S(1)}, u32[]{:S(2)}, u32[]{:S(2)}) collective-permute-start(bf16[4,272,128]{2,1,0:T(8,128)(2,1)S(1)} %get-tuple-element.16.refs_0_), channel_id=1, source_target_pairs={{1,0},{8,1},{9,8},{16,9},{17,16},{24,17},{25,24},{3,2},{10,3},{11,... | collective-permute-start | bytes 835592 | tf_op jit(solution)/shard_map/ppermute | solution.py:516
  28.2 3.3 %collective-permute-start.3 = (bf16[4,272,128]{2,1,0:T(8,128)(2,1)S(1)}, bf16[4,272,128]{2,1,0:T(8,128)(2,1)S(1)}, u32[]{:S(2)}, u32[]{:S(2)}) collective-permute-start(bf16[4,272,128]{2,1,0:T(8,128)(2,1)S(1)} %get-tuple-element.17.refs_1_), channel_id=1, source_target_pairs={{0,1},{1,8},{8,9},{9,16},{16,17},{17,24},{24,25},{2,3},{3,10},{10,... | collective-permute-start | bytes 835592 | tf_op jit(solution)/shard_map/ppermute | solution.py:515
  31.5 1.2 %collective-permute-start.5 = (bf16[816,128]{1,0:T(8,128)(2,1)S(1)}, bf16[816,128]{1,0:T(8,128)(2,1)S(1)}, u32[]{:S(2)}, u32[]{:S(2)}) collective-permute-start(bf16[816,128]{1,0:T(8,128)(2,1)S(1)} %get-tuple-element.18.refs_5_), channel_id=1, source_target_pairs={{0,1},{1,0},{2,3},{3,2},{4,5},{5,4},{6,7},{7,6},{8,9},{9,8},{10,11... | collective-permute-start | bytes 626696 | tf_op jit(solution)/shard_map/ppermute | solution.py:470
  32.6 12.7 %collective-permute-done.5.refs_6_ = bf16[816,128]{1,0:T(8,128)(2,1)S(1)} collective-permute-done((bf16[816,128]{1,0:T(8,128)(2,1)S(1)}, bf16[816,128]{1,0:T(8,128)(2,1)S(1)}, u32[]{:S(2)}, u32[]{:S(2)}) %collective-permute-start.5) | collective-permute-done | bytes 208928 | tf_op jit(solution)/shard_map/ppermute | solution.py:470
  45.3 0.0 collective-permute-done.4.refs_3_
  45.4 0.0 collective-permute-done.3.refs_2_
  45.4 17.9 %shard_map.138 = bf16[8,256,128]{2,1,0:T(8,128)(2,1)} custom-call(bf16[4,272,128]{2,1,0:T(8,128)(2,1)S(1)} %get-tuple-element.16.refs_0_, bf16[4,272,128]{2,1,0:T(8,128)(2,1)S(1)} %get-tuple-element.17.refs_1_, bf16[4,272,128]{2,1,0:T(8,128)(2,1)S(1)} %collective-permute-done.3.refs_2_, bf16[4,272,128]{2,1,0:T(8,128)(2,1)S(1)} %collective-permute-done.4.refs_3_, ...), custom_call_target="tpu_custom_call" | custom-call | tf_op jit(solution)/shard_map/pallas_call | solution.py:437
Async XLA Ops:
  1.4 10.3 %collective-permute-start.2 = (bf16[816,128]{1,0:T(8,128)(2,1)S(1)}, bf16[816,128]{1,0:T(8,128)(2,1)S(1)}, u32[]{:S(2)}, u32[]{:S(2)}) collective-permute-start(bf16[816,128]{1,0:T(8,128)(2,1)S(1)} %get-tuple-element.15.refs_5_), channel_id=1, source_target_pairs={{0,1},{1,0},{2,3},{3,2},{4,5},{5,4},{6,7},{7,6},{8,9},{9,8},{10,11... | collective-permute-start | bytes 626696 | tf_op jit(solution)/shard_map/ppermute | solution.py:470
  2.7 5.9 %collective-permute-start = (bf16[9,8,128]{2,1,0:T(8,128)(2,1)S(1)}, bf16[9,8,128]{2,1,0:T(8,128)(2,1)S(1)}, u32[]{:S(2)}, u32[]{:S(2)}) collective-permute-start(bf16[9,8,128]{2,1,0:T(8,128)(2,1)S(1)} %get-tuple-element.12), channel_id=1, source_target_pairs={{0,2},{2,4},{4,6},{1,3},{3,5},{5,7},{8,10},{10,12},{12,14},{9,11},... | collective-permute-start | bytes 55304 | tf_op jit(solution)/shard_map/ppermute | solution.py:489
  6.7 5.1 %collective-permute-start.1 = (bf16[9,8,128]{2,1,0:T(8,128)(2,1)S(1)}, bf16[9,8,128]{2,1,0:T(8,128)(2,1)S(1)}, u32[]{:S(2)}, u32[]{:S(2)}) collective-permute-start(bf16[9,8,128]{2,1,0:T(8,128)(2,1)S(1)} %get-tuple-element.13), channel_id=1, source_target_pairs={{2,0},{4,2},{6,4},{3,1},{5,3},{7,5},{10,8},{12,10},{14,12},{11,9},... | collective-permute-start | bytes 55304 | tf_op jit(solution)/shard_map/ppermute | solution.py:490
  26.2 19.2 %collective-permute-start.4 = (bf16[4,272,128]{2,1,0:T(8,128)(2,1)S(1)}, bf16[4,272,128]{2,1,0:T(8,128)(2,1)S(1)}, u32[]{:S(2)}, u32[]{:S(2)}) collective-permute-start(bf16[4,272,128]{2,1,0:T(8,128)(2,1)S(1)} %get-tuple-element.16.refs_0_), channel_id=1, source_target_pairs={{1,0},{8,1},{9,8},{16,9},{17,16},{24,17},{25,24},{3,2},{10,3},{11,... | collective-permute-start | bytes 835592 | tf_op jit(solution)/shard_map/ppermute | solution.py:516
  28.2 17.2 %collective-permute-start.3 = (bf16[4,272,128]{2,1,0:T(8,128)(2,1)S(1)}, bf16[4,272,128]{2,1,0:T(8,128)(2,1)S(1)}, u32[]{:S(2)}, u32[]{:S(2)}) collective-permute-start(bf16[4,272,128]{2,1,0:T(8,128)(2,1)S(1)} %get-tuple-element.17.refs_1_), channel_id=1, source_target_pairs={{0,1},{1,8},{8,9},{9,16},{16,17},{17,24},{24,25},{2,3},{3,10},{10,... | collective-permute-start | bytes 835592 | tf_op jit(solution)/shard_map/ppermute | solution.py:515
  31.5 13.9 %collective-permute-start.5 = (bf16[816,128]{1,0:T(8,128)(2,1)S(1)}, bf16[816,128]{1,0:T(8,128)(2,1)S(1)}, u32[]{:S(2)}, u32[]{:S(2)}) collective-permute-start(bf16[816,128]{1,0:T(8,128)(2,1)S(1)} %get-tuple-element.18.refs_5_), channel_id=1, source_target_pairs={{0,1},{1,0},{2,3},{3,2},{4,5},{5,4},{6,7},{7,6},{8,9},{9,8},{10,11... | collective-permute-start | bytes 626696 | tf_op jit(solution)/shard_map/ppermute | solution.py:470

commit v4 on v3

--- a/solution.py
+++ b/solution.py
@@ -25,12 +25,6 @@
     return lax.dot_general(a, b, (((1,), (0,)), ((), ())), preferred_element_type=F32)
 
 
-def layer_norm(x, gain, shift):
-    center = x - jnp.mean(x, axis=-1, keepdims=True)
-    spread = jnp.mean(center * center, axis=-1, keepdims=True)
-    return (center * lax.rsqrt(spread + EPS) * gain + shift).astype(BF)
-
-
 def gelu(v):
     half = 0.5 * v
     return half + half * lax.erf(v * math.sqrt(0.5))
@@ -45,23 +39,54 @@
     return jnp.concatenate([rows * mask for mask in masks], axis=0)
 
 
-def attend(q, k, v, bias, allowed, masks, ones):
-    scores = dot_nt(q, stack_heads(k, masks)) + bias
-    if allowed is not None:
-        scores = jnp.where(allowed, scores, NEG)
-    lanes = 128
-    first = lax.broadcasted_iota(jnp.int32, (q.shape[0], lanes), 1) < WIN * WIN
-    parts = []
-    for start in range(0, scores.shape[1], lanes):
-        s = scores[:, start : start + lanes]
-        low = jnp.max(jnp.where(first, s, NEG), axis=-1, keepdims=True)
-        high = jnp.max(jnp.where(first, NEG, s), axis=-1, keepdims=True)
-        parts.append(jnp.exp2(s - jnp.where(first, low, high)).astype(BF))
-    weights = jnp.concatenate(parts, axis=1)
-    rhs = jnp.concatenate([stack_heads(v, masks), ones], axis=1)
-    summed = dot_nn(weights, rhs)
-    width = v.shape[1]
-    return summed[:, :width] / summed[:, width:]
+def window_pieces(read, bias, allowed, write, masks, ones):
+    at = {}
+
+    def score():
+        q, k, at["v"] = read()
+        at["s"] = dot_nt(q, stack_heads(k, masks))
+
+    def reduce():
+        scores = at["s"] + bias()
+        if allowed is not None:
+            scores = jnp.where(allowed(), scores, NEG)
+        first = lax.broadcasted_iota(jnp.int32, (scores.shape[0], 128), 1) < WIN * WIN
+        parts = []
+        for start in range(0, scores.shape[1], 128):
+            s = scores[:, start : start + 128]
+            low = jnp.max(jnp.where(first, s, NEG), axis=-1, keepdims=True)
+            high = jnp.max(jnp.where(first, NEG, s), axis=-1, keepdims=True)
+            parts.append((s, jnp.where(first, low, high)))
+        at["s"] = parts
+
+    def mix():
+        weights = jnp.concatenate([jnp.exp2(s - m).astype(BF) for s, m in at["s"]], axis=1)
+        rhs = jnp.concatenate([stack_heads(at["v"], masks), ones], axis=1)
+        at["o"] = dot_nn(weights, rhs)
+
+    def store():
+        width = at["o"].shape[1] // 2
+        write((at["o"][:, :width] / at["o"][:, width:]).astype(BF))
+
+    return [score, reduce, mix, store]
+
+
+def skewed(pipelines):
+    depth = max(len(p) for p in pipelines)
+    return [
+        pipelines[n][t - n]
+        for t in range(len(pipelines) + depth - 1)
+        for n in range(len(pipelines))
+        if 0 <= t - n < len(pipelines[n])
+    ]
+
+
+def weave(*threads):
+    order = sorted(
+        ((k + 0.5) / len(thread), n, k) for n, thread in enumerate(threads) for k in range(len(thread))
+    )
+    for _, n, k in order:
+        threads[n][k]()
 
 
 def pick(low_rows, high_rows, skip, wide):
@@ -210,39 +235,105 @@
         high = [rows[2 * h + 1][g] for g in range(len(self.packs)) for h in range(own_heads)]
         return pick(low, high, skip, wide)
 
-    def queries(self, x, scale):
+    def norm_pieces(self, at, k):
+        def mean():
+            x = at["x"]
+            at["center"] = x - jnp.mean(x, axis=-1, keepdims=True)
+
+        def spread():
+            center = at["center"]
+            at["spread"] = jnp.mean(center * center, axis=-1, keepdims=True)
+
+        def normed():
+            scaled = at["center"] * lax.rsqrt(at["spread"] + EPS)
+            at["normed"] = (scaled * self.row(k) + self.row(2 + k)).astype(BF)
+
+        return [mean, spread, normed]
+
+    def project_pieces(self, load, stores):
+        at = {}
         c = self.c
-        product = dot_nn(layer_norm(x, self.row(0), self.row(2)), self.qkv[...]) + self.rows[6:7, 0 : 3 * c]
-        return (
-            (product[:, :c] * scale).astype(BF),
-            product[:, c : 2 * c].astype(BF),
-            product[:, 2 * c :].astype(BF),
-        )
-
-    def keys(self, x):
-        c = self.c
-        normed = layer_norm(x, self.row(0), self.row(2))
-        product = dot_nn(normed, self.qkv[:, c:]) + self.rows[6:7, c : 3 * c]
-        return product[:, :c].astype(BF), product[:, c:].astype(BF)
-
-    def finish(self, x, attended):
-        middle = x + dot_nn(attended, self.proj[...]) + self.row(4)
-        middle = middle.astype(BF).astype(F32)
-        normed = layer_norm(middle, self.row(1), self.row(3))
-        hidden = gelu(dot_nn(normed, self.fc1[...]) + self.rows[7:8, :]).astype(BF)
-        return middle + dot_nn(hidden, self.fc2[...]) + self.row(5)
+
+        def begin():
+            at["x"] = load()
+
+        def product(m, scale, store):
+            def dot():
+                at[m] = dot_nn(at["normed"], self.qkv[:, m * c : (m + 1) * c])
+
+            def keep():
+                value = at.pop(m) + self.rows[6:7, m * c : (m + 1) * c]
+                store((value if scale is None else value * scale).astype(BF))
+
+            return dot, keep
+
+        mean, spread, normed = self.norm_pieces(at, 0)
+        made = [product(*entry) for entry in stores]
+
+        def start():
+            begin()
+            mean()
+
+        return [start, spread, normed] + [dot for dot, _ in made] + [keep for _, keep in made]
+
+    def finish_pieces(self, load, attended, store):
+        at = {}
+        width = 256
+
+        def project():
+            at["p"] = dot_nn(attended(), self.proj[...])
+
+        def begin():
+            middle = (load() + at.pop("p") + self.row(4)).astype(BF).astype(F32)
+            at["x"] = middle
+            at["middle"] = middle
+
+        mean, spread, normed = self.norm_pieces(at, 1)
+
+        def start():
+            begin()
+            mean()
+
+        def up(k):
+            def dot():
+                at["up", k] = dot_nn(at["normed"], self.fc1[:, k : k + width])
+
+            return dot
+
+        def act(k):
+            def gate():
+                at["act", k] = gelu(at.pop(("up", k)) + self.rows[7:8, k : k + width]).astype(BF)
+
+            return gate
+
+        def down(k):
+            def dot():
+                at["down", k] = dot_nn(at.pop(("act", k)), self.fc2[k : k + width, :])
+
+            return dot
+
+        def end():
+            total = at["middle"] + self.row(5)
+            for k in starts:
+                total = total + at["down", k]
+            store(total)
+
+        starts = range(0, self.fc2.shape[0], width)
+        pieces = [project, start, spread, normed]
+        chains = [[up(k), act(k), down(k)] for k in starts]
+        return pieces + skewed(chains) + [end]
 
 
 def pipeline(chunks, first, second, third):
-    def trip(i, carry):
-        for u in range(2):
-            t = 2 * i + u
-            third(jnp.clip(t - 2, 0, chunks - 1), u)
-            second(jnp.clip(t - 1, 0, chunks - 1), 1 - u)
-            first(jnp.minimum(t, chunks - 1), u)
-        return carry
-
-    lax.fori_loop(0, (chunks + 3) // 2, trip, 0)
+    for t in range(chunks + 2):
+        threads = []
+        if t >= 2:
+            threads.append(third(t - 2))
+        if 1 <= t <= chunks:
+            threads.append(second(t - 1))
+        if t < chunks:
+            threads.append(first(t))
+        weave(*threads)
 
 
 def regular_kernel(
@@ -293,27 +384,45 @@
     span = group * WIN
 
     def load(i):
-        block = x_ref[:, pl.ds(pl.multiple_of(i * span, span), span), :].astype(F32)
+        block = x_ref[:, i * span : (i + 1) * span, :].astype(F32)
         return jnp.concatenate(
             [block[r, n * WIN : (n + 1) * WIN] for n in range(group) for r in range(WIN)], axis=0
         )
 
-    def first(i, slot):
-        for m, value in enumerate(w.queries(load(i), scale)):
-            qkv_ref[slot, m] = value
-
-    def second(i, slot):
-        for n in range(group):
-            at = slice(n * tokens, (n + 1) * tokens)
-            q, k, v = (qkv_ref[slot, m, at] for m in range(3))
-            att_ref[slot, at] = attend(q, k, v, bias_ref[...], None, masks, ones).astype(BF)
-
-    def third(i, slot):
-        out = w.finish(load(i), att_ref[slot])
-        for r in range(WIN):
-            out_ref[r, pl.ds(pl.multiple_of(i * span, span), span), :] = jnp.concatenate(
-                [out[n * tokens + r * WIN : n * tokens + (r + 1) * WIN] for n in range(group)], axis=0
-            ).astype(BF)
+    def first(i):
+        def keep(m):
+            def store(value):
+                qkv_ref[i % 2, m] = value
+
+            return store
+
+        return w.project_pieces(
+            lambda: load(i), [(0, scale, keep(0)), (1, None, keep(1)), (2, None, keep(2))]
+        )
+
+    def second(i):
+        def window(n):
+            rows = slice(n * tokens, (n + 1) * tokens)
+
+            def write(value):
+                att_ref[i % 2, rows] = value
+
+            return window_pieces(
+                lambda: [qkv_ref[i % 2, m, rows] for m in range(3)],
+                lambda: bias_ref[...], None, write, masks, ones,
+            )
+
+        return skewed([window(n) for n in range(group)])
+
+    def third(i):
+        def store(out):
+            for r in range(WIN):
+                out_ref[r, i * span : (i + 1) * span, :] = jnp.concatenate(
+                    [out[n * tokens + r * WIN : n * tokens + (r + 1) * WIN] for n in range(group)],
+                    axis=0,
+                ).astype(BF)
+
+        return w.finish_pieces(lambda: load(i), lambda: att_ref[i % 2], store)
 
     for r in range(WIN):
         x_ref[r, cols : cols + 2 * WIN, :] = jnp.concatenate([left_ref[r], right_ref[r]], axis=0)
@@ -373,59 +482,80 @@
         qid_ref[s] = parts[0]
         both = jnp.concatenate(parts + parts, axis=0)
         kid_ref[s] = both.T
-    earlier = lax.broadcasted_iota(jnp.int32, (WIN, group * WIN, c), 1) % WIN < SHIFT
+    earlier = lax.broadcasted_iota(jnp.int32, (WIN, c), 0) < SHIFT
 
     def gather(ref, i):
-        start = pl.multiple_of(i * group * WIN, WIN)
-        before = ref[:, pl.ds(start, group * WIN), :]
-        after = ref[:, pl.ds(start + WIN, group * WIN), :]
-        both = jnp.where(earlier, after, before)
-        return jnp.concatenate(
-            [
-                both[s * SHIFT + r, n * WIN : (n + 1) * WIN]
-                for n in range(group) for s in range(2) for r in range(SHIFT)
-            ],
-            axis=0,
+        pieces = []
+        for n in range(group):
+            start = (i * group + n) * WIN
+            for r in range(WIN):
+                before = ref[r, start : start + WIN, :]
+                after = ref[r, start + WIN : start + 2 * WIN, :]
+                pieces.append(jnp.where(earlier, after, before))
+        return jnp.concatenate(pieces, axis=0)
+
+    def first(i):
+        def keep(target):
+            def store(value):
+                target[...] = value
+
+            return store
+
+        slot = i % 2
+        own = w.project_pieces(
+            lambda: gather(own_ref, i),
+            [(0, scale, keep(q_ref.at[slot]))]
+            + [(1 + m, None, keep(kv_ref.at[slot, m, 0])) for m in range(2)],
         )
-
-    def first(i, slot):
-        q, *own = w.queries(gather(own_ref, i), scale)
-        q_ref[slot] = q
-        for m, value in enumerate(own):
-            kv_ref[slot, m, 0] = value
-        for m, value in enumerate(w.keys(gather(halo_ref, i))):
-            kv_ref[slot, m, 1] = value
-
-    def second(i, slot):
-        for n in range(group):
+        halo = w.project_pieces(
+            lambda: gather(halo_ref, i), [(1 + m, None, keep(kv_ref.at[slot, m, 1])) for m in range(2)]
+        )
+        return skewed([own, halo])
+
+    def second(i):
+        slot = i % 2
+
+        def window(n, s):
             j = i * group + n
-            for s in range(2):
-                at = slice((n * 2 + s) * half, (n * 2 + s + 1) * half)
+            rows = slice((n * 2 + s) * half, (n * 2 + s + 1) * half)
+
+            def read():
                 k, v = (
-                    jnp.concatenate([kv_ref[slot, m, 0, at], kv_ref[slot, m, 1, at]], axis=0)
+                    jnp.concatenate([kv_ref[slot, m, 0, rows], kv_ref[slot, m, 1, rows]], axis=0)
                     for m in range(2)
                 )
-                keys = kid_ref[s, pl.ds(j, 1), :]
-                queries = jnp.take_along_axis(qid_ref[s], jnp.full((half, 128), j, jnp.int32), axis=1)
-                allowed = jnp.concatenate([queries, queries], axis=1) == jnp.concatenate(
-                    [keys, keys], axis=1
+                return q_ref[slot, rows], k, v
+
+            def allowed():
+                keys = kid_ref[s, j : j + 1, :]
+                queries = jnp.broadcast_to(qid_ref[s, :, j : j + 1], (half, 128))
+                same = queries == keys
+                return jnp.concatenate([same, same], axis=1)
+
+            def write(value):
+                att_ref[slot, rows] = value
+
+            return window_pieces(
+                read, lambda: bias_ref[s * half : (s + 1) * half], allowed, write, masks, ones
+            )
+
+        return skewed([window(n, s) for n in range(group) for s in range(2)])
+
+    def third(i):
+        start = i * group * WIN
+
+        def store(out):
+            for r in range(WIN):
+                s, a = r // SHIFT, r % SHIFT
+                res_ref[r, start : start + group * WIN, :] = jnp.concatenate(
+                    [
+                        out[(n * 2 + s) * half + a * WIN : (n * 2 + s) * half + (a + 1) * WIN]
+                        for n in range(group)
+                    ],
+                    axis=0,
                 )
-                att_ref[slot, at] = attend(
-                    q_ref[slot, at], k, v, bias_ref[s * half : (s + 1) * half], allowed, masks, ones
-                ).astype(BF)
-
-    def third(i, slot):
-        out = w.finish(gather(own_ref, i), att_ref[slot])
-        start = pl.multiple_of(i * group * WIN, WIN)
-        for r in range(WIN):
-            s, a = r // SHIFT, r % SHIFT
-            res_ref[r, pl.ds(start, group * WIN), :] = jnp.concatenate(
-                [
-                    out[(n * 2 + s) * half + a * WIN : (n * 2 + s) * half + (a + 1) * WIN]
-                    for n in range(group)
-                ],
-                axis=0,
-            )
+
+        return w.finish_pieces(lambda: gather(own_ref, i), lambda: att_ref[i % 2], store)
 
     pipeline((cols + WIN) // (group * WIN), first, second, third)
     low = lax.broadcasted_iota(jnp.int32, (WIN, cols, c), 1) % WIN < SHIFT

time: 64.1 us -> 54 us (0.84)
  Pallas kernels: 33.6 us -> 23.6 us
    pallas_call x3, Pallas kernels: 33.6 us -> 23.6 us  [call(): pl.pallas_call(kernel, out_shape=out_shapes, scratch_shapes=scratch, comp...]
where the time goes in v4:
time: 54 us; the launch traced here: 53.1 us
  Pallas kernels  23.6 us (44%)
  waiting for transfers between devices  15.7 us (29%)
  starting transfers between devices  13.8 us (26%)
    pallas_call x3, Pallas kernels, call(): pl.pallas_call(kernel, out_shape=out_shapes, scratch_shapes=scratch, comp...  23.6 us
    ppermute x2, waiting for transfers between devices, others(): found.append(lax.ppermute(found[-1], 'ch', swap))  12.5 us
    ppermute x1, starting transfers between devices, both_blocks(): left = lax.ppermute(right_edge, 'col', neighbours('col', 1))  3.95 us
    ppermute x1, starting transfers between devices, both_blocks(): above = lax.ppermute(bottom, ('row', 'ch'), neighbours(('row', 'ch'), 1))  3.44 us
    ppermute x1, waiting for transfers between devices, both_blocks(): right = lax.ppermute(left_edge, 'col', neighbours('col', -1))  3.14 us
    ppermute x2, starting transfers between devices, others(): found.append(lax.ppermute(found[-1], 'ch', swap))  2.49 us
    ppermute x1, starting transfers between devices, both_blocks(): below = lax.ppermute(top, ('row', 'ch'), neighbours(('row', 'ch'), -1))  2.02 us
    ppermute x1, starting transfers between devices, both_blocks(): right = lax.ppermute(left_edge, 'col', neighbours('col', -1))  1.92 us
  transfers between devices with their start and end apart: 6, of which 2 were waited for; matrix products, arithmetic and copies ran while one was open for 0% of the time, Pallas kernels for 0%

profile of v4, /device:TPU:9, one launch (start us, length us, event | category | flops | bytes accessed | tf_op | source)
XLA Modules:
  0.0 53.1 jit_solution(1555088232310304331)
XLA Ops:
  0.0 1.4 %shard_map.136 = (bf16[816,128]{1,0:T(8,128)(2,1)S(1)}, bf16[816,128]{1,0:T(8,128)(2,1)S(1)}, bf16[9,8,128]{2,1,0:T(8,128)(2,1)S(1)}, bf16[9,8,128]{2,1,0:T(8,128)(2,1)S(1)}, s32[64,128]{1,0:T(8,128)S(1)}) custom-call(bf16[8,256,128]{2,1,0:T(8,128)(2,1)} %refs_0_.3, s32[8,256]{1,0:T(8,128)} %refs_1_.3, s32[64,64]{1,0:T(8,128)} %refs_2_.1, ...), custom_call_target="tpu_custom_call" | custom-call | tf_op jit(solution)/shard_map/pallas_call | solution.py:567
  1.4 1.3 %collective-permute-start.2 = (bf16[816,128]{1,0:T(8,128)(2,1)S(1)}, bf16[816,128]{1,0:T(8,128)(2,1)S(1)}, u32[]{:S(2)}, u32[]{:S(2)}) collective-permute-start(bf16[816,128]{1,0:T(8,128)(2,1)S(1)} %get-tuple-element.15.refs_5_), channel_id=1, source_target_pairs={{0,1},{1,0},{2,3},{3,2},{4,5},{5,4},{6,7},{7,6},{8,9},{9,8},{10,11... | collective-permute-start | bytes 626696 | tf_op jit(solution)/shard_map/ppermute | solution.py:600
  2.7 3.9 %collective-permute-start = (bf16[9,8,128]{2,1,0:T(8,128)(2,1)S(1)}, bf16[9,8,128]{2,1,0:T(8,128)(2,1)S(1)}, u32[]{:S(2)}, u32[]{:S(2)}) collective-permute-start(bf16[9,8,128]{2,1,0:T(8,128)(2,1)S(1)} %get-tuple-element.12), channel_id=1, source_target_pairs={{0,2},{2,4},{4,6},{1,3},{3,5},{5,7},{8,10},{10,12},{12,14},{9,11},... | collective-permute-start | bytes 55304 | tf_op jit(solution)/shard_map/ppermute | solution.py:619
  6.7 1.9 %collective-permute-start.1 = (bf16[9,8,128]{2,1,0:T(8,128)(2,1)S(1)}, bf16[9,8,128]{2,1,0:T(8,128)(2,1)S(1)}, u32[]{:S(2)}, u32[]{:S(2)}) collective-permute-start(bf16[9,8,128]{2,1,0:T(8,128)(2,1)S(1)} %get-tuple-element.13), channel_id=1, source_target_pairs={{2,0},{4,2},{6,4},{3,1},{5,3},{7,5},{10,8},{12,10},{14,12},{11,9},... | collective-permute-start | bytes 55304 | tf_op jit(solution)/shard_map/ppermute | solution.py:620
  8.6 0.0 collective-permute-done.refs_2_
  8.6 3.1 %collective-permute-done.1.refs_3_ = bf16[9,8,128]{2,1,0:T(8,128)(2,1)S(1)} collective-permute-done((bf16[9,8,128]{2,1,0:T(8,128)(2,1)S(1)}, bf16[9,8,128]{2,1,0:T(8,128)(2,1)S(1)}, u32[]{:S(2)}, u32[]{:S(2)}) %collective-permute-start.1) | collective-permute-done | bytes 18464 | tf_op jit(solution)/shard_map/ppermute | solution.py:620
  11.8 0.0 collective-permute-done.2.refs_6_
  11.8 10.0 %shard_map.137 = (bf16[4,272,128]{2,1,0:T(8,128)(2,1)S(1)}, bf16[4,272,128]{2,1,0:T(8,128)(2,1)S(1)}) custom-call(bf16[8,256,128]{2,1,0:T(8,128)(2,1)} %refs_0_.3, s32[8,256]{1,0:T(8,128)} %refs_1_.3, bf16[9,8,128]{2,1,0:T(8,128)(2,1)S(1)} %collective-permute-done.refs_2_, bf16[9,8,128]{2,1,0:T(8,128)(2,1)S(1)} %collective-permute-done.1.refs_3_, ...), custom_call_target="tpu_custom_call" | custom-call | tf_op jit(solution)/shard_map/pallas_call | solution.py:567
  21.8 2.0 %collective-permute-start.4 = (bf16[4,272,128]{2,1,0:T(8,128)(2,1)S(1)}, bf16[4,272,128]{2,1,0:T(8,128)(2,1)S(1)}, u32[]{:S(2)}, u32[]{:S(2)}) collective-permute-start(bf16[4,272,128]{2,1,0:T(8,128)(2,1)S(1)} %get-tuple-element.16.refs_0_), channel_id=1, source_target_pairs={{1,0},{8,1},{9,8},{16,9},{17,16},{24,17},{25,24},{3,2},{10,3},{11,... | collective-permute-start | bytes 835592 | tf_op jit(solution)/shard_map/ppermute | solution.py:646
  23.8 3.4 %collective-permute-start.3 = (bf16[4,272,128]{2,1,0:T(8,128)(2,1)S(1)}, bf16[4,272,128]{2,1,0:T(8,128)(2,1)S(1)}, u32[]{:S(2)}, u32[]{:S(2)}) collective-permute-start(bf16[4,272,128]{2,1,0:T(8,128)(2,1)S(1)} %get-tuple-element.17.refs_1_), channel_id=1, source_target_pairs={{0,1},{1,8},{8,9},{9,16},{16,17},{17,24},{24,25},{2,3},{3,10},{10,... | collective-permute-start | bytes 835592 | tf_op jit(solution)/shard_map/ppermute | solution.py:645
  27.3 1.2 %collective-permute-start.5 = (bf16[816,128]{1,0:T(8,128)(2,1)S(1)}, bf16[816,128]{1,0:T(8,128)(2,1)S(1)}, u32[]{:S(2)}, u32[]{:S(2)}) collective-permute-start(bf16[816,128]{1,0:T(8,128)(2,1)S(1)} %get-tuple-element.18.refs_5_), channel_id=1, source_target_pairs={{0,1},{1,0},{2,3},{3,2},{4,5},{5,4},{6,7},{7,6},{8,9},{9,8},{10,11... | collective-permute-start | bytes 626696 | tf_op jit(solution)/shard_map/ppermute | solution.py:600
  28.5 12.5 %collective-permute-done.5.refs_6_ = bf16[816,128]{1,0:T(8,128)(2,1)S(1)} collective-permute-done((bf16[816,128]{1,0:T(8,128)(2,1)S(1)}, bf16[816,128]{1,0:T(8,128)(2,1)S(1)}, u32[]{:S(2)}, u32[]{:S(2)}) %collective-permute-start.5) | collective-permute-done | bytes 208928 | tf_op jit(solution)/shard_map/ppermute | solution.py:600
  41.0 0.0 collective-permute-done.4.refs_3_
  41.0 0.0 collective-permute-done.3.refs_2_
  41.0 12.1 %shard_map.138 = bf16[8,256,128]{2,1,0:T(8,128)(2,1)} custom-call(bf16[4,272,128]{2,1,0:T(8,128)(2,1)S(1)} %get-tuple-element.16.refs_0_, bf16[4,272,128]{2,1,0:T(8,128)(2,1)S(1)} %get-tuple-element.17.refs_1_, bf16[4,272,128]{2,1,0:T(8,128)(2,1)S(1)} %collective-permute-done.3.refs_2_, bf16[4,272,128]{2,1,0:T(8,128)(2,1)S(1)} %collective-permute-done.4.refs_3_, ...), custom_call_target="tpu_custom_call" | custom-call | tf_op jit(solution)/shard_map/pallas_call | solution.py:567
Async XLA Ops:
  1.4 10.3 %collective-permute-start.2 = (bf16[816,128]{1,0:T(8,128)(2,1)S(1)}, bf16[816,128]{1,0:T(8,128)(2,1)S(1)}, u32[]{:S(2)}, u32[]{:S(2)}) collective-permute-start(bf16[816,128]{1,0:T(8,128)(2,1)S(1)} %get-tuple-element.15.refs_5_), channel_id=1, source_target_pairs={{0,1},{1,0},{2,3},{3,2},{4,5},{5,4},{6,7},{7,6},{8,9},{9,8},{10,11... | collective-permute-start | bytes 626696 | tf_op jit(solution)/shard_map/ppermute | solution.py:600
  2.7 5.9 %collective-permute-start = (bf16[9,8,128]{2,1,0:T(8,128)(2,1)S(1)}, bf16[9,8,128]{2,1,0:T(8,128)(2,1)S(1)}, u32[]{:S(2)}, u32[]{:S(2)}) collective-permute-start(bf16[9,8,128]{2,1,0:T(8,128)(2,1)S(1)} %get-tuple-element.12), channel_id=1, source_target_pairs={{0,2},{2,4},{4,6},{1,3},{3,5},{5,7},{8,10},{10,12},{12,14},{9,11},... | collective-permute-start | bytes 55304 | tf_op jit(solution)/shard_map/ppermute | solution.py:619
  6.7 5.1 %collective-permute-start.1 = (bf16[9,8,128]{2,1,0:T(8,128)(2,1)S(1)}, bf16[9,8,128]{2,1,0:T(8,128)(2,1)S(1)}, u32[]{:S(2)}, u32[]{:S(2)}) collective-permute-start(bf16[9,8,128]{2,1,0:T(8,128)(2,1)S(1)} %get-tuple-element.13), channel_id=1, source_target_pairs={{2,0},{4,2},{6,4},{3,1},{5,3},{7,5},{10,8},{12,10},{14,12},{11,9},... | collective-permute-start | bytes 55304 | tf_op jit(solution)/shard_map/ppermute | solution.py:620
  21.8 19.2 %collective-permute-start.4 = (bf16[4,272,128]{2,1,0:T(8,128)(2,1)S(1)}, bf16[4,272,128]{2,1,0:T(8,128)(2,1)S(1)}, u32[]{:S(2)}, u32[]{:S(2)}) collective-permute-start(bf16[4,272,128]{2,1,0:T(8,128)(2,1)S(1)} %get-tuple-element.16.refs_0_), channel_id=1, source_target_pairs={{1,0},{8,1},{9,8},{16,9},{17,16},{24,17},{25,24},{3,2},{10,3},{11,... | collective-permute-start | bytes 835592 | tf_op jit(solution)/shard_map/ppermute | solution.py:646
  23.8 17.2 %collective-permute-start.3 = (bf16[4,272,128]{2,1,0:T(8,128)(2,1)S(1)}, bf16[4,272,128]{2,1,0:T(8,128)(2,1)S(1)}, u32[]{:S(2)}, u32[]{:S(2)}) collective-permute-start(bf16[4,272,128]{2,1,0:T(8,128)(2,1)S(1)} %get-tuple-element.17.refs_1_), channel_id=1, source_target_pairs={{0,1},{1,8},{8,9},{9,16},{16,17},{17,24},{24,25},{2,3},{3,10},{10,... | collective-permute-start | bytes 835592 | tf_op jit(solution)/shard_map/ppermute | solution.py:645
  27.3 13.7 %collective-permute-start.5 = (bf16[816,128]{1,0:T(8,128)(2,1)S(1)}, bf16[816,128]{1,0:T(8,128)(2,1)S(1)}, u32[]{:S(2)}, u32[]{:S(2)}) collective-permute-start(bf16[816,128]{1,0:T(8,128)(2,1)S(1)} %get-tuple-element.18.refs_5_), channel_id=1, source_target_pairs={{0,1},{1,0},{2,3},{3,2},{4,5},{5,4},{6,7},{7,6},{8,9},{9,8},{10,11... | collective-permute-start | bytes 626696 | tf_op jit(solution)/shard_map/ppermute | solution.py:600

commit v5 on v4

--- a/solution.py
+++ b/solution.py
@@ -336,11 +336,15 @@
         weave(*threads)
 
 
+def parity():
+    return (lax.axis_index("row") * lax.axis_size("ch") + lax.axis_index("ch")) % 2
+
+
 def regular_kernel(
     x_hbm, labels_hbm, left_ref, right_ref, rel_ref, *refs, groups, own_heads, entries, part, hidden
 ):
     packs, refs = refs[:groups], refs[groups:]
-    (top_ref, bottom_ref, bias_ref, x_ref, labels_ref, sems, out_ref, qkv_ref, att_ref), scratch = refs[:9], refs[9:]
+    (near_ref, far_ref, bias_ref, x_ref, labels_ref, sems, out_ref, qkv_ref, att_ref, id_ref), scratch = refs[:10], refs[10:]
     cols = x_hbm.shape[1]
     x_copy = pltpu.make_async_copy(x_hbm, x_ref.at[:, 0:cols], sems.at[0])
     labels_copy = pltpu.make_async_copy(labels_hbm, labels_ref, sems.at[1])
@@ -376,9 +380,7 @@
     window = lax.broadcasted_iota(jnp.int32, (span, 128), 1)
     chosen = ((source - 128 + SHIFT) // WIN == window) & (source >= 128 - SHIFT)
     ids = dot_nn(spread, chosen.astype(F32).astype(BF))
-    for r in range(WIN):
-        target = top_ref if r < SHIFT else bottom_ref
-        target[r % SHIFT, cols + WIN :, :] = ids[r * WIN : (r + 1) * WIN].astype(BF)
+    id_ref[...] = ids.reshape(WIN, WIN, 128).astype(BF)
 
     group = 4
     span = group * WIN
@@ -430,22 +432,29 @@
     x_copy.wait()
     pipeline(x_ref.shape[1] // span, first, second, third)
     before = lax.broadcasted_iota(jnp.int32, (WIN, c), 0) < SHIFT
-    for r in range(WIN):
-        target = top_ref if r < SHIFT else bottom_ref
-        target[r % SHIFT, 0:cols, :] = out_ref[r, 0:cols, :]
-        edges = out_ref[r, cols : cols + 2 * WIN, :].astype(F32)
-        edge = jnp.where(before, edges[WIN:], edges[:WIN])
-        target[r % SHIFT, cols : cols + WIN, :] = edge.astype(BF)
-
-
-def shifted_kernel(
-    top_ref, bottom_ref, above_ref, below_ref, rel_ref, *refs,
-    group, groups, own_heads, entries, part, hidden,
-):
+    for target, side in ((near_ref, 1 - parity()), (far_ref, parity())):
+        for r in range(SHIFT):
+            row = side * SHIFT + r
+            target[r, 0:cols, :] = out_ref[row, 0:cols, :]
+            edges = out_ref[row, cols : cols + 2 * WIN, :].astype(F32)
+            edge = jnp.where(before, edges[WIN:], edges[:WIN])
+            target[r, cols : cols + WIN, :] = edge.astype(BF)
+            target[r, cols + WIN :, :] = id_ref[row]
+
+
+def even_split(count, most):
+    parts = -(-count // most)
+    return [(count * k // parts, count * (k + 1) // parts) for k in range(parts)]
+
+
+def shifted_kernel(own_in, halo_in, rel_ref, *refs, chunks, near, groups, own_heads, entries, part, hidden):
     packs, refs = refs[:groups], refs[groups:]
-    (out_ref, bias_ref, own_ref, halo_ref, res_ref, qid_ref, kid_ref), refs = refs[:7], refs[7:]
+    if not near:
+        done_ref, refs = refs[0], refs[1:]
+    (out_ref, bias_ref, own_ref, halo_ref, res_ref), refs = refs[:5], refs[5:]
     (q_ref, kv_ref, att_ref), scratch = refs[:3], refs[3:]
-    c = top_ref.shape[2]
+    side = 1 - parity() if near else parity()
+    c = own_in.shape[2]
     cols = out_ref.shape[1]
     heads = own_heads * groups
     depth = c // heads
@@ -467,41 +476,40 @@
     )
     lane = lax.broadcasted_iota(jnp.int32, rel.shape, 1)
     rel = jnp.where(lane % WIN < SHIFT, pltpu.roll(rel, 128 - SHIFT, 1), pltpu.roll(rel, SHIFT, 1))
-    rel = jnp.concatenate([pltpu.roll(rel[half:], half, 1), rel[:half]], axis=0)
+    rel = jnp.where(side == 0, pltpu.roll(rel[half:], half, 1), rel[:half])
     bias_ref[...] = w.bias(own_heads, entries - 128, rel)
 
-    for s, (own, halo) in enumerate(((top_ref, above_ref), (bottom_ref, below_ref))):
-        parts = []
-        for dst, src in ((own_ref, own), (halo_ref, halo)):
-            value = src[...].astype(F32)
-            edge = value[:, cols : cols + WIN]
-            dst[s * SHIFT : (s + 1) * SHIFT, 0:WIN, :] = edge
-            dst[s * SHIFT : (s + 1) * SHIFT, WIN : WIN + cols, :] = value[:, :cols]
-            dst[s * SHIFT : (s + 1) * SHIFT, WIN + cols :, :] = edge
-            parts.append(value[:, cols + WIN :].reshape(half, 128))
-        qid_ref[s] = parts[0]
-        both = jnp.concatenate(parts + parts, axis=0)
-        kid_ref[s] = both.T
+    parts = []
+    for dst, src in ((own_ref, own_in), (halo_ref, halo_in)):
+        value = src[...].astype(F32)
+        edge = value[:, cols : cols + WIN]
+        dst[:, 0:WIN, :] = edge
+        dst[:, WIN : WIN + cols, :] = value[:, :cols]
+        dst[:, WIN + cols :, :] = edge
+        parts.append(value[:, cols + WIN :].reshape(half, 128))
+    query_ids = parts[0]
+    key_ids = jnp.concatenate(parts + parts, axis=0).T
     earlier = lax.broadcasted_iota(jnp.int32, (WIN, c), 0) < SHIFT
 
     def gather(ref, i):
         pieces = []
-        for n in range(group):
-            start = (i * group + n) * WIN
-            for r in range(WIN):
-                before = ref[r, start : start + WIN, :]
-                after = ref[r, start + WIN : start + 2 * WIN, :]
+        for j in range(*chunks[i]):
+            for r in range(SHIFT):
+                before = ref[r, j * WIN : (j + 1) * WIN, :]
+                after = ref[r, (j + 1) * WIN : (j + 2) * WIN, :]
                 pieces.append(jnp.where(earlier, after, before))
         return jnp.concatenate(pieces, axis=0)
 
     def first(i):
+        slot = i % 2
+        count = (chunks[i][1] - chunks[i][0]) * half
+
         def keep(target):
             def store(value):
-                target[...] = value
+                target[0:count] = value
 
             return store
 
-        slot = i % 2
         own = w.project_pieces(
             lambda: gather(own_ref, i),
             [(0, scale, keep(q_ref.at[slot]))]
@@ -514,10 +522,10 @@
 
     def second(i):
         slot = i % 2
-
-        def window(n, s):
-            j = i * group + n
-            rows = slice((n * 2 + s) * half, (n * 2 + s + 1) * half)
+        base = chunks[i][0]
+
+        def window(j):
+            rows = slice((j - base) * half, (j - base + 1) * half)
 
             def read():
                 k, v = (
@@ -527,39 +535,41 @@
                 return q_ref[slot, rows], k, v
 
             def allowed():
-                keys = kid_ref[s, j : j + 1, :]
-                queries = jnp.broadcast_to(qid_ref[s, :, j : j + 1], (half, 128))
-                same = queries == keys
+                same = jnp.broadcast_to(query_ids[:, j : j + 1], (half, 128)) == key_ids[j : j + 1, :]
                 return jnp.concatenate([same, same], axis=1)
 
             def write(value):
                 att_ref[slot, rows] = value
 
-            return window_pieces(
-                read, lambda: bias_ref[s * half : (s + 1) * half], allowed, write, masks, ones
-            )
-
-        return skewed([window(n, s) for n in range(group) for s in range(2)])
+            return window_pieces(read, lambda: bias_ref[...], allowed, write, masks, ones)
+
+        return skewed([window(j) for j in range(*chunks[i])])
 
     def third(i):
-        start = i * group * WIN
+        base, stop = chunks[i]
 
         def store(out):
-            for r in range(WIN):
-                s, a = r // SHIFT, r % SHIFT
-                res_ref[r, start : start + group * WIN, :] = jnp.concatenate(
+            for r in range(SHIFT):
+                res_ref[r, base * WIN : stop * WIN, :] = jnp.concatenate(
                     [
-                        out[(n * 2 + s) * half + a * WIN : (n * 2 + s) * half + (a + 1) * WIN]
-                        for n in range(group)
+                        out[n * half + r * WIN : n * half + (r + 1) * WIN]
+                        for n in range(stop - base)
                     ],
                     axis=0,
                 )
 
-        return w.finish_pieces(lambda: gather(own_ref, i), lambda: att_ref[i % 2], store)
-
-    pipeline((cols + WIN) // (group * WIN), first, second, third)
-    low = lax.broadcasted_iota(jnp.int32, (WIN, cols, c), 1) % WIN < SHIFT
-    out_ref[...] = jnp.where(low, res_ref[:, 0:cols, :], res_ref[:, WIN : WIN + cols, :]).astype(BF)
+        return w.finish_pieces(
+            lambda: gather(own_ref, i), lambda: att_ref[i % 2, 0 : (stop - base) * half], store
+        )
+
+    pipeline(len(chunks), first, second, third)
+    low = lax.broadcasted_iota(jnp.int32, (SHIFT, cols, c), 1) % WIN < SHIFT
+    result = jnp.where(low, res_ref[:, 0:cols, :], res_ref[:, WIN : WIN + cols, :]).astype(BF)
+    if near:
+        out_ref[...] = result
+    else:
+        out_ref[pl.ds(side * SHIFT, SHIFT)] = result
+        out_ref[pl.ds((1 - side) * SHIFT, SHIFT)] = done_ref[...]
 
 
 def call(kernel, out_shapes, scratch, *args, in_specs=None):
@@ -631,32 +641,43 @@
     strip = jax.ShapeDtypeStruct((SHIFT, tile_cols + 2 * WIN, c), BF)
     bias_scratch = pltpu.VMEM((tokens, own_heads * groups * tokens), F32)
     wide = pltpu.VMEM((WIN, tile_cols + 4 * WIN, c), BF)
-    top, bottom = call(
+    near, far = call(
         lambda *refs: regular_kernel(*refs, **sizes),
         (strip, strip),
         [
             bias_scratch, wide, pltpu.VMEM(labels.shape, jnp.int32), pltpu.SemaphoreType.DMA((2,)),
             wide, pltpu.VMEM((2, 3, 4 * tokens, c), BF), pltpu.VMEM((2, 4 * tokens, c), BF),
+            pltpu.VMEM((WIN, WIN, 128), BF),
         ] + weights_scratch,
         in_hbm(image_tokens), in_hbm(labels), left, right, rel2, *packs0,
         in_specs=[pl.BlockSpec(memory_space=pltpu.HBM)] * 2
         + [pl.BlockSpec(memory_space=pltpu.VMEM)] * (3 + groups),
     )
-    above = lax.ppermute(bottom, ("row", "ch"), neighbours(("row", "ch"), 1))
-    below = lax.ppermute(top, ("row", "ch"), neighbours(("row", "ch"), -1))
-    wins = tile_cols // WIN + 1
-    group = max(g for g in range(1, 5) if wins % g == 0)
-    wide = pltpu.VMEM((WIN, tile_cols + 2 * WIN, c), F32)
+    bands = lax.axis_size(("row", "ch"))
+
+    def swapped(value, first):
+        pairs = [(m, m + 1) for m in range(first, bands - 1, 2)]
+        return lax.ppermute(value, ("row", "ch"), pairs + [(j, i) for i, j in pairs])
+
+    near_halo = swapped(near, 0)
+    far_halo = swapped(far, 1)
+    chunks = even_split(tile_cols // WIN + 1, 7)
+    most = max(stop - base for base, stop in chunks) * SHIFT * WIN
+    strip_wide = pltpu.VMEM((SHIFT, tile_cols + 2 * WIN, c), F32)
+    scratch = [
+        pltpu.VMEM((SHIFT * WIN, own_heads * groups * tokens), F32), strip_wide, strip_wide,
+        pltpu.VMEM((SHIFT, tile_cols + WIN, c), F32),
+        pltpu.VMEM((2, most, c), BF), pltpu.VMEM((2, 2, 2, most, c), BF), pltpu.VMEM((2, most, c), BF),
+    ] + weights_scratch
+    near_out = call(
+        lambda *refs: shifted_kernel(*refs, chunks=chunks, near=True, **sizes),
+        jax.ShapeDtypeStruct((SHIFT, tile_cols, c), BF),
+        scratch, near, near_halo, rel2, *packs1,
+    )
     return call(
-        lambda *refs: shifted_kernel(*refs, group=group, **sizes),
+        lambda *refs: shifted_kernel(*refs, chunks=chunks, near=False, **sizes),
         jax.ShapeDtypeStruct(image_tokens.shape, BF),
-        [
-            bias_scratch, wide, wide, pltpu.VMEM((WIN, tile_cols + WIN, c), F32),
-            pltpu.VMEM((2, SHIFT * WIN, 128), F32), pltpu.VMEM((2, 128, 128), F32),
-            pltpu.VMEM((2, group * tokens, c), BF), pltpu.VMEM((2, 2, 2, group * tokens, c), BF),
-            pltpu.VMEM((2, group * tokens, c), BF),
-        ] + weights_scratch,
-        top, bottom, above, below, rel2, *packs1,
+        scratch, far, far_halo, rel2, *packs1, near_out,
     )
 
 

time: 54 us -> 53.1 us (0.983); the launches traced: 53.1 us -> 52.8 us
  starting transfers between devices: 13.8 us -> 12.1 us
  Pallas kernels: 23.6 us -> 25 us
    ppermute x2, starting transfers between devices: 5.46 us -> 3.49 us  [swapped(): lax.ppermute(value, ('row', 'ch'), pairs + [(j, i) for i, j in pairs])]
    pallas_call x3 -> x4, Pallas kernels: 23.6 us -> 25 us  [call(): pl.pallas_call(kernel, out_shape=out_shapes, scratch_shapes=scratch, comp...]
  transfers between devices with their start and end apart: 6 -> 6, of which waited for: 2 -> 2; matrix products, arithmetic and copies ran while one was open for 0% -> 0% of each run, Pallas kernels for 0% -> 12%
where the time goes in v5:
time: 53.1 us; the launch traced here: 52.8 us
  Pallas kernels  25 us (47%)
  waiting for transfers between devices  15.6 us (29%)
  starting transfers between devices  12.1 us (23%)
    pallas_call x4, Pallas kernels, call(): pl.pallas_call(kernel, out_shape=out_shapes, scratch_shapes=scratch, comp...  25 us
    ppermute x2, waiting for transfers between devices, others(): found.append(lax.ppermute(found[-1], 'ch', swap))  12.4 us
    ppermute x1, starting transfers between devices, both_blocks(): left = lax.ppermute(right_edge, 'col', neighbours('col', 1))  3.95 us
    ppermute x2, starting transfers between devices, swapped(): lax.ppermute(value, ('row', 'ch'), pairs + [(j, i) for i, j in pairs])  3.49 us
    ppermute x1, waiting for transfers between devices, both_blocks(): right = lax.ppermute(left_edge, 'col', neighbours('col', -1))  3.14 us
    ppermute x2, starting transfers between devices, others(): found.append(lax.ppermute(found[-1], 'ch', swap))  2.73 us
    ppermute x1, starting transfers between devices, both_blocks(): right = lax.ppermute(left_edge, 'col', neighbours('col', -1))  1.92 us
  transfers between devices with their start and end apart: 6, of which 2 were waited for; matrix products, arithmetic and copies ran while one was open for 0% of the time, Pallas kernels for 12%

profile of v5, /device:TPU:9, one launch (start us, length us, event | category | flops | bytes accessed | tf_op | source)
XLA Modules:
  0.0 52.8 jit_solution(10784326752501557766)
XLA Ops:
  0.0 1.4 %shard_map.136 = (bf16[816,128]{1,0:T(8,128)(2,1)S(1)}, bf16[816,128]{1,0:T(8,128)(2,1)S(1)}, bf16[9,8,128]{2,1,0:T(8,128)(2,1)S(1)}, bf16[9,8,128]{2,1,0:T(8,128)(2,1)S(1)}, s32[64,128]{1,0:T(8,128)S(1)}) custom-call(bf16[8,256,128]{2,1,0:T(8,128)(2,1)} %refs_0_.3, s32[8,256]{1,0:T(8,128)} %refs_1_.3, s32[64,64]{1,0:T(8,128)} %refs_2_.1, ...), custom_call_target="tpu_custom_call" | custom-call | tf_op jit(solution)/shard_map/pallas_call | solution.py:577
  1.4 1.3 %collective-permute-start.2 = (bf16[816,128]{1,0:T(8,128)(2,1)S(1)}, bf16[816,128]{1,0:T(8,128)(2,1)S(1)}, u32[]{:S(2)}, u32[]{:S(2)}) collective-permute-start(bf16[816,128]{1,0:T(8,128)(2,1)S(1)} %get-tuple-element.15.refs_5_), channel_id=1, source_target_pairs={{0,1},{1,0},{2,3},{3,2},{4,5},{5,4},{6,7},{7,6},{8,9},{9,8},{10,11... | collective-permute-start | bytes 626696 | tf_op jit(solution)/shard_map/ppermute | solution.py:610
  2.7 3.9 %collective-permute-start = (bf16[9,8,128]{2,1,0:T(8,128)(2,1)S(1)}, bf16[9,8,128]{2,1,0:T(8,128)(2,1)S(1)}, u32[]{:S(2)}, u32[]{:S(2)}) collective-permute-start(bf16[9,8,128]{2,1,0:T(8,128)(2,1)S(1)} %get-tuple-element.12), channel_id=1, source_target_pairs={{0,2},{2,4},{4,6},{1,3},{3,5},{5,7},{8,10},{10,12},{12,14},{9,11},... | collective-permute-start | bytes 55304 | tf_op jit(solution)/shard_map/ppermute | solution.py:629
  6.7 1.9 %collective-permute-start.1 = (bf16[9,8,128]{2,1,0:T(8,128)(2,1)S(1)}, bf16[9,8,128]{2,1,0:T(8,128)(2,1)S(1)}, u32[]{:S(2)}, u32[]{:S(2)}) collective-permute-start(bf16[9,8,128]{2,1,0:T(8,128)(2,1)S(1)} %get-tuple-element.13), channel_id=1, source_target_pairs={{2,0},{4,2},{6,4},{3,1},{5,3},{7,5},{10,8},{12,10},{14,12},{11,9},... | collective-permute-start | bytes 55304 | tf_op jit(solution)/shard_map/ppermute | solution.py:630
  8.6 0.0 collective-permute-done.refs_2_
  8.6 3.1 %collective-permute-done.1.refs_3_ = bf16[9,8,128]{2,1,0:T(8,128)(2,1)S(1)} collective-permute-done((bf16[9,8,128]{2,1,0:T(8,128)(2,1)S(1)}, bf16[9,8,128]{2,1,0:T(8,128)(2,1)S(1)}, u32[]{:S(2)}, u32[]{:S(2)}) %collective-permute-start.1) | collective-permute-done | bytes 18464 | tf_op jit(solution)/shard_map/ppermute | solution.py:630
  11.8 0.0 collective-permute-done.2.refs_6_
  11.8 9.9 %shard_map.137 = (bf16[4,272,128]{2,1,0:T(8,128)(2,1)S(1)}, bf16[4,272,128]{2,1,0:T(8,128)(2,1)S(1)}) custom-call(bf16[8,256,128]{2,1,0:T(8,128)(2,1)} %refs_0_.3, s32[8,256]{1,0:T(8,128)} %refs_1_.3, bf16[9,8,128]{2,1,0:T(8,128)(2,1)S(1)} %collective-permute-done.refs_2_, bf16[9,8,128]{2,1,0:T(8,128)(2,1)S(1)} %collective-permute-done.1.refs_3_, ...), custom_call_target="tpu_custom_call" | custom-call | tf_op jit(solution)/shard_map/pallas_call | solution.py:577
  21.7 0.3 collective-permute-start.5
  22.0 3.2 %collective-permute-start.3 = (bf16[4,272,128]{2,1,0:T(8,128)(2,1)S(1)}, bf16[4,272,128]{2,1,0:T(8,128)(2,1)S(1)}, u32[]{:S(2)}, u32[]{:S(2)}) collective-permute-start(bf16[4,272,128]{2,1,0:T(8,128)(2,1)S(1)} %get-tuple-element.16.refs_0_), channel_id=1, source_target_pairs={{1,8},{9,16},{17,24},{8,1},{16,9},{24,17},{3,10},{11,18},{19,26},{... | collective-permute-start | bytes 835592 | tf_op jit(solution)/shard_map/ppermute | solution.py:660
  25.2 1.4 %collective-permute-start.4 = (bf16[816,128]{1,0:T(8,128)(2,1)S(1)}, bf16[816,128]{1,0:T(8,128)(2,1)S(1)}, u32[]{:S(2)}, u32[]{:S(2)}) collective-permute-start(bf16[816,128]{1,0:T(8,128)(2,1)S(1)} %get-tuple-element.17.refs_3_), channel_id=1, source_target_pairs={{0,1},{1,0},{2,3},{3,2},{4,5},{5,4},{6,7},{7,6},{8,9},{9,8},{10,11... | collective-permute-start | bytes 626696 | tf_op jit(solution)/shard_map/ppermute | solution.py:610
  26.6 12.4 %collective-permute-done.4.refs_4_ = bf16[816,128]{1,0:T(8,128)(2,1)S(1)} collective-permute-done((bf16[816,128]{1,0:T(8,128)(2,1)S(1)}, bf16[816,128]{1,0:T(8,128)(2,1)S(1)}, u32[]{:S(2)}, u32[]{:S(2)}) %collective-permute-start.4) | collective-permute-done | bytes 208928 | tf_op jit(solution)/shard_map/ppermute | solution.py:610
  39.1 0.0 collective-permute-done.5.refs_1_
  39.1 6.5 %shard_map.138.refs_5_ = bf16[4,256,128]{2,1,0:T(8,128)(2,1)S(1)} custom-call(bf16[4,272,128]{2,1,0:T(8,128)(2,1)S(1)} %get-tuple-element.18.refs_0_, bf16[4,272,128]{2,1,0:T(8,128)(2,1)S(1)} %collective-permute-done.5.refs_1_, s32[64,128]{1,0:T(8,128)S(1)} %get-tuple-element.14.refs_4_.refs_2_, bf16[816,128]{1,0:T(8,128)(2,1)S(1)} %get-tuple-element.17.refs_3_, ...), custom_call_target="tpu_custom_call" | custom-call | tf_op jit(solution)/shard_map/pallas_call | solution.py:577
  45.5 0.0 collective-permute-done.3.refs_1_
  45.5 7.3 %shard_map.139 = bf16[8,256,128]{2,1,0:T(8,128)(2,1)} custom-call(bf16[4,272,128]{2,1,0:T(8,128)(2,1)S(1)} %get-tuple-element.16.refs_0_, bf16[4,272,128]{2,1,0:T(8,128)(2,1)S(1)} %collective-permute-done.3.refs_1_, s32[64,128]{1,0:T(8,128)S(1)} %get-tuple-element.14.refs_4_.refs_2_, bf16[816,128]{1,0:T(8,128)(2,1)S(1)} %get-tuple-element.17.refs_3_, ...), custom_call_target="tpu_custom_call" | custom-call | tf_op jit(solution)/shard_map/pallas_call | solution.py:577
Async XLA Ops:
  1.4 10.3 %collective-permute-start.2 = (bf16[816,128]{1,0:T(8,128)(2,1)S(1)}, bf16[816,128]{1,0:T(8,128)(2,1)S(1)}, u32[]{:S(2)}, u32[]{:S(2)}) collective-permute-start(bf16[816,128]{1,0:T(8,128)(2,1)S(1)} %get-tuple-element.15.refs_5_), channel_id=1, source_target_pairs={{0,1},{1,0},{2,3},{3,2},{4,5},{5,4},{6,7},{7,6},{8,9},{9,8},{10,11... | collective-permute-start | bytes 626696 | tf_op jit(solution)/shard_map/ppermute | solution.py:610
  2.7 5.9 %collective-permute-start = (bf16[9,8,128]{2,1,0:T(8,128)(2,1)S(1)}, bf16[9,8,128]{2,1,0:T(8,128)(2,1)S(1)}, u32[]{:S(2)}, u32[]{:S(2)}) collective-permute-start(bf16[9,8,128]{2,1,0:T(8,128)(2,1)S(1)} %get-tuple-element.12), channel_id=1, source_target_pairs={{0,2},{2,4},{4,6},{1,3},{3,5},{5,7},{8,10},{10,12},{12,14},{9,11},... | collective-permute-start | bytes 55304 | tf_op jit(solution)/shard_map/ppermute | solution.py:629
  6.7 5.1 %collective-permute-start.1 = (bf16[9,8,128]{2,1,0:T(8,128)(2,1)S(1)}, bf16[9,8,128]{2,1,0:T(8,128)(2,1)S(1)}, u32[]{:S(2)}, u32[]{:S(2)}) collective-permute-start(bf16[9,8,128]{2,1,0:T(8,128)(2,1)S(1)} %get-tuple-element.13), channel_id=1, source_target_pairs={{2,0},{4,2},{6,4},{3,1},{5,3},{7,5},{10,8},{12,10},{14,12},{11,9},... | collective-permute-start | bytes 55304 | tf_op jit(solution)/shard_map/ppermute | solution.py:630
  21.7 17.4 %collective-permute-start.5 = (bf16[4,272,128]{2,1,0:T(8,128)(2,1)S(1)}, bf16[4,272,128]{2,1,0:T(8,128)(2,1)S(1)}, u32[]{:S(2)}, u32[]{:S(2)}) collective-permute-start(bf16[4,272,128]{2,1,0:T(8,128)(2,1)S(1)} %get-tuple-element.18.refs_0_), channel_id=1, source_target_pairs={{0,1},{8,9},{16,17},{24,25},{1,0},{9,8},{17,16},{25,24},{2,3},{10,... | collective-permute-start | bytes 835592 | tf_op jit(solution)/shard_map/ppermute | solution.py:660
  22.0 23.5 %collective-permute-start.3 = (bf16[4,272,128]{2,1,0:T(8,128)(2,1)S(1)}, bf16[4,272,128]{2,1,0:T(8,128)(2,1)S(1)}, u32[]{:S(2)}, u32[]{:S(2)}) collective-permute-start(bf16[4,272,128]{2,1,0:T(8,128)(2,1)S(1)} %get-tuple-element.16.refs_0_), channel_id=1, source_target_pairs={{1,8},{9,16},{17,24},{8,1},{16,9},{24,17},{3,10},{11,18},{19,26},{... | collective-permute-start | bytes 835592 | tf_op jit(solution)/shard_map/ppermute | solution.py:660
  25.2 13.9 %collective-permute-start.4 = (bf16[816,128]{1,0:T(8,128)(2,1)S(1)}, bf16[816,128]{1,0:T(8,128)(2,1)S(1)}, u32[]{:S(2)}, u32[]{:S(2)}) collective-permute-start(bf16[816,128]{1,0:T(8,128)(2,1)S(1)} %get-tuple-element.17.refs_3_), channel_id=1, source_target_pairs={{0,1},{1,0},{2,3},{3,2},{4,5},{5,4},{6,7},{7,6},{8,9},{9,8},{10,11... | collective-permute-start | bytes 626696 | tf_op jit(solution)/shard_map/ppermute | solution.py:610

commit v6 on v5

--- a/solution.py
+++ b/solution.py
@@ -66,7 +66,7 @@
 
     def store():
         width = at["o"].shape[1] // 2
-        write((at["o"][:, :width] / at["o"][:, width:]).astype(BF))
+        write(at["o"][:, :width] / at["o"][:, width:])
 
     return [score, reduce, mix, store]
 
@@ -78,6 +78,15 @@
         for t in range(len(pipelines) + depth - 1)
         for n in range(len(pipelines))
         if 0 <= t - n < len(pipelines[n])
+    ]
+
+
+def offset(threads, lag):
+    return [
+        thread[t - n * lag]
+        for t in range(max(len(thread) + n * lag for n, thread in enumerate(threads)))
+        for n, thread in enumerate(threads)
+        if 0 <= t - n * lag < len(thread)
     ]
 
 
@@ -199,9 +208,9 @@
             out.append(value[row : row + rows, :width])
         return out
 
-    def load(self):
+    def load(self, attention=True):
         c, part, hidden = self.c, self.part, self.hidden
-        for m in range(3):
+        for m in range(3 if attention else 0):
             rows = jnp.concatenate([p[m * part : (m + 1) * part, :] for p in self.packs], axis=0)
             self.qkv[:, m * c : (m + 1) * c] = rows.astype(F32).T.astype(BF)
         for g, p in enumerate(self.packs):
@@ -274,7 +283,7 @@
             begin()
             mean()
 
-        return [start, spread, normed] + [dot for dot, _ in made] + [keep for _, keep in made]
+        return [start, spread, normed], [dot for dot, _ in made] + [keep for _, keep in made]
 
     def finish_pieces(self, load, attended, store):
         at = {}
@@ -319,56 +328,28 @@
             store(total)
 
         starts = range(0, self.fc2.shape[0], width)
-        pieces = [project, start, spread, normed]
         chains = [[up(k), act(k), down(k)] for k in starts]
-        return pieces + skewed(chains) + [end]
+        return [project, start, spread, normed], skewed(chains) + [end]
 
 
 def pipeline(chunks, first, second, third):
-    for t in range(chunks + 2):
-        threads = []
-        if t >= 2:
-            threads.append(third(t - 2))
-        if 1 <= t <= chunks:
-            threads.append(second(t - 1))
-        if t < chunks:
-            threads.append(first(t))
-        weave(*threads)
+    stages = []
+    for i in range(chunks):
+        norm, rest = first(i)
+        mlp_start, mlp_rest = third(i)
+        stages.append([norm, rest, second(i), mlp_start, mlp_rest])
+    depth = len(stages[0])
+    for t in range(chunks + depth - 1):
+        weave(*[stages[t - d][d] for d in reversed(range(depth)) if 0 <= t - d < chunks])
 
 
 def parity():
     return (lax.axis_index("row") * lax.axis_size("ch") + lax.axis_index("ch")) % 2
 
 
-def regular_kernel(
-    x_hbm, labels_hbm, left_ref, right_ref, rel_ref, *refs, groups, own_heads, entries, part, hidden
-):
-    packs, refs = refs[:groups], refs[groups:]
-    (near_ref, far_ref, bias_ref, x_ref, labels_ref, sems, out_ref, qkv_ref, att_ref, id_ref), scratch = refs[:10], refs[10:]
-    cols = x_hbm.shape[1]
-    x_copy = pltpu.make_async_copy(x_hbm, x_ref.at[:, 0:cols], sems.at[0])
-    labels_copy = pltpu.make_async_copy(labels_hbm, labels_ref, sems.at[1])
-    x_copy.start()
-    labels_copy.start()
-    c = x_ref.shape[2]
-    heads = own_heads * groups
-    depth = c // heads
-    tokens = WIN * WIN
-    scale = depth ** (-0.5) * LOG2E
-    w = Weights(packs, scratch, c, part, hidden)
-    w.load()
-    masks = head_masks(heads, depth, c)
-    ones = jnp.concatenate(masks, axis=0)
-    bias_ref[...] = w.bias(own_heads, entries - 128, rel_ref[...])
-
-    labels_copy.wait()
+def edge_ids(left_ref, right_ref, labels):
     lanes = jnp.concatenate(
-        [
-            left_ref[WIN].astype(F32),
-            (labels_ref[...] + 1).astype(F32),
-            right_ref[WIN].astype(F32),
-        ],
-        axis=1,
+        [left_ref[WIN].astype(F32), (labels + 1).astype(F32), right_ref[WIN].astype(F32)], axis=1
     )
     span = lanes.shape[1]
     lane = lax.broadcasted_iota(jnp.int32, (WIN, span), 1)
@@ -379,67 +360,156 @@
     source = lax.broadcasted_iota(jnp.int32, (span, 128), 0)
     window = lax.broadcasted_iota(jnp.int32, (span, 128), 1)
     chosen = ((source - 128 + SHIFT) // WIN == window) & (source >= 128 - SHIFT)
-    ids = dot_nn(spread, chosen.astype(F32).astype(BF))
-    id_ref[...] = ids.reshape(WIN, WIN, 128).astype(BF)
-
-    group = 4
-    span = group * WIN
-
-    def load(i):
-        block = x_ref[:, i * span : (i + 1) * span, :].astype(F32)
-        return jnp.concatenate(
-            [block[r, n * WIN : (n + 1) * WIN] for n in range(group) for r in range(WIN)], axis=0
+    return dot_nn(spread, chosen.astype(F32).astype(BF)).reshape(WIN, WIN, 128).astype(BF)
+
+
+class Rows:
+
+    def __init__(self, weights, x_ref, out_ref, cols):
+        self.w, self.x, self.out, self.cols = weights, x_ref, out_ref, cols
+
+    def pieces(self, start, count, attended):
+        span = slice(start * WIN, (start + count) * WIN)
+
+        def load():
+            block = self.x[:, span, :].astype(F32)
+            return jnp.concatenate(
+                [block[r, n * WIN : (n + 1) * WIN] for n in range(count) for r in range(SHIFT)], axis=0
+            )
+
+        def store(out):
+            for r in range(SHIFT):
+                rows = [
+                    out[(n * SHIFT + r) * WIN : (n * SHIFT + r + 1) * WIN] for n in range(count)
+                ]
+                if start * WIN < self.cols:
+                    self.out[r, span, :] = jnp.concatenate(rows, axis=0).astype(BF)
+                else:
+                    before = lax.broadcasted_iota(jnp.int32, rows[0].shape, 0) < SHIFT
+                    self.out[r, span.start : span.start + WIN, :] = jnp.where(
+                        before, rows[1], rows[0]
+                    ).astype(BF)
+
+        return self.w.finish_pieces(load, attended, store)
+
+
+def block0_chunks(cols):
+    wins = cols // WIN
+    return [(n, 4) for n in range(0, wins, 4)] + [(wins, 2)]
+
+
+def put_edges(x_ref, left_ref, right_ref, cols, base=0):
+    for r in range(x_ref.shape[0]):
+        x_ref[r, cols : cols + 2 * WIN, :] = jnp.concatenate(
+            [left_ref[base + r], right_ref[base + r]], axis=0
         )
 
+
+def regular_kernel(
+    x_hbm, labels_hbm, left_ref, right_ref, rel_ref, *refs, groups, own_heads, entries, part, hidden
+):
+    packs, refs = refs[:groups], refs[groups:]
+    (near_ref, rest_ref, ids_ref, bias_ref, x_ref, side_ref), refs = refs[:6], refs[6:]
+    (labels_ref, sems, qkv_ref, att_ref), scratch = refs[:4], refs[4:]
+    side = 1 - parity()
+    cols = x_hbm.shape[1]
+    x_copy = pltpu.make_async_copy(x_hbm, x_ref.at[:, 0:cols], sems.at[0])
+    labels_copy = pltpu.make_async_copy(labels_hbm, labels_ref, sems.at[1])
+    side_copy = pltpu.make_async_copy(
+        x_hbm.at[pl.ds(side * SHIFT, SHIFT)], side_ref.at[:, 0:cols], sems.at[2]
+    )
+    x_copy.start()
+    labels_copy.start()
+    side_copy.start()
+    c = x_ref.shape[2]
+    heads = own_heads * groups
+    depth = c // heads
+    tokens = WIN * WIN
+    half = SHIFT * WIN
+    scale = depth ** (-0.5) * LOG2E
+    w = Weights(packs, scratch, c, part, hidden)
+    w.load()
+    masks = head_masks(heads, depth, c)
+    ones = jnp.concatenate(masks, axis=0)
+    bias_ref[...] = w.bias(own_heads, entries - 128, rel_ref[...])
+    labels_copy.wait()
+    ids_ref[...] = edge_ids(left_ref, right_ref, labels_ref[...])
+    put_edges(x_ref, left_ref, right_ref, cols)
+    put_edges(side_ref, left_ref, right_ref, cols, side * SHIFT)
+    x_copy.wait()
+    side_copy.wait()
+    chunks = block0_chunks(cols)
+    finish = Rows(w, side_ref, near_ref, cols)
+
     def first(i):
+        start, count = chunks[i]
+
+        def load():
+            block = x_ref[:, start * WIN : (start + count) * WIN, :].astype(F32)
+            return jnp.concatenate(
+                [block[r, n * WIN : (n + 1) * WIN] for n in range(count) for r in range(WIN)], axis=0
+            )
+
         def keep(m):
             def store(value):
-                qkv_ref[i % 2, m] = value
+                qkv_ref[i % 2, m, 0 : count * tokens] = value
 
             return store
 
-        return w.project_pieces(
-            lambda: load(i), [(0, scale, keep(0)), (1, None, keep(1)), (2, None, keep(2))]
-        )
+        return w.project_pieces(load, [(0, scale, keep(0)), (1, None, keep(1)), (2, None, keep(2))])
 
     def second(i):
+        start, count = chunks[i]
+
         def window(n):
             rows = slice(n * tokens, (n + 1) * tokens)
 
             def write(value):
-                att_ref[i % 2, rows] = value
+                low, high = value[:half], value[half:]
+                att_ref[i % 2, n * half : (n + 1) * half] = jnp.where(side == 0, low, high).astype(BF)
+                rest_ref[(start + n) * half : (start + n + 1) * half] = jnp.where(
+                    side == 0, high, low
+                ).astype(BF)
 
             return window_pieces(
                 lambda: [qkv_ref[i % 2, m, rows] for m in range(3)],
                 lambda: bias_ref[...], None, write, masks, ones,
             )
 
-        return skewed([window(n) for n in range(group)])
+        return skewed([window(n) for n in range(count)])
 
     def third(i):
-        def store(out):
-            for r in range(WIN):
-                out_ref[r, i * span : (i + 1) * span, :] = jnp.concatenate(
-                    [out[n * tokens + r * WIN : n * tokens + (r + 1) * WIN] for n in range(group)],
-                    axis=0,
-                ).astype(BF)
-
-        return w.finish_pieces(lambda: load(i), lambda: att_ref[i % 2], store)
-
-    for r in range(WIN):
-        x_ref[r, cols : cols + 2 * WIN, :] = jnp.concatenate([left_ref[r], right_ref[r]], axis=0)
-    x_ref[:, cols + 2 * WIN :, :] = jnp.zeros((WIN, x_ref.shape[1] - cols - 2 * WIN, c), BF)
+        start, count = chunks[i]
+        return finish.pieces(start, count, lambda: att_ref[i % 2, 0 : count * half])
+
+    pipeline(len(chunks), first, second, third)
+    for r in range(SHIFT):
+        near_ref[r, cols + WIN :, :] = ids_ref[side * SHIFT + r]
+
+
+def rest_kernel(x_hbm, left_ref, right_ref, att_ref, ids_ref, *refs, groups, own_heads, entries, part, hidden):
+    packs, refs = refs[:groups], refs[groups:]
+    (far_ref, x_ref, sems), scratch = refs[:3], refs[3:]
+    cols = x_hbm.shape[1]
+    side = parity()
+    x_copy = pltpu.make_async_copy(
+        x_hbm.at[pl.ds(side * SHIFT, SHIFT)], x_ref.at[:, 0:cols], sems.at[0]
+    )
+    x_copy.start()
+    w = Weights(packs, scratch, x_ref.shape[2], part, hidden)
+    w.load(attention=False)
+    put_edges(x_ref, left_ref, right_ref, cols, side * SHIFT)
+    finish = Rows(w, x_ref, far_ref, cols)
+    half = SHIFT * WIN
+    for r in range(SHIFT):
+        far_ref[r, cols + WIN :, :] = ids_ref[side * SHIFT + r]
     x_copy.wait()
-    pipeline(x_ref.shape[1] // span, first, second, third)
-    before = lax.broadcasted_iota(jnp.int32, (WIN, c), 0) < SHIFT
-    for target, side in ((near_ref, 1 - parity()), (far_ref, parity())):
-        for r in range(SHIFT):
-            row = side * SHIFT + r
-            target[r, 0:cols, :] = out_ref[row, 0:cols, :]
-            edges = out_ref[row, cols : cols + 2 * WIN, :].astype(F32)
-            edge = jnp.where(before, edges[WIN:], edges[:WIN])
-            target[r, cols : cols + WIN, :] = edge.astype(BF)
-            target[r, cols + WIN :, :] = id_ref[row]
+    threads = []
+    for start, count in block0_chunks(cols):
+        rows = slice(start * half, (start + count) * half)
+        threads.append(sum(finish.pieces(start, count, lambda rows=rows: att_ref[rows]), []))
+    for piece in offset(threads, 4):
+        piece()
 
 
 def even_split(count, most):
@@ -518,7 +588,7 @@
         halo = w.project_pieces(
             lambda: gather(halo_ref, i), [(1 + m, None, keep(kv_ref.at[slot, m, 1])) for m in range(2)]
         )
-        return skewed([own, halo])
+        return [skewed(list(pair)) for pair in zip(own, halo)]
 
     def second(i):
         slot = i % 2
@@ -539,7 +609,7 @@
                 return jnp.concatenate([same, same], axis=1)
 
             def write(value):
-                att_ref[slot, rows] = value
+                att_ref[slot, rows] = value.astype(BF)
 
             return window_pieces(read, lambda: bias_ref[...], allowed, write, masks, ones)
 
@@ -640,26 +710,38 @@
     ]
     strip = jax.ShapeDtypeStruct((SHIFT, tile_cols + 2 * WIN, c), BF)
     bias_scratch = pltpu.VMEM((tokens, own_heads * groups * tokens), F32)
-    wide = pltpu.VMEM((WIN, tile_cols + 4 * WIN, c), BF)
-    near, far = call(
-        lambda *refs: regular_kernel(*refs, **sizes),
-        (strip, strip),
-        [
-            bias_scratch, wide, pltpu.VMEM(labels.shape, jnp.int32), pltpu.SemaphoreType.DMA((2,)),
-            wide, pltpu.VMEM((2, 3, 4 * tokens, c), BF), pltpu.VMEM((2, 4 * tokens, c), BF),
-            pltpu.VMEM((WIN, WIN, 128), BF),
-        ] + weights_scratch,
-        in_hbm(image_tokens), in_hbm(labels), left, right, rel2, *packs0,
-        in_specs=[pl.BlockSpec(memory_space=pltpu.HBM)] * 2
-        + [pl.BlockSpec(memory_space=pltpu.VMEM)] * (3 + groups),
-    )
+    wide = pltpu.VMEM((WIN, tile_cols + 2 * WIN, c), BF)
+    half_wide = pltpu.VMEM((SHIFT, tile_cols + 2 * WIN, c), BF)
     bands = lax.axis_size(("row", "ch"))
 
     def swapped(value, first):
         pairs = [(m, m + 1) for m in range(first, bands - 1, 2)]
         return lax.ppermute(value, ("row", "ch"), pairs + [(j, i) for i, j in pairs])
 
+    in_vmem = pl.BlockSpec(memory_space=pltpu.VMEM)
+    near, rest, ids = call(
+        lambda *refs: regular_kernel(*refs, **sizes),
+        (
+            strip,
+            jax.ShapeDtypeStruct((SHIFT * (tile_cols + 2 * WIN), c), BF),
+            jax.ShapeDtypeStruct((WIN, WIN, 128), BF),
+        ),
+        [
+            bias_scratch, wide, half_wide,
+            pltpu.VMEM(labels.shape, jnp.int32), pltpu.SemaphoreType.DMA((3,)),
+            pltpu.VMEM((2, 3, 4 * tokens, c), BF), pltpu.VMEM((2, 2 * tokens, c), BF),
+        ] + weights_scratch,
+        in_hbm(image_tokens), in_hbm(labels), left, right, rel2, *packs0,
+        in_specs=[pl.BlockSpec(memory_space=pltpu.HBM)] * 2 + [in_vmem] * (3 + groups),
+    )
     near_halo = swapped(near, 0)
+    far = call(
+        lambda *refs: rest_kernel(*refs, **sizes),
+        strip,
+        [half_wide, pltpu.SemaphoreType.DMA((1,))] + weights_scratch,
+        in_hbm(image_tokens), left, right, rest, ids, *packs0,
+        in_specs=[pl.BlockSpec(memory_space=pltpu.HBM)] + [in_vmem] * (4 + groups),
+    )
     far_halo = swapped(far, 1)
     chunks = even_split(tile_cols // WIN + 1, 7)
     most = max(stop - base for base, stop in chunks) * SHIFT * WIN

time: 53.1 us -> 51.8 us (0.976)
  waiting for transfers between devices: 15.6 us -> 13.4 us
  Pallas kernels: 25 us -> 26 us
    ppermute x2, waiting for transfers between devices: 12.4 us -> 10.3 us  [others(): found.append(lax.ppermute(found[-1], 'ch', swap))]
    pallas_call x4 -> x5, Pallas kernels: 25 us -> 26 us  [call(): pl.pallas_call(kernel, out_shape=out_shapes, scratch_shapes=scratch, comp...]
  transfers between devices with their start and end apart: 6 -> 6, of which waited for: 2 -> 2; matrix products, arithmetic and copies ran while one was open for 0% -> 0% of each run, Pallas kernels for 12% -> 19%
where the time goes in v6:
time: 51.8 us; the launch traced here: 51.6 us
  Pallas kernels  26 us (50%)
  waiting for transfers between devices  13.4 us (26%)
  starting transfers between devices  12.1 us (23%)
    pallas_call x5, Pallas kernels, call(): pl.pallas_call(kernel, out_shape=out_shapes, scratch_shapes=scratch, comp...  26 us
    ppermute x2, waiting for transfers between devices, others(): found.append(lax.ppermute(found[-1], 'ch', swap))  10.3 us
    ppermute x1, starting transfers between devices, both_blocks(): left = lax.ppermute(right_edge, 'col', neighbours('col', 1))  3.95 us
    ppermute x2, starting transfers between devices, swapped(): lax.ppermute(value, ('row', 'ch'), pairs + [(j, i) for i, j in pairs])  3.51 us
    ppermute x1, waiting for transfers between devices, both_blocks(): right = lax.ppermute(left_edge, 'col', neighbours('col', -1))  3.14 us
    ppermute x2, starting transfers between devices, others(): found.append(lax.ppermute(found[-1], 'ch', swap))  2.71 us
    ppermute x1, starting transfers between devices, both_blocks(): right = lax.ppermute(left_edge, 'col', neighbours('col', -1))  1.92 us
  transfers between devices with their start and end apart: 6, of which 2 were waited for; matrix products, arithmetic and copies ran while one was open for 0% of the time, Pallas kernels for 19%

profile of v6, /device:TPU:9, one launch (start us, length us, event | category | flops | bytes accessed | tf_op | source)
XLA Modules:
  0.0 51.6 jit_solution(10412040243266165052)
XLA Ops:
  0.0 1.4 %shard_map.136 = (bf16[816,128]{1,0:T(8,128)(2,1)S(1)}, bf16[816,128]{1,0:T(8,128)(2,1)S(1)}, bf16[9,8,128]{2,1,0:T(8,128)(2,1)S(1)}, bf16[9,8,128]{2,1,0:T(8,128)(2,1)S(1)}, s32[64,128]{1,0:T(8,128)S(1)}) custom-call(bf16[8,256,128]{2,1,0:T(8,128)(2,1)} %refs_0_.5, s32[8,256]{1,0:T(8,128)} %refs_1_.3, s32[64,64]{1,0:T(8,128)} %refs_2_.1, ...), custom_call_target="tpu_custom_call" | custom-call | tf_op jit(solution)/shard_map/pallas_call | solution.py:647
  1.4 1.3 %collective-permute-start.2 = (bf16[816,128]{1,0:T(8,128)(2,1)S(1)}, bf16[816,128]{1,0:T(8,128)(2,1)S(1)}, u32[]{:S(2)}, u32[]{:S(2)}) collective-permute-start(bf16[816,128]{1,0:T(8,128)(2,1)S(1)} %get-tuple-element.16.refs_5_), channel_id=1, source_target_pairs={{0,1},{1,0},{2,3},{3,2},{4,5},{5,4},{6,7},{7,6},{8,9},{9,8},{10,11... | collective-permute-start | bytes 626696 | tf_op jit(solution)/shard_map/ppermute | solution.py:680
  2.7 3.9 %collective-permute-start = (bf16[9,8,128]{2,1,0:T(8,128)(2,1)S(1)}, bf16[9,8,128]{2,1,0:T(8,128)(2,1)S(1)}, u32[]{:S(2)}, u32[]{:S(2)}) collective-permute-start(bf16[9,8,128]{2,1,0:T(8,128)(2,1)S(1)} %get-tuple-element.13), channel_id=1, source_target_pairs={{0,2},{2,4},{4,6},{1,3},{3,5},{5,7},{8,10},{10,12},{12,14},{9,11},... | collective-permute-start | bytes 55304 | tf_op jit(solution)/shard_map/ppermute | solution.py:699
  6.7 1.9 %collective-permute-start.1 = (bf16[9,8,128]{2,1,0:T(8,128)(2,1)S(1)}, bf16[9,8,128]{2,1,0:T(8,128)(2,1)S(1)}, u32[]{:S(2)}, u32[]{:S(2)}) collective-permute-start(bf16[9,8,128]{2,1,0:T(8,128)(2,1)S(1)} %get-tuple-element.14), channel_id=1, source_target_pairs={{2,0},{4,2},{6,4},{3,1},{5,3},{7,5},{10,8},{12,10},{14,12},{11,9},... | collective-permute-start | bytes 55304 | tf_op jit(solution)/shard_map/ppermute | solution.py:700
  8.6 0.0 collective-permute-done.refs_2_.refs_1_
  8.6 3.1 %collective-permute-done.1.refs_3_.refs_2_ = bf16[9,8,128]{2,1,0:T(8,128)(2,1)S(1)} collective-permute-done((bf16[9,8,128]{2,1,0:T(8,128)(2,1)S(1)}, bf16[9,8,128]{2,1,0:T(8,128)(2,1)S(1)}, u32[]{:S(2)}, u32[]{:S(2)}) %collective-permute-start.1) | collective-permute-done | bytes 18464 | tf_op jit(solution)/shard_map/ppermute | solution.py:700
  11.8 0.0 collective-permute-done.2.refs_6_
  11.8 7.7 %shard_map.137 = (bf16[4,272,128]{2,1,0:T(8,128)(2,1)S(1)}, bf16[1088,128]{1,0:T(8,128)(2,1)S(1)}, bf16[8,8,128]{2,1,0:T(8,128)(2,1)S(1)}) custom-call(bf16[8,256,128]{2,1,0:T(8,128)(2,1)} %refs_0_.5, s32[8,256]{1,0:T(8,128)} %refs_1_.3, bf16[9,8,128]{2,1,0:T(8,128)(2,1)S(1)} %collective-permute-done.refs_2_.refs_1_, ...), custom_call_target="tpu_custom_call" | custom-call | tf_op jit(solution)/shard_map/pallas_call | solution.py:647
  19.5 0.3 collective-permute-start.5
  19.8 3.4 %shard_map.138.refs_0_ = bf16[4,272,128]{2,1,0:T(8,128)(2,1)S(1)} custom-call(bf16[8,256,128]{2,1,0:T(8,128)(2,1)} %refs_0_.5, bf16[9,8,128]{2,1,0:T(8,128)(2,1)S(1)} %collective-permute-done.refs_2_.refs_1_, bf16[9,8,128]{2,1,0:T(8,128)(2,1)S(1)} %collective-permute-done.1.refs_3_.refs_2_, bf16[1088,128]{1,0:T(8,128)(2,1)S(1)} %get-tuple-element.17.refs_3_, ...), custom_call_target="tpu_custom_call" | custom-call | tf_op jit(solution)/shard_map/pallas_call | solution.py:647
  23.2 3.2 %collective-permute-start.3 = (bf16[4,272,128]{2,1,0:T(8,128)(2,1)S(1)}, bf16[4,272,128]{2,1,0:T(8,128)(2,1)S(1)}, u32[]{:S(2)}, u32[]{:S(2)}) collective-permute-start(bf16[4,272,128]{2,1,0:T(8,128)(2,1)S(1)} %shard_map.138.refs_0_), channel_id=1, source_target_pairs={{1,8},{9,16},{17,24},{8,1},{16,9},{24,17},{3,10},{11,18},{19,26},{... | collective-permute-start | bytes 835592 | tf_op jit(solution)/shard_map/ppermute | solution.py:719
  26.5 1.4 %collective-permute-start.4 = (bf16[816,128]{1,0:T(8,128)(2,1)S(1)}, bf16[816,128]{1,0:T(8,128)(2,1)S(1)}, u32[]{:S(2)}, u32[]{:S(2)}) collective-permute-start(bf16[816,128]{1,0:T(8,128)(2,1)S(1)} %get-tuple-element.19.refs_3_), channel_id=1, source_target_pairs={{0,1},{1,0},{2,3},{3,2},{4,5},{5,4},{6,7},{7,6},{8,9},{9,8},{10,11... | collective-permute-start | bytes 626696 | tf_op jit(solution)/shard_map/ppermute | solution.py:680
  27.9 10.3 %collective-permute-done.4.refs_4_ = bf16[816,128]{1,0:T(8,128)(2,1)S(1)} collective-permute-done((bf16[816,128]{1,0:T(8,128)(2,1)S(1)}, bf16[816,128]{1,0:T(8,128)(2,1)S(1)}, u32[]{:S(2)}, u32[]{:S(2)}) %collective-permute-start.4) | collective-permute-done | bytes 208928 | tf_op jit(solution)/shard_map/ppermute | solution.py:680
  38.1 0.0 collective-permute-done.5.refs_1_
  38.1 6.3 %shard_map.139.refs_5_ = bf16[4,256,128]{2,1,0:T(8,128)(2,1)S(1)} custom-call(bf16[4,272,128]{2,1,0:T(8,128)(2,1)S(1)} %get-tuple-element.20.refs_0_, bf16[4,272,128]{2,1,0:T(8,128)(2,1)S(1)} %collective-permute-done.5.refs_1_, s32[64,128]{1,0:T(8,128)S(1)} %get-tuple-element.15.refs_4_.refs_2_, bf16[816,128]{1,0:T(8,128)(2,1)S(1)} %get-tuple-element.19.refs_3_, ...), custom_call_target="tpu_custom_call" | custom-call | tf_op jit(solution)/shard_map/pallas_call | solution.py:647
  44.5 0.0 collective-permute-done.3.refs_1_
  44.5 7.1 %shard_map.140 = bf16[8,256,128]{2,1,0:T(8,128)(2,1)} custom-call(bf16[4,272,128]{2,1,0:T(8,128)(2,1)S(1)} %shard_map.138.refs_0_, bf16[4,272,128]{2,1,0:T(8,128)(2,1)S(1)} %collective-permute-done.3.refs_1_, s32[64,128]{1,0:T(8,128)S(1)} %get-tuple-element.15.refs_4_.refs_2_, bf16[816,128]{1,0:T(8,128)(2,1)S(1)} %get-tuple-element.19.refs_3_, ...), custom_call_target="tpu_custom_call" | custom-call | tf_op jit(solution)/shard_map/pallas_call | solution.py:647
Async XLA Ops:
  1.4 10.3 %collective-permute-start.2 = (bf16[816,128]{1,0:T(8,128)(2,1)S(1)}, bf16[816,128]{1,0:T(8,128)(2,1)S(1)}, u32[]{:S(2)}, u32[]{:S(2)}) collective-permute-start(bf16[816,128]{1,0:T(8,128)(2,1)S(1)} %get-tuple-element.16.refs_5_), channel_id=1, source_target_pairs={{0,1},{1,0},{2,3},{3,2},{4,5},{5,4},{6,7},{7,6},{8,9},{9,8},{10,11... | collective-permute-start | bytes 626696 | tf_op jit(solution)/shard_map/ppermute | solution.py:680
  2.7 5.9 %collective-permute-start = (bf16[9,8,128]{2,1,0:T(8,128)(2,1)S(1)}, bf16[9,8,128]{2,1,0:T(8,128)(2,1)S(1)}, u32[]{:S(2)}, u32[]{:S(2)}) collective-permute-start(bf16[9,8,128]{2,1,0:T(8,128)(2,1)S(1)} %get-tuple-element.13), channel_id=1, source_target_pairs={{0,2},{2,4},{4,6},{1,3},{3,5},{5,7},{8,10},{10,12},{12,14},{9,11},... | collective-permute-start | bytes 55304 | tf_op jit(solution)/shard_map/ppermute | solution.py:699
  6.7 5.1 %collective-permute-start.1 = (bf16[9,8,128]{2,1,0:T(8,128)(2,1)S(1)}, bf16[9,8,128]{2,1,0:T(8,128)(2,1)S(1)}, u32[]{:S(2)}, u32[]{:S(2)}) collective-permute-start(bf16[9,8,128]{2,1,0:T(8,128)(2,1)S(1)} %get-tuple-element.14), channel_id=1, source_target_pairs={{2,0},{4,2},{6,4},{3,1},{5,3},{7,5},{10,8},{12,10},{14,12},{11,9},... | collective-permute-start | bytes 55304 | tf_op jit(solution)/shard_map/ppermute | solution.py:700
  19.5 18.6 %collective-permute-start.5 = (bf16[4,272,128]{2,1,0:T(8,128)(2,1)S(1)}, bf16[4,272,128]{2,1,0:T(8,128)(2,1)S(1)}, u32[]{:S(2)}, u32[]{:S(2)}) collective-permute-start(bf16[4,272,128]{2,1,0:T(8,128)(2,1)S(1)} %get-tuple-element.20.refs_0_), channel_id=1, source_target_pairs={{0,1},{8,9},{16,17},{24,25},{1,0},{9,8},{17,16},{25,24},{2,3},{10,... | collective-permute-start | bytes 835592 | tf_op jit(solution)/shard_map/ppermute | solution.py:719
  23.2 21.2 %collective-permute-start.3 = (bf16[4,272,128]{2,1,0:T(8,128)(2,1)S(1)}, bf16[4,272,128]{2,1,0:T(8,128)(2,1)S(1)}, u32[]{:S(2)}, u32[]{:S(2)}) collective-permute-start(bf16[4,272,128]{2,1,0:T(8,128)(2,1)S(1)} %shard_map.138.refs_0_), channel_id=1, source_target_pairs={{1,8},{9,16},{17,24},{8,1},{16,9},{24,17},{3,10},{11,18},{19,26},{... | collective-permute-start | bytes 835592 | tf_op jit(solution)/shard_map/ppermute | solution.py:719
  26.5 11.7 %collective-permute-start.4 = (bf16[816,128]{1,0:T(8,128)(2,1)S(1)}, bf16[816,128]{1,0:T(8,128)(2,1)S(1)}, u32[]{:S(2)}, u32[]{:S(2)}) collective-permute-start(bf16[816,128]{1,0:T(8,128)(2,1)S(1)} %get-tuple-element.19.refs_3_), channel_id=1, source_target_pairs={{0,1},{1,0},{2,3},{3,2},{4,5},{5,4},{6,7},{7,6},{8,9},{9,8},{10,11... | collective-permute-start | bytes 626696 | tf_op jit(solution)/shard_map/ppermute | solution.py:680

commit v7 on v6

--- a/solution.py
+++ b/solution.py
@@ -208,20 +208,8 @@
             out.append(value[row : row + rows, :width])
         return out
 
-    def load(self, attention=True):
+    def load_rows(self):
         c, part, hidden = self.c, self.part, self.hidden
-        for m in range(3 if attention else 0):
-            rows = jnp.concatenate([p[m * part : (m + 1) * part, :] for p in self.packs], axis=0)
-            self.qkv[:, m * c : (m + 1) * c] = rows.astype(F32).T.astype(BF)
-        for g, p in enumerate(self.packs):
-            at = 3 * part
-            self.proj[g * part : (g + 1) * part, :] = p[at : at + part, :]
-            at += part
-            for k in range(hidden // 128):
-                lane = g * hidden + k * 128
-                self.fc1[:, lane : lane + 128] = p[at : at + c, :]
-                at += c
-            self.fc2[g * hidden : (g + 1) * hidden, :] = p[at : at + hidden, :]
         vectors = [self.small(GAIN + k)[0] for k in range(2)]
         vectors += [self.small(SHIFTS + k)[0] for k in range(2)]
         vectors += [self.small(PROJB)[0], self.small(FC2B)[0]]
@@ -235,6 +223,24 @@
             [row[g] for g in range(len(self.packs)) for row in rows], axis=1
         )
 
+    def load_qkv(self):
+        c, part = self.c, self.part
+        for m in range(3):
+            rows = jnp.concatenate([p[m * part : (m + 1) * part, :] for p in self.packs], axis=0)
+            self.qkv[:, m * c : (m + 1) * c] = rows.astype(F32).T.astype(BF)
+
+    def load_rest(self):
+        c, part, hidden = self.c, self.part, self.hidden
+        for g, p in enumerate(self.packs):
+            at = 3 * part
+            self.proj[g * part : (g + 1) * part, :] = p[at : at + part, :]
+            at += part
+            for k in range(hidden // 128):
+                lane = g * hidden + k * 128
+                self.fc1[:, lane : lane + 128] = p[at : at + c, :]
+                at += c
+            self.fc2[g * hidden : (g + 1) * hidden, :] = p[at : at + hidden, :]
+
     def row(self, k):
         return self.rows[k : k + 1, 0 : self.c]
 
@@ -259,7 +265,7 @@
 
         return [mean, spread, normed]
 
-    def project_pieces(self, load, stores):
+    def project_pieces(self, load, stores, normed_load=None):
         at = {}
         c = self.c
 
@@ -283,7 +289,14 @@
             begin()
             mean()
 
-        return [start, spread, normed], [dot for dot, _ in made] + [keep for _, keep in made]
+        rest = [dot for dot, _ in made] + [keep for _, keep in made]
+        if normed_load is None:
+            return [start, spread, normed], rest
+
+        def read():
+            at["normed"] = normed_load()
+
+        return [read] + rest
 
     def finish_pieces(self, load, attended, store):
         at = {}
@@ -332,15 +345,14 @@
         return [project, start, spread, normed], skewed(chains) + [end]
 
 
-def pipeline(chunks, first, second, third):
-    stages = []
-    for i in range(chunks):
-        norm, rest = first(i)
-        mlp_start, mlp_rest = third(i)
-        stages.append([norm, rest, second(i), mlp_start, mlp_rest])
+def pipeline(chunks, extra, *makers):
+    stages = [[stage for make in makers for stage in make(i)] for i in range(chunks)]
     depth = len(stages[0])
     for t in range(chunks + depth - 1):
-        weave(*[stages[t - d][d] for d in reversed(range(depth)) if 0 <= t - d < chunks])
+        threads = [stages[t - d][d] for d in reversed(range(depth)) if 0 <= t - d < chunks]
+        if t == 0:
+            threads.append(extra)
+        weave(*threads)
 
 
 def parity():
@@ -393,9 +405,9 @@
         return self.w.finish_pieces(load, attended, store)
 
 
-def block0_chunks(cols):
+def block0_chunks(cols, size=4):
     wins = cols // WIN
-    return [(n, 4) for n in range(0, wins, 4)] + [(wins, 2)]
+    return [(n, min(size, wins - n)) for n in range(0, wins, size)] + [(wins, 2)]
 
 
 def put_edges(x_ref, left_ref, right_ref, cols, base=0):
@@ -405,50 +417,80 @@
         )
 
 
+def norm_kernel(x_hbm, left_ref, right_ref, pack_ref, normed_ref, x_ref, rows_ref, sem, *, part, hidden):
+    cols = x_hbm.shape[1]
+    x_copy = pltpu.make_async_copy(x_hbm, x_ref.at[:, 0:cols], sem.at[0])
+    x_copy.start()
+    w = Weights([pack_ref], (None, None, None, None, rows_ref), x_ref.shape[2], part, hidden)
+    for k in range(2):
+        rows_ref[k : k + 1, :] = w.small(GAIN + k)[0]
+        rows_ref[2 + k : 3 + k, :] = w.small(SHIFTS + k)[0]
+    put_edges(x_ref, left_ref, right_ref, cols)
+    x_copy.wait()
+    tokens = WIN * WIN
+
+    def chunk(start, count):
+        at = {}
+
+        def begin():
+            block = x_ref[:, start * WIN : (start + count) * WIN, :].astype(F32)
+            at["x"] = jnp.concatenate(
+                [block[r, n * WIN : (n + 1) * WIN] for n in range(count) for r in range(WIN)], axis=0
+            )
+
+        def keep():
+            normed_ref[start * tokens : (start + count) * tokens] = at["normed"]
+
+        mean, spread, normed = w.norm_pieces(at, 0)
+        return [begin, mean, spread, normed, keep]
+
+    wins = cols // WIN + 2
+    for piece in offset([chunk(n, 2) for n in range(0, wins, 2)], 1):
+        piece()
+
+
 def regular_kernel(
-    x_hbm, labels_hbm, left_ref, right_ref, rel_ref, *refs, groups, own_heads, entries, part, hidden
+    x_hbm, labels_hbm, left_ref, right_ref, rel_ref, normed_ref, *refs,
+    groups, own_heads, entries, part, hidden,
 ):
     packs, refs = refs[:groups], refs[groups:]
-    (near_ref, rest_ref, ids_ref, bias_ref, x_ref, side_ref), refs = refs[:6], refs[6:]
+    (near_ref, rest_ref, ids_ref, bias_ref, side_ref), refs = refs[:5], refs[5:]
     (labels_ref, sems, qkv_ref, att_ref), scratch = refs[:4], refs[4:]
     side = 1 - parity()
     cols = x_hbm.shape[1]
-    x_copy = pltpu.make_async_copy(x_hbm, x_ref.at[:, 0:cols], sems.at[0])
-    labels_copy = pltpu.make_async_copy(labels_hbm, labels_ref, sems.at[1])
+    labels_copy = pltpu.make_async_copy(labels_hbm, labels_ref, sems.at[0])
     side_copy = pltpu.make_async_copy(
-        x_hbm.at[pl.ds(side * SHIFT, SHIFT)], side_ref.at[:, 0:cols], sems.at[2]
-    )
-    x_copy.start()
+        x_hbm.at[pl.ds(side * SHIFT, SHIFT)], side_ref.at[:, 0:cols], sems.at[1]
+    )
     labels_copy.start()
     side_copy.start()
-    c = x_ref.shape[2]
+    c = side_ref.shape[2]
     heads = own_heads * groups
     depth = c // heads
     tokens = WIN * WIN
     half = SHIFT * WIN
     scale = depth ** (-0.5) * LOG2E
     w = Weights(packs, scratch, c, part, hidden)
-    w.load()
     masks = head_masks(heads, depth, c)
     ones = jnp.concatenate(masks, axis=0)
-    bias_ref[...] = w.bias(own_heads, entries - 128, rel_ref[...])
+    w.load_rows()
+    w.load_qkv()
+
+    def pick_bias():
+        bias_ref[...] = w.bias(own_heads, entries - 128, rel_ref[...])
+
+    def put_ids():
+        ids_ref[...] = edge_ids(left_ref, right_ref, labels_ref[...])
+
     labels_copy.wait()
-    ids_ref[...] = edge_ids(left_ref, right_ref, labels_ref[...])
-    put_edges(x_ref, left_ref, right_ref, cols)
+    side_copy.wait()
     put_edges(side_ref, left_ref, right_ref, cols, side * SHIFT)
-    x_copy.wait()
-    side_copy.wait()
+    extra = [pick_bias, put_ids, w.load_rest]
     chunks = block0_chunks(cols)
     finish = Rows(w, side_ref, near_ref, cols)
 
     def first(i):
         start, count = chunks[i]
-
-        def load():
-            block = x_ref[:, start * WIN : (start + count) * WIN, :].astype(F32)
-            return jnp.concatenate(
-                [block[r, n * WIN : (n + 1) * WIN] for n in range(count) for r in range(WIN)], axis=0
-            )
 
         def keep(m):
             def store(value):
@@ -456,7 +498,9 @@
 
             return store
 
-        return w.project_pieces(load, [(0, scale, keep(0)), (1, None, keep(1)), (2, None, keep(2))])
+        rows = slice(start * tokens, (start + count) * tokens)
+        entries_of = [(0, scale, keep(0)), (1, None, keep(1)), (2, None, keep(2))]
+        return [w.project_pieces(None, entries_of, lambda: normed_ref[rows])]
 
     def second(i):
         start, count = chunks[i]
@@ -476,13 +520,13 @@
                 lambda: bias_ref[...], None, write, masks, ones,
             )
 
-        return skewed([window(n) for n in range(count)])
+        return [skewed([window(n) for n in range(count)])]
 
     def third(i):
         start, count = chunks[i]
         return finish.pieces(start, count, lambda: att_ref[i % 2, 0 : count * half])
 
-    pipeline(len(chunks), first, second, third)
+    pipeline(len(chunks), extra, first, second, third)
     for r in range(SHIFT):
         near_ref[r, cols + WIN :, :] = ids_ref[side * SHIFT + r]
 
@@ -497,7 +541,8 @@
     )
     x_copy.start()
     w = Weights(packs, scratch, x_ref.shape[2], part, hidden)
-    w.load(attention=False)
+    w.load_rows()
+    w.load_rest()
     put_edges(x_ref, left_ref, right_ref, cols, side * SHIFT)
     finish = Rows(w, x_ref, far_ref, cols)
     half = SHIFT * WIN
@@ -505,10 +550,10 @@
         far_ref[r, cols + WIN :, :] = ids_ref[side * SHIFT + r]
     x_copy.wait()
     threads = []
-    for start, count in block0_chunks(cols):
+    for start, count in block0_chunks(cols, 8):
         rows = slice(start * half, (start + count) * half)
         threads.append(sum(finish.pieces(start, count, lambda rows=rows: att_ref[rows]), []))
-    for piece in offset(threads, 4):
+    for piece in offset(threads, 3):
         piece()
 
 
@@ -532,22 +577,23 @@
     tokens = WIN * WIN
     scale = depth ** (-0.5) * LOG2E
     w = Weights(packs, scratch, c, part, hidden)
-    w.load()
+    w.load_rows()
     masks = head_masks(heads, depth, c)
     ones = jnp.concatenate(masks, axis=0)
 
-    rel = rel_ref[...]
-    rel = jnp.concatenate(
-        [
-            jnp.concatenate([rel[a + SHIFT : a + WIN], rel[a : a + SHIFT]], axis=0)
-            for a in range(0, tokens, WIN)
-        ],
-        axis=0,
-    )
-    lane = lax.broadcasted_iota(jnp.int32, rel.shape, 1)
-    rel = jnp.where(lane % WIN < SHIFT, pltpu.roll(rel, 128 - SHIFT, 1), pltpu.roll(rel, SHIFT, 1))
-    rel = jnp.where(side == 0, pltpu.roll(rel[half:], half, 1), rel[:half])
-    bias_ref[...] = w.bias(own_heads, entries - 128, rel)
+    def pick_bias():
+        rel = rel_ref[...]
+        rel = jnp.concatenate(
+            [
+                jnp.concatenate([rel[a + SHIFT : a + WIN], rel[a : a + SHIFT]], axis=0)
+                for a in range(0, tokens, WIN)
+            ],
+            axis=0,
+        )
+        lane = lax.broadcasted_iota(jnp.int32, rel.shape, 1)
+        rel = jnp.where(lane % WIN < SHIFT, pltpu.roll(rel, 128 - SHIFT, 1), pltpu.roll(rel, SHIFT, 1))
+        rel = jnp.where(side == 0, pltpu.roll(rel[half:], half, 1), rel[:half])
+        bias_ref[...] = w.bias(own_heads, entries - 128, rel)
 
     parts = []
     for dst, src in ((own_ref, own_in), (halo_ref, halo_in)):
@@ -613,7 +659,7 @@
 
             return window_pieces(read, lambda: bias_ref[...], allowed, write, masks, ones)
 
-        return skewed([window(j) for j in range(*chunks[i])])
+        return [skewed([window(j) for j in range(*chunks[i])])]
 
     def third(i):
         base, stop = chunks[i]
@@ -632,7 +678,7 @@
             lambda: gather(own_ref, i), lambda: att_ref[i % 2, 0 : (stop - base) * half], store
         )
 
-    pipeline(len(chunks), first, second, third)
+    pipeline(len(chunks), [w.load_qkv, pick_bias, w.load_rest], first, second, third)
     low = lax.broadcasted_iota(jnp.int32, (SHIFT, cols, c), 1) % WIN < SHIFT
     result = jnp.where(low, res_ref[:, 0:cols, :], res_ref[:, WIN : WIN + cols, :]).astype(BF)
     if near:
@@ -719,6 +765,13 @@
         return lax.ppermute(value, ("row", "ch"), pairs + [(j, i) for i, j in pairs])
 
     in_vmem = pl.BlockSpec(memory_space=pltpu.VMEM)
+    normed = call(
+        lambda *refs: norm_kernel(*refs, part=part, hidden=hidden),
+        jax.ShapeDtypeStruct((tokens * (tile_cols // WIN + 2), c), BF),
+        [wide, pltpu.VMEM((4, c), F32), pltpu.SemaphoreType.DMA((1,))],
+        in_hbm(image_tokens), left, right, own0,
+        in_specs=[pl.BlockSpec(memory_space=pltpu.HBM)] + [in_vmem] * 3,
+    )
     near, rest, ids = call(
         lambda *refs: regular_kernel(*refs, **sizes),
         (
@@ -727,12 +780,12 @@
             jax.ShapeDtypeStruct((WIN, WIN, 128), BF),
         ),
         [
-            bias_scratch, wide, half_wide,
-            pltpu.VMEM(labels.shape, jnp.int32), pltpu.SemaphoreType.DMA((3,)),
+            bias_scratch, half_wide,
+            pltpu.VMEM(labels.shape, jnp.int32), pltpu.SemaphoreType.DMA((2,)),
             pltpu.VMEM((2, 3, 4 * tokens, c), BF), pltpu.VMEM((2, 2 * tokens, c), BF),
         ] + weights_scratch,
-        in_hbm(image_tokens), in_hbm(labels), left, right, rel2, *packs0,
-        in_specs=[pl.BlockSpec(memory_space=pltpu.HBM)] * 2 + [in_vmem] * (3 + groups),
+        in_hbm(image_tokens), in_hbm(labels), left, right, rel2, normed, *packs0,
+        in_specs=[pl.BlockSpec(memory_space=pltpu.HBM)] * 2 + [in_vmem] * (4 + groups),
     )
     near_halo = swapped(near, 0)
     far = call(
@@ -743,7 +796,7 @@
         in_specs=[pl.BlockSpec(memory_space=pltpu.HBM)] + [in_vmem] * (4 + groups),
     )
     far_halo = swapped(far, 1)
-    chunks = even_split(tile_cols // WIN + 1, 7)
+    chunks = even_split(tile_cols // WIN + 1, 11)
     most = max(stop - base for base, stop in chunks) * SHIFT * WIN
     strip_wide = pltpu.VMEM((SHIFT, tile_cols + 2 * WIN, c), F32)
     scratch = [

time: 51.8 us -> 51.9 us (level)
    pallas_call x5 -> x6, Pallas kernels: 26 us -> 26.1 us  [call(): pl.pallas_call(kernel, out_shape=out_shapes, scratch_shapes=scratch, comp...]
  transfers between devices with their start and end apart: 6 -> 6, of which waited for: 2 -> 2; matrix products, arithmetic and copies ran while one was open for 0% -> 0% of each run, Pallas kernels for 19% -> 21%
where the time goes in v7:
time: 51.9 us; the launch traced here: 51.5 us
  Pallas kernels  26.1 us (50%)
  waiting for transfers between devices  13.2 us (25%)
  starting transfers between devices  12.1 us (23%)
    pallas_call x6, Pallas kernels, call(): pl.pallas_call(kernel, out_shape=out_shapes, scratch_shapes=scratch, comp...  26.1 us
    ppermute x2, waiting for transfers between devices, others(): found.append(lax.ppermute(found[-1], 'ch', swap))  10.1 us
    ppermute x1, starting transfers between devices, both_blocks(): left = lax.ppermute(right_edge, 'col', neighbours('col', 1))  3.95 us
    ppermute x2, starting transfers between devices, swapped(): lax.ppermute(value, ('row', 'ch'), pairs + [(j, i) for i, j in pairs])  3.51 us
    ppermute x1, waiting for transfers between devices, both_blocks(): right = lax.ppermute(left_edge, 'col', neighbours('col', -1))  3.14 us
    ppermute x2, starting transfers between devices, others(): found.append(lax.ppermute(found[-1], 'ch', swap))  2.72 us
    ppermute x1, starting transfers between devices, both_blocks(): right = lax.ppermute(left_edge, 'col', neighbours('col', -1))  1.92 us
  transfers between devices with their start and end apart: 6, of which 2 were waited for; matrix products, arithmetic and copies ran while one was open for 0% of the time, Pallas kernels for 21%

profile of v7, /device:TPU:9, one launch (start us, length us, event | category | flops | bytes accessed | tf_op | source)
XLA Modules:
  0.0 51.5 jit_solution(15015964307503378757)
XLA Ops:
  0.0 1.4 %shard_map.136 = (bf16[816,128]{1,0:T(8,128)(2,1)S(1)}, bf16[816,128]{1,0:T(8,128)(2,1)S(1)}, bf16[9,8,128]{2,1,0:T(8,128)(2,1)S(1)}, bf16[9,8,128]{2,1,0:T(8,128)(2,1)S(1)}, s32[64,128]{1,0:T(8,128)S(1)}) custom-call(bf16[8,256,128]{2,1,0:T(8,128)(2,1)} %refs_0_.7, s32[8,256]{1,0:T(8,128)} %refs_1_.3, s32[64,64]{1,0:T(8,128)} %refs_2_.1, ...), custom_call_target="tpu_custom_call" | custom-call | tf_op jit(solution)/shard_map/pallas_call | solution.py:693
  1.4 1.3 %collective-permute-start.2 = (bf16[816,128]{1,0:T(8,128)(2,1)S(1)}, bf16[816,128]{1,0:T(8,128)(2,1)S(1)}, u32[]{:S(2)}, u32[]{:S(2)}) collective-permute-start(bf16[816,128]{1,0:T(8,128)(2,1)S(1)} %get-tuple-element.16.refs_3_.refs_6_.refs_5_), channel_id=1, source_target_pairs={{0,1},{1,0},{2,3},{3,2},{4,5},{5,4},{6,7},{7,6},{8,9},{9,8},{10,11... | collective-permute-start | bytes 626696 | tf_op jit(solution)/shard_map/ppermute | solution.py:726
  2.7 3.9 %collective-permute-start = (bf16[9,8,128]{2,1,0:T(8,128)(2,1)S(1)}, bf16[9,8,128]{2,1,0:T(8,128)(2,1)S(1)}, u32[]{:S(2)}, u32[]{:S(2)}) collective-permute-start(bf16[9,8,128]{2,1,0:T(8,128)(2,1)S(1)} %get-tuple-element.13), channel_id=1, source_target_pairs={{0,2},{2,4},{4,6},{1,3},{3,5},{5,7},{8,10},{10,12},{12,14},{9,11},... | collective-permute-start | bytes 55304 | tf_op jit(solution)/shard_map/ppermute | solution.py:745
  6.7 1.9 %collective-permute-start.1 = (bf16[9,8,128]{2,1,0:T(8,128)(2,1)S(1)}, bf16[9,8,128]{2,1,0:T(8,128)(2,1)S(1)}, u32[]{:S(2)}, u32[]{:S(2)}) collective-permute-start(bf16[9,8,128]{2,1,0:T(8,128)(2,1)S(1)} %get-tuple-element.14), channel_id=1, source_target_pairs={{2,0},{4,2},{6,4},{3,1},{5,3},{7,5},{10,8},{12,10},{14,12},{11,9},... | collective-permute-start | bytes 55304 | tf_op jit(solution)/shard_map/ppermute | solution.py:746
  8.6 0.0 collective-permute-done.refs_1_.refs_2_
  8.6 3.1 %collective-permute-done.1.refs_2_.refs_3_ = bf16[9,8,128]{2,1,0:T(8,128)(2,1)S(1)} collective-permute-done((bf16[9,8,128]{2,1,0:T(8,128)(2,1)S(1)}, bf16[9,8,128]{2,1,0:T(8,128)(2,1)S(1)}, u32[]{:S(2)}, u32[]{:S(2)}) %collective-permute-start.1) | collective-permute-done | bytes 18464 | tf_op jit(solution)/shard_map/ppermute | solution.py:746
  11.8 2.4 %shard_map.137.refs_5_ = bf16[2176,128]{1,0:T(8,128)(2,1)S(1)} custom-call(bf16[8,256,128]{2,1,0:T(8,128)(2,1)} %refs_0_.7, bf16[9,8,128]{2,1,0:T(8,128)(2,1)S(1)} %collective-permute-done.refs_1_.refs_2_, bf16[9,8,128]{2,1,0:T(8,128)(2,1)S(1)} %collective-permute-done.1.refs_2_.refs_3_, bf16[816,128]{1,0:T(8,128)(2,1)S(1)} %get-tuple-element.16.refs_3_.refs_6_.refs_5_), custom_call_target="tpu_custom_call" | custom-call | tf_op jit(solution)/shard_map/pallas_call | solution.py:693
  14.2 0.0 collective-permute-done.2.refs_7_.refs_6_
  14.2 7.0 %shard_map.138 = (bf16[4,272,128]{2,1,0:T(8,128)(2,1)S(1)}, bf16[1088,128]{1,0:T(8,128)(2,1)S(1)}, bf16[8,8,128]{2,1,0:T(8,128)(2,1)S(1)}) custom-call(bf16[8,256,128]{2,1,0:T(8,128)(2,1)} %refs_0_.7, s32[8,256]{1,0:T(8,128)} %refs_1_.3, bf16[9,8,128]{2,1,0:T(8,128)(2,1)S(1)} %collective-permute-done.refs_1_.refs_2_, ...), custom_call_target="tpu_custom_call" | custom-call | tf_op jit(solution)/shard_map/pallas_call | solution.py:693
  21.2 0.3 collective-permute-start.5
  21.5 2.6 %shard_map.139.refs_0_ = bf16[4,272,128]{2,1,0:T(8,128)(2,1)S(1)} custom-call(bf16[8,256,128]{2,1,0:T(8,128)(2,1)} %refs_0_.7, bf16[9,8,128]{2,1,0:T(8,128)(2,1)S(1)} %collective-permute-done.refs_1_.refs_2_, bf16[9,8,128]{2,1,0:T(8,128)(2,1)S(1)} %collective-permute-done.1.refs_2_.refs_3_, bf16[1088,128]{1,0:T(8,128)(2,1)S(1)} %get-tuple-element.17.refs_3_, ...), custom_call_target="tpu_custom_call" | custom-call | tf_op jit(solution)/shard_map/pallas_call | solution.py:693
  24.2 3.2 %collective-permute-start.3 = (bf16[4,272,128]{2,1,0:T(8,128)(2,1)S(1)}, bf16[4,272,128]{2,1,0:T(8,128)(2,1)S(1)}, u32[]{:S(2)}, u32[]{:S(2)}) collective-permute-start(bf16[4,272,128]{2,1,0:T(8,128)(2,1)S(1)} %shard_map.139.refs_0_), channel_id=1, source_target_pairs={{1,8},{9,16},{17,24},{8,1},{16,9},{24,17},{3,10},{11,18},{19,26},{... | collective-permute-start | bytes 835592 | tf_op jit(solution)/shard_map/ppermute | solution.py:765
  27.4 1.4 %collective-permute-start.4 = (bf16[816,128]{1,0:T(8,128)(2,1)S(1)}, bf16[816,128]{1,0:T(8,128)(2,1)S(1)}, u32[]{:S(2)}, u32[]{:S(2)}) collective-permute-start(bf16[816,128]{1,0:T(8,128)(2,1)S(1)} %get-tuple-element.19.refs_3_), channel_id=1, source_target_pairs={{0,1},{1,0},{2,3},{3,2},{4,5},{5,4},{6,7},{7,6},{8,9},{9,8},{10,11... | collective-permute-start | bytes 626696 | tf_op jit(solution)/shard_map/ppermute | solution.py:726
  28.8 10.0 %collective-permute-done.4.refs_4_ = bf16[816,128]{1,0:T(8,128)(2,1)S(1)} collective-permute-done((bf16[816,128]{1,0:T(8,128)(2,1)S(1)}, bf16[816,128]{1,0:T(8,128)(2,1)S(1)}, u32[]{:S(2)}, u32[]{:S(2)}) %collective-permute-start.4) | collective-permute-done | bytes 208928 | tf_op jit(solution)/shard_map/ppermute | solution.py:726
  38.9 0.0 collective-permute-done.5.refs_1_
  38.9 5.9 %shard_map.140.refs_5_ = bf16[4,256,128]{2,1,0:T(8,128)(2,1)S(1)} custom-call(bf16[4,272,128]{2,1,0:T(8,128)(2,1)S(1)} %get-tuple-element.20.refs_0_, bf16[4,272,128]{2,1,0:T(8,128)(2,1)S(1)} %collective-permute-done.5.refs_1_, s32[64,128]{1,0:T(8,128)S(1)} %get-tuple-element.15.refs_4_.refs_2_, bf16[816,128]{1,0:T(8,128)(2,1)S(1)} %get-tuple-element.19.refs_3_, ...), custom_call_target="tpu_custom_call" | custom-call | tf_op jit(solution)/shard_map/pallas_call | solution.py:693
  44.8 0.0 collective-permute-done.3.refs_1_
  44.8 6.7 %shard_map.141 = bf16[8,256,128]{2,1,0:T(8,128)(2,1)} custom-call(bf16[4,272,128]{2,1,0:T(8,128)(2,1)S(1)} %shard_map.139.refs_0_, bf16[4,272,128]{2,1,0:T(8,128)(2,1)S(1)} %collective-permute-done.3.refs_1_, s32[64,128]{1,0:T(8,128)S(1)} %get-tuple-element.15.refs_4_.refs_2_, bf16[816,128]{1,0:T(8,128)(2,1)S(1)} %get-tuple-element.19.refs_3_, ...), custom_call_target="tpu_custom_call" | custom-call | tf_op jit(solution)/shard_map/pallas_call | solution.py:693
Async XLA Ops:
  1.4 12.8 %collective-permute-start.2 = (bf16[816,128]{1,0:T(8,128)(2,1)S(1)}, bf16[816,128]{1,0:T(8,128)(2,1)S(1)}, u32[]{:S(2)}, u32[]{:S(2)}) collective-permute-start(bf16[816,128]{1,0:T(8,128)(2,1)S(1)} %get-tuple-element.16.refs_3_.refs_6_.refs_5_), channel_id=1, source_target_pairs={{0,1},{1,0},{2,3},{3,2},{4,5},{5,4},{6,7},{7,6},{8,9},{9,8},{10,11... | collective-permute-start | bytes 626696 | tf_op jit(solution)/shard_map/ppermute | solution.py:726
  2.7 5.9 %collective-permute-start = (bf16[9,8,128]{2,1,0:T(8,128)(2,1)S(1)}, bf16[9,8,128]{2,1,0:T(8,128)(2,1)S(1)}, u32[]{:S(2)}, u32[]{:S(2)}) collective-permute-start(bf16[9,8,128]{2,1,0:T(8,128)(2,1)S(1)} %get-tuple-element.13), channel_id=1, source_target_pairs={{0,2},{2,4},{4,6},{1,3},{3,5},{5,7},{8,10},{10,12},{12,14},{9,11},... | collective-permute-start | bytes 55304 | tf_op jit(solution)/shard_map/ppermute | solution.py:745
  6.7 5.1 %collective-permute-start.1 = (bf16[9,8,128]{2,1,0:T(8,128)(2,1)S(1)}, bf16[9,8,128]{2,1,0:T(8,128)(2,1)S(1)}, u32[]{:S(2)}, u32[]{:S(2)}) collective-permute-start(bf16[9,8,128]{2,1,0:T(8,128)(2,1)S(1)} %get-tuple-element.14), channel_id=1, source_target_pairs={{2,0},{4,2},{6,4},{3,1},{5,3},{7,5},{10,8},{12,10},{14,12},{11,9},... | collective-permute-start | bytes 55304 | tf_op jit(solution)/shard_map/ppermute | solution.py:746
  21.2 17.6 %collective-permute-start.5 = (bf16[4,272,128]{2,1,0:T(8,128)(2,1)S(1)}, bf16[4,272,128]{2,1,0:T(8,128)(2,1)S(1)}, u32[]{:S(2)}, u32[]{:S(2)}) collective-permute-start(bf16[4,272,128]{2,1,0:T(8,128)(2,1)S(1)} %get-tuple-element.20.refs_0_), channel_id=1, source_target_pairs={{0,1},{8,9},{16,17},{24,25},{1,0},{9,8},{17,16},{25,24},{2,3},{10,... | collective-permute-start | bytes 835592 | tf_op jit(solution)/shard_map/ppermute | solution.py:765
  24.2 20.6 %collective-permute-start.3 = (bf16[4,272,128]{2,1,0:T(8,128)(2,1)S(1)}, bf16[4,272,128]{2,1,0:T(8,128)(2,1)S(1)}, u32[]{:S(2)}, u32[]{:S(2)}) collective-permute-start(bf16[4,272,128]{2,1,0:T(8,128)(2,1)S(1)} %shard_map.139.refs_0_), channel_id=1, source_target_pairs={{1,8},{9,16},{17,24},{8,1},{16,9},{24,17},{3,10},{11,18},{19,26},{... | collective-permute-start | bytes 835592 | tf_op jit(solution)/shard_map/ppermute | solution.py:765
  27.4 11.5 %collective-permute-start.4 = (bf16[816,128]{1,0:T(8,128)(2,1)S(1)}, bf16[816,128]{1,0:T(8,128)(2,1)S(1)}, u32[]{:S(2)}, u32[]{:S(2)}) collective-permute-start(bf16[816,128]{1,0:T(8,128)(2,1)S(1)} %get-tuple-element.19.refs_3_), channel_id=1, source_target_pairs={{0,1},{1,0},{2,3},{3,2},{4,5},{5,4},{6,7},{7,6},{8,9},{9,8},{10,11... | collective-permute-start | bytes 626696 | tf_op jit(solution)/shard_map/ppermute | solution.py:726

commit v8 on v7

--- a/solution.py
+++ b/solution.py
@@ -417,15 +417,14 @@
         )
 
 
-def norm_kernel(x_hbm, left_ref, right_ref, pack_ref, normed_ref, x_ref, rows_ref, sem, *, part, hidden):
+def norm_kernel(x_hbm, pack_ref, normed_ref, x_ref, rows_ref, sem, *, part, hidden):
     cols = x_hbm.shape[1]
-    x_copy = pltpu.make_async_copy(x_hbm, x_ref.at[:, 0:cols], sem.at[0])
+    x_copy = pltpu.make_async_copy(x_hbm, x_ref, sem.at[0])
     x_copy.start()
     w = Weights([pack_ref], (None, None, None, None, rows_ref), x_ref.shape[2], part, hidden)
     for k in range(2):
         rows_ref[k : k + 1, :] = w.small(GAIN + k)[0]
         rows_ref[2 + k : 3 + k, :] = w.small(SHIFTS + k)[0]
-    put_edges(x_ref, left_ref, right_ref, cols)
     x_copy.wait()
     tokens = WIN * WIN
 
@@ -444,8 +443,8 @@
         mean, spread, normed = w.norm_pieces(at, 0)
         return [begin, mean, spread, normed, keep]
 
-    wins = cols // WIN + 2
-    for piece in offset([chunk(n, 2) for n in range(0, wins, 2)], 1):
+    wins = cols // WIN
+    for piece in offset([chunk(n, min(4, wins - n)) for n in range(0, wins, 4)], 1):
         piece()
 
 
@@ -500,7 +499,16 @@
 
         rows = slice(start * tokens, (start + count) * tokens)
         entries_of = [(0, scale, keep(0)), (1, None, keep(1)), (2, None, keep(2))]
-        return [w.project_pieces(None, entries_of, lambda: normed_ref[rows])]
+        if start * WIN < cols:
+            return [w.project_pieces(None, entries_of, lambda: normed_ref[rows])]
+
+        def edges():
+            return jnp.concatenate(
+                [e[0:WIN].astype(F32).reshape(tokens, c) for e in (left_ref, right_ref)], axis=0
+            )
+
+        norm, rest = w.project_pieces(edges, entries_of)
+        return [norm + rest]
 
     def second(i):
         start, count = chunks[i]
@@ -564,11 +572,17 @@
 
 def shifted_kernel(own_in, halo_in, rel_ref, *refs, chunks, near, groups, own_heads, entries, part, hidden):
     packs, refs = refs[:groups], refs[groups:]
+    side = 1 - parity() if near else parity()
+    copies = []
     if not near:
-        done_ref, refs = refs[0], refs[1:]
+        done_ref, out_hbm, out_ref, sems = refs[0], refs[1], refs[2], refs[3]
+        refs = refs[2:3] + refs[4:]
+        copies.append(
+            pltpu.make_async_copy(done_ref, out_hbm.at[pl.ds((1 - side) * SHIFT, SHIFT)], sems.at[0])
+        )
+        copies[0].start()
     (out_ref, bias_ref, own_ref, halo_ref, res_ref), refs = refs[:5], refs[5:]
     (q_ref, kv_ref, att_ref), scratch = refs[:3], refs[3:]
-    side = 1 - parity() if near else parity()
     c = own_in.shape[2]
     cols = out_ref.shape[1]
     heads = own_heads * groups
@@ -673,23 +687,32 @@
                     ],
                     axis=0,
                 )
+            begin = (base - 1) // 2 * 2 * WIN if i else 0
+            end = (stop - 1) // 2 * 2 * WIN if i + 1 < len(chunks) else cols
+            low = lax.broadcasted_iota(jnp.int32, (SHIFT, end - begin, c), 1) % WIN < SHIFT
+            out_ref[:, begin:end, :] = jnp.where(
+                low, res_ref[:, begin:end, :], res_ref[:, begin + WIN : end + WIN, :]
+            ).astype(BF)
+            if not near:
+                copies.append(
+                    pltpu.make_async_copy(
+                        out_ref.at[:, begin:end],
+                        out_hbm.at[pl.ds(side * SHIFT, SHIFT), begin:end],
+                        sems.at[1 + i],
+                    )
+                )
+                copies[-1].start()
 
         return w.finish_pieces(
             lambda: gather(own_ref, i), lambda: att_ref[i % 2, 0 : (stop - base) * half], store
         )
 
     pipeline(len(chunks), [w.load_qkv, pick_bias, w.load_rest], first, second, third)
-    low = lax.broadcasted_iota(jnp.int32, (SHIFT, cols, c), 1) % WIN < SHIFT
-    result = jnp.where(low, res_ref[:, 0:cols, :], res_ref[:, WIN : WIN + cols, :]).astype(BF)
-    if near:
-        out_ref[...] = result
-    else:
-        out_ref[pl.ds(side * SHIFT, SHIFT)] = result
-        out_ref[pl.ds((1 - side) * SHIFT, SHIFT)] = done_ref[...]
-
-
-def call(kernel, out_shapes, scratch, *args, in_specs=None):
-    specs = {} if in_specs is None else {"in_specs": in_specs}
+    for copy in copies:
+        copy.wait()
+
+
+def call(kernel, out_shapes, scratch, *args, **specs):
     return pl.pallas_call(
         kernel,
         out_shape=out_shapes,
@@ -756,7 +779,6 @@
     ]
     strip = jax.ShapeDtypeStruct((SHIFT, tile_cols + 2 * WIN, c), BF)
     bias_scratch = pltpu.VMEM((tokens, own_heads * groups * tokens), F32)
-    wide = pltpu.VMEM((WIN, tile_cols + 2 * WIN, c), BF)
     half_wide = pltpu.VMEM((SHIFT, tile_cols + 2 * WIN, c), BF)
     bands = lax.axis_size(("row", "ch"))
 
@@ -767,10 +789,13 @@
     in_vmem = pl.BlockSpec(memory_space=pltpu.VMEM)
     normed = call(
         lambda *refs: norm_kernel(*refs, part=part, hidden=hidden),
-        jax.ShapeDtypeStruct((tokens * (tile_cols // WIN + 2), c), BF),
-        [wide, pltpu.VMEM((4, c), F32), pltpu.SemaphoreType.DMA((1,))],
-        in_hbm(image_tokens), left, right, own0,
-        in_specs=[pl.BlockSpec(memory_space=pltpu.HBM)] + [in_vmem] * 3,
+        jax.ShapeDtypeStruct((tokens * (tile_cols // WIN), c), BF),
+        [
+            pltpu.VMEM(image_tokens.shape, BF), pltpu.VMEM((4, c), F32),
+            pltpu.SemaphoreType.DMA((1,)),
+        ],
+        in_hbm(image_tokens), own0,
+        in_specs=[pl.BlockSpec(memory_space=pltpu.HBM), in_vmem],
     )
     near, rest, ids = call(
         lambda *refs: regular_kernel(*refs, **sizes),
@@ -812,7 +837,9 @@
     return call(
         lambda *refs: shifted_kernel(*refs, chunks=chunks, near=False, **sizes),
         jax.ShapeDtypeStruct(image_tokens.shape, BF),
-        scratch, far, far_halo, rel2, *packs1, near_out,
+        [pltpu.VMEM((SHIFT, tile_cols, c), BF), pltpu.SemaphoreType.DMA((1 + len(chunks),))] + scratch,
+        far, far_halo, rel2, *packs1, near_out,
+        out_specs=pl.BlockSpec(memory_space=pltpu.HBM),
     )
 
 

time: 51.9 us -> 49.6 us (0.956)
  waiting for transfers between devices: 13.2 us -> 11.4 us
    ppermute x1, waiting for transfers between devices: 3.14 us -> 1.14 us  [both_blocks(): right = lax.ppermute(left_edge, 'col', neighbours('col', -1))]
    pallas_call x6, Pallas kernels: 26.1 us -> 25.6 us  [call(): pl.pallas_call(kernel, out_shape=out_shapes, scratch_shapes=scratch, comp...]
where the time goes in v8:
time: 49.6 us; the launch traced here: 49.3 us
  Pallas kernels  25.6 us (52%)
  starting transfers between devices  12.1 us (24%)
  waiting for transfers between devices  11.4 us (23%)
    pallas_call x6, Pallas kernels, call(): pl.pallas_call(kernel, out_shape=out_shapes, scratch_shapes=scratch, comp...  25.6 us
    ppermute x2, waiting for transfers between devices, others(): found.append(lax.ppermute(found[-1], 'ch', swap))  10.3 us
    ppermute x1, starting transfers between devices, both_blocks(): left = lax.ppermute(right_edge, 'col', neighbours('col', 1))  3.95 us
    ppermute x2, starting transfers between devices, swapped(): lax.ppermute(value, ('row', 'ch'), pairs + [(j, i) for i, j in pairs])  3.5 us
    ppermute x2, starting transfers between devices, others(): found.append(lax.ppermute(found[-1], 'ch', swap))  2.72 us
    ppermute x1, starting transfers between devices, both_blocks(): right = lax.ppermute(left_edge, 'col', neighbours('col', -1))  1.92 us
    ppermute x1, waiting for transfers between devices, both_blocks(): right = lax.ppermute(left_edge, 'col', neighbours('col', -1))  1.14 us
  transfers between devices with their start and end apart: 6, of which 2 were waited for; matrix products, arithmetic and copies ran while one was open for 0% of the time, Pallas kernels for 21%

profile of v8, /device:TPU:9, one launch (start us, length us, event | category | flops | bytes accessed | tf_op | source)
XLA Modules:
  0.0 49.3 jit_solution(2818391788673515384)
XLA Ops:
  0.0 1.4 %shard_map.136 = (bf16[816,128]{1,0:T(8,128)(2,1)S(1)}, bf16[816,128]{1,0:T(8,128)(2,1)S(1)}, bf16[9,8,128]{2,1,0:T(8,128)(2,1)S(1)}, bf16[9,8,128]{2,1,0:T(8,128)(2,1)S(1)}, s32[64,128]{1,0:T(8,128)S(1)}) custom-call(bf16[8,256,128]{2,1,0:T(8,128)(2,1)} %refs_0_.7, s32[8,256]{1,0:T(8,128)} %refs_1_.3, s32[64,64]{1,0:T(8,128)} %refs_2_.1, ...), custom_call_target="tpu_custom_call" | custom-call | tf_op jit(solution)/shard_map/pallas_call | solution.py:716
  1.4 1.3 %collective-permute-start.2 = (bf16[816,128]{1,0:T(8,128)(2,1)S(1)}, bf16[816,128]{1,0:T(8,128)(2,1)S(1)}, u32[]{:S(2)}, u32[]{:S(2)}) collective-permute-start(bf16[816,128]{1,0:T(8,128)(2,1)S(1)} %get-tuple-element.16.refs_1_.refs_6_.refs_5_), channel_id=1, source_target_pairs={{0,1},{1,0},{2,3},{3,2},{4,5},{5,4},{6,7},{7,6},{8,9},{9,8},{10,11... | collective-permute-start | bytes 626696 | tf_op jit(solution)/shard_map/ppermute | solution.py:749
  2.7 3.9 %collective-permute-start = (bf16[9,8,128]{2,1,0:T(8,128)(2,1)S(1)}, bf16[9,8,128]{2,1,0:T(8,128)(2,1)S(1)}, u32[]{:S(2)}, u32[]{:S(2)}) collective-permute-start(bf16[9,8,128]{2,1,0:T(8,128)(2,1)S(1)} %get-tuple-element.13), channel_id=1, source_target_pairs={{0,2},{2,4},{4,6},{1,3},{3,5},{5,7},{8,10},{10,12},{12,14},{9,11},... | collective-permute-start | bytes 55304 | tf_op jit(solution)/shard_map/ppermute | solution.py:768
  6.7 1.9 %collective-permute-start.1 = (bf16[9,8,128]{2,1,0:T(8,128)(2,1)S(1)}, bf16[9,8,128]{2,1,0:T(8,128)(2,1)S(1)}, u32[]{:S(2)}, u32[]{:S(2)}) collective-permute-start(bf16[9,8,128]{2,1,0:T(8,128)(2,1)S(1)} %get-tuple-element.14), channel_id=1, source_target_pairs={{2,0},{4,2},{6,4},{3,1},{5,3},{7,5},{10,8},{12,10},{14,12},{11,9},... | collective-permute-start | bytes 55304 | tf_op jit(solution)/shard_map/ppermute | solution.py:769
  8.6 2.0 %shard_map.137.refs_5_ = bf16[2048,128]{1,0:T(8,128)(2,1)S(1)} custom-call(bf16[8,256,128]{2,1,0:T(8,128)(2,1)} %refs_0_.7, bf16[816,128]{1,0:T(8,128)(2,1)S(1)} %get-tuple-element.16.refs_1_.refs_6_.refs_5_), custom_call_target="tpu_custom_call" | custom-call | tf_op jit(solution)/shard_map/pallas_call | solution.py:716
  10.6 0.0 collective-permute-done.refs_2_.refs_1_
  10.6 1.1 %collective-permute-done.1.refs_3_.refs_2_ = bf16[9,8,128]{2,1,0:T(8,128)(2,1)S(1)} collective-permute-done((bf16[9,8,128]{2,1,0:T(8,128)(2,1)S(1)}, bf16[9,8,128]{2,1,0:T(8,128)(2,1)S(1)}, u32[]{:S(2)}, u32[]{:S(2)}) %collective-permute-start.1) | collective-permute-done | bytes 18464 | tf_op jit(solution)/shard_map/ppermute | solution.py:769
  11.8 0.0 collective-permute-done.2.refs_7_.refs_6_
  11.8 7.0 %shard_map.138 = (bf16[4,272,128]{2,1,0:T(8,128)(2,1)S(1)}, bf16[1088,128]{1,0:T(8,128)(2,1)S(1)}, bf16[8,8,128]{2,1,0:T(8,128)(2,1)S(1)}) custom-call(bf16[8,256,128]{2,1,0:T(8,128)(2,1)} %refs_0_.7, s32[8,256]{1,0:T(8,128)} %refs_1_.3, bf16[9,8,128]{2,1,0:T(8,128)(2,1)S(1)} %collective-permute-done.refs_2_.refs_1_, ...), custom_call_target="tpu_custom_call" | custom-call | tf_op jit(solution)/shard_map/pallas_call | solution.py:716
  18.8 0.3 collective-permute-start.5
  19.1 2.6 %shard_map.139.refs_0_ = bf16[4,272,128]{2,1,0:T(8,128)(2,1)S(1)} custom-call(bf16[8,256,128]{2,1,0:T(8,128)(2,1)} %refs_0_.7, bf16[9,8,128]{2,1,0:T(8,128)(2,1)S(1)} %collective-permute-done.refs_2_.refs_1_, bf16[9,8,128]{2,1,0:T(8,128)(2,1)S(1)} %collective-permute-done.1.refs_3_.refs_2_, bf16[1088,128]{1,0:T(8,128)(2,1)S(1)} %get-tuple-element.17.refs_3_, ...), custom_call_target="tpu_custom_call" | custom-call | tf_op jit(solution)/shard_map/pallas_call | solution.py:716
  21.7 3.2 %collective-permute-start.3 = (bf16[4,272,128]{2,1,0:T(8,128)(2,1)S(1)}, bf16[4,272,128]{2,1,0:T(8,128)(2,1)S(1)}, u32[]{:S(2)}, u32[]{:S(2)}) collective-permute-start(bf16[4,272,128]{2,1,0:T(8,128)(2,1)S(1)} %shard_map.139.refs_0_), channel_id=1, source_target_pairs={{1,8},{9,16},{17,24},{8,1},{16,9},{24,17},{3,10},{11,18},{19,26},{... | collective-permute-start | bytes 835592 | tf_op jit(solution)/shard_map/ppermute | solution.py:787
  24.9 1.4 %collective-permute-start.4 = (bf16[816,128]{1,0:T(8,128)(2,1)S(1)}, bf16[816,128]{1,0:T(8,128)(2,1)S(1)}, u32[]{:S(2)}, u32[]{:S(2)}) collective-permute-start(bf16[816,128]{1,0:T(8,128)(2,1)S(1)} %get-tuple-element.19.refs_3_), channel_id=1, source_target_pairs={{0,1},{1,0},{2,3},{3,2},{4,5},{5,4},{6,7},{7,6},{8,9},{9,8},{10,11... | collective-permute-start | bytes 626696 | tf_op jit(solution)/shard_map/ppermute | solution.py:749
  26.3 10.3 %collective-permute-done.4.refs_4_ = bf16[816,128]{1,0:T(8,128)(2,1)S(1)} collective-permute-done((bf16[816,128]{1,0:T(8,128)(2,1)S(1)}, bf16[816,128]{1,0:T(8,128)(2,1)S(1)}, u32[]{:S(2)}, u32[]{:S(2)}) %collective-permute-start.4) | collective-permute-done | bytes 208928 | tf_op jit(solution)/shard_map/ppermute | solution.py:749
  36.6 0.0 collective-permute-done.5.refs_1_
  36.6 5.9 %shard_map.140.refs_5_ = bf16[4,256,128]{2,1,0:T(8,128)(2,1)S(1)} custom-call(bf16[4,272,128]{2,1,0:T(8,128)(2,1)S(1)} %get-tuple-element.20.refs_0_, bf16[4,272,128]{2,1,0:T(8,128)(2,1)S(1)} %collective-permute-done.5.refs_1_, s32[64,128]{1,0:T(8,128)S(1)} %get-tuple-element.15.refs_4_.refs_2_, bf16[816,128]{1,0:T(8,128)(2,1)S(1)} %get-tuple-element.19.refs_3_, ...), custom_call_target="tpu_custom_call" | custom-call | tf_op jit(solution)/shard_map/pallas_call | solution.py:716
  42.5 0.0 collective-permute-done.3.refs_1_
  42.5 6.6 %shard_map.141 = bf16[8,256,128]{2,1,0:T(8,128)(2,1)} custom-call(bf16[4,272,128]{2,1,0:T(8,128)(2,1)S(1)} %shard_map.139.refs_0_, bf16[4,272,128]{2,1,0:T(8,128)(2,1)S(1)} %collective-permute-done.3.refs_1_, s32[64,128]{1,0:T(8,128)S(1)} %get-tuple-element.15.refs_4_.refs_2_, bf16[816,128]{1,0:T(8,128)(2,1)S(1)} %get-tuple-element.19.refs_3_, ...), custom_call_target="tpu_custom_call" | custom-call | tf_op jit(solution)/shard_map/pallas_call | solution.py:716
Async XLA Ops:
  1.4 10.3 %collective-permute-start.2 = (bf16[816,128]{1,0:T(8,128)(2,1)S(1)}, bf16[816,128]{1,0:T(8,128)(2,1)S(1)}, u32[]{:S(2)}, u32[]{:S(2)}) collective-permute-start(bf16[816,128]{1,0:T(8,128)(2,1)S(1)} %get-tuple-element.16.refs_1_.refs_6_.refs_5_), channel_id=1, source_target_pairs={{0,1},{1,0},{2,3},{3,2},{4,5},{5,4},{6,7},{7,6},{8,9},{9,8},{10,11... | collective-permute-start | bytes 626696 | tf_op jit(solution)/shard_map/ppermute | solution.py:749
  2.7 7.9 %collective-permute-start = (bf16[9,8,128]{2,1,0:T(8,128)(2,1)S(1)}, bf16[9,8,128]{2,1,0:T(8,128)(2,1)S(1)}, u32[]{:S(2)}, u32[]{:S(2)}) collective-permute-start(bf16[9,8,128]{2,1,0:T(8,128)(2,1)S(1)} %get-tuple-element.13), channel_id=1, source_target_pairs={{0,2},{2,4},{4,6},{1,3},{3,5},{5,7},{8,10},{10,12},{12,14},{9,11},... | collective-permute-start | bytes 55304 | tf_op jit(solution)/shard_map/ppermute | solution.py:768
  6.7 5.1 %collective-permute-start.1 = (bf16[9,8,128]{2,1,0:T(8,128)(2,1)S(1)}, bf16[9,8,128]{2,1,0:T(8,128)(2,1)S(1)}, u32[]{:S(2)}, u32[]{:S(2)}) collective-permute-start(bf16[9,8,128]{2,1,0:T(8,128)(2,1)S(1)} %get-tuple-element.14), channel_id=1, source_target_pairs={{2,0},{4,2},{6,4},{3,1},{5,3},{7,5},{10,8},{12,10},{14,12},{11,9},... | collective-permute-start | bytes 55304 | tf_op jit(solution)/shard_map/ppermute | solution.py:769
  18.8 17.8 %collective-permute-start.5 = (bf16[4,272,128]{2,1,0:T(8,128)(2,1)S(1)}, bf16[4,272,128]{2,1,0:T(8,128)(2,1)S(1)}, u32[]{:S(2)}, u32[]{:S(2)}) collective-permute-start(bf16[4,272,128]{2,1,0:T(8,128)(2,1)S(1)} %get-tuple-element.20.refs_0_), channel_id=1, source_target_pairs={{0,1},{8,9},{16,17},{24,25},{1,0},{9,8},{17,16},{25,24},{2,3},{10,... | collective-permute-start | bytes 835592 | tf_op jit(solution)/shard_map/ppermute | solution.py:787
  21.7 20.8 %collective-permute-start.3 = (bf16[4,272,128]{2,1,0:T(8,128)(2,1)S(1)}, bf16[4,272,128]{2,1,0:T(8,128)(2,1)S(1)}, u32[]{:S(2)}, u32[]{:S(2)}) collective-permute-start(bf16[4,272,128]{2,1,0:T(8,128)(2,1)S(1)} %shard_map.139.refs_0_), channel_id=1, source_target_pairs={{1,8},{9,16},{17,24},{8,1},{16,9},{24,17},{3,10},{11,18},{19,26},{... | collective-permute-start | bytes 835592 | tf_op jit(solution)/shard_map/ppermute | solution.py:787
  24.9 11.7 %collective-permute-start.4 = (bf16[816,128]{1,0:T(8,128)(2,1)S(1)}, bf16[816,128]{1,0:T(8,128)(2,1)S(1)}, u32[]{:S(2)}, u32[]{:S(2)}) collective-permute-start(bf16[816,128]{1,0:T(8,128)(2,1)S(1)} %get-tuple-element.19.refs_3_), channel_id=1, source_target_pairs={{0,1},{1,0},{2,3},{3,2},{4,5},{5,4},{6,7},{7,6},{8,9},{9,8},{10,11... | collective-permute-start | bytes 626696 | tf_op jit(solution)/shard_map/ppermute | solution.py:749

commit v9 on v8

--- a/solution.py
+++ b/solution.py
@@ -87,6 +87,14 @@
         for t in range(max(len(thread) + n * lag for n, thread in enumerate(threads)))
         for n, thread in enumerate(threads)
         if 0 <= t - n * lag < len(thread)
+    ]
+
+
+def grouped(pipelines, size):
+    groups = [pipelines[n : n + size] for n in range(0, len(pipelines), size)]
+    return [
+        [lambda k=k, group=group: [p[k]() for p in group] for k in range(len(group[0]))]
+        for group in groups
     ]
 
 
@@ -350,8 +358,7 @@
     depth = len(stages[0])
     for t in range(chunks + depth - 1):
         threads = [stages[t - d][d] for d in reversed(range(depth)) if 0 <= t - d < chunks]
-        if t == 0:
-            threads.append(extra)
+        threads.append(extra.get(t, []))
         weave(*threads)
 
 
@@ -405,7 +412,7 @@
         return self.w.finish_pieces(load, attended, store)
 
 
-def block0_chunks(cols, size=4):
+def block0_chunks(cols, size=16):
     wins = cols // WIN
     return [(n, min(size, wins - n)) for n in range(0, wins, size)] + [(wins, 2)]
 
@@ -528,20 +535,23 @@
                 lambda: bias_ref[...], None, write, masks, ones,
             )
 
-        return [skewed([window(n) for n in range(count)])]
+        return [skewed(grouped([window(n) for n in range(count)], 99))]
 
     def third(i):
         start, count = chunks[i]
         return finish.pieces(start, count, lambda: att_ref[i % 2, 0 : count * half])
 
-    pipeline(len(chunks), extra, first, second, third)
+    pipeline(len(chunks), {0: extra}, first, second, third)
     for r in range(SHIFT):
         near_ref[r, cols + WIN :, :] = ids_ref[side * SHIFT + r]
 
 
-def rest_kernel(x_hbm, left_ref, right_ref, att_ref, ids_ref, *refs, groups, own_heads, entries, part, hidden):
-    packs, refs = refs[:groups], refs[groups:]
-    (far_ref, x_ref, sems), scratch = refs[:3], refs[3:]
+def rest_kernel(
+    x_hbm, left_ref, right_ref, att_ref, ids_ref, near_ref, *refs,
+    chunks, groups, own_heads, entries, part, hidden,
+):
+    packs, next_packs, refs = refs[:groups], refs[groups : 2 * groups], refs[2 * groups :]
+    (far_ref, qkv_ref, x_ref, strip_ref, next_qkv, next_rows, sems), scratch = refs[:7], refs[7:]
     cols = x_hbm.shape[1]
     side = parity()
     x_copy = pltpu.make_async_copy(
@@ -561,8 +571,14 @@
     for start, count in block0_chunks(cols, 8):
         rows = slice(start * half, (start + count) * half)
         threads.append(sum(finish.pieces(start, count, lambda rows=rows: att_ref[rows]), []))
-    for piece in offset(threads, 3):
-        piece()
+    c = x_ref.shape[2]
+    scale = (c // (own_heads * groups)) ** (-0.5) * LOG2E
+    following = Weights(next_packs, (next_qkv, None, None, None, next_rows), c, part, hidden)
+    following.load_rows()
+    following.load_qkv()
+    spread_message(near_ref, strip_ref)
+    owns = [own_pieces(following, strip_ref, qkv_ref, span, scale) for span in chunks]
+    weave(offset(threads, 3), offset(owns, 5))
 
 
 def even_split(count, most):
@@ -570,19 +586,60 @@
     return [(count * k // parts, count * (k + 1) // parts) for k in range(parts)]
 
 
-def shifted_kernel(own_in, halo_in, rel_ref, *refs, chunks, near, groups, own_heads, entries, part, hidden):
+def spread_message(src, dst):
+    cols = src.shape[1] - 2 * WIN
+    value = src[...].astype(F32)
+    edge = value[:, cols : cols + WIN]
+    dst[:, 0:WIN, :] = edge
+    dst[:, WIN : WIN + cols, :] = value[:, :cols]
+    dst[:, WIN + cols :, :] = edge
+    return value[:, cols + WIN :].reshape(SHIFT * WIN, 128)
+
+
+def gather(ref, span):
+    earlier = lax.broadcasted_iota(jnp.int32, (WIN, ref.shape[2]), 0) < SHIFT
+    pieces = []
+    for j in range(*span):
+        for r in range(SHIFT):
+            before = ref[r, j * WIN : (j + 1) * WIN, :]
+            after = ref[r, (j + 1) * WIN : (j + 2) * WIN, :]
+            pieces.append(jnp.where(earlier, after, before))
+    return jnp.concatenate(pieces, axis=0)
+
+
+def own_pieces(w, strip, qkv, span, scale):
+    rows = slice(span[0] * SHIFT * WIN, span[1] * SHIFT * WIN)
+
+    def keep(m):
+        def store(value):
+            qkv[m, rows] = value
+
+        return store
+
+    norm, rest = w.project_pieces(
+        lambda: gather(strip, span), [(m, None if m else scale, keep(m)) for m in range(3)]
+    )
+    return norm + rest
+
+
+def shifted_kernel(
+    own_in, halo_in, qkv_in, rel_ref, *refs, chunks, near, groups, own_heads, entries, part, hidden
+):
     packs, refs = refs[:groups], refs[groups:]
     side = 1 - parity() if near else parity()
     copies = []
-    if not near:
-        done_ref, out_hbm, out_ref, sems = refs[0], refs[1], refs[2], refs[3]
-        refs = refs[2:3] + refs[4:]
+    if near:
+        next_in, out_ref, next_qkv, next_ref = refs[:4]
+        refs = refs[4:]
+    else:
+        done_ref, out_hbm, out_ref, sems = refs[:4]
+        refs = refs[4:]
         copies.append(
             pltpu.make_async_copy(done_ref, out_hbm.at[pl.ds((1 - side) * SHIFT, SHIFT)], sems.at[0])
         )
         copies[0].start()
-    (out_ref, bias_ref, own_ref, halo_ref, res_ref), refs = refs[:5], refs[5:]
-    (q_ref, kv_ref, att_ref), scratch = refs[:3], refs[3:]
+    (bias_ref, own_ref, halo_ref, res_ref), refs = refs[:4], refs[4:]
+    (kv_ref, att_ref), scratch = refs[:2], refs[2:]
     c = own_in.shape[2]
     cols = out_ref.shape[1]
     heads = own_heads * groups
@@ -609,26 +666,9 @@
         rel = jnp.where(side == 0, pltpu.roll(rel[half:], half, 1), rel[:half])
         bias_ref[...] = w.bias(own_heads, entries - 128, rel)
 
-    parts = []
-    for dst, src in ((own_ref, own_in), (halo_ref, halo_in)):
-        value = src[...].astype(F32)
-        edge = value[:, cols : cols + WIN]
-        dst[:, 0:WIN, :] = edge
-        dst[:, WIN : WIN + cols, :] = value[:, :cols]
-        dst[:, WIN + cols :, :] = edge
-        parts.append(value[:, cols + WIN :].reshape(half, 128))
-    query_ids = parts[0]
-    key_ids = jnp.concatenate(parts + parts, axis=0).T
-    earlier = lax.broadcasted_iota(jnp.int32, (WIN, c), 0) < SHIFT
-
-    def gather(ref, i):
-        pieces = []
-        for j in range(*chunks[i]):
-            for r in range(SHIFT):
-                before = ref[r, j * WIN : (j + 1) * WIN, :]
-                after = ref[r, (j + 1) * WIN : (j + 2) * WIN, :]
-                pieces.append(jnp.where(earlier, after, before))
-        return jnp.concatenate(pieces, axis=0)
+    halo_ids = spread_message(halo_in, halo_ref)
+    query_ids = spread_message(own_in, own_ref)
+    key_ids = jnp.concatenate([query_ids, halo_ids] * 2, axis=0).T
 
     def first(i):
         slot = i % 2
@@ -640,15 +680,11 @@
 
             return store
 
-        own = w.project_pieces(
-            lambda: gather(own_ref, i),
-            [(0, scale, keep(q_ref.at[slot]))]
-            + [(1 + m, None, keep(kv_ref.at[slot, m, 0])) for m in range(2)],
+        norm, rest = w.project_pieces(
+            lambda: gather(halo_ref, chunks[i]),
+            [(1 + m, None, keep(kv_ref.at[slot, m])) for m in range(2)],
         )
-        halo = w.project_pieces(
-            lambda: gather(halo_ref, i), [(1 + m, None, keep(kv_ref.at[slot, m, 1])) for m in range(2)]
-        )
-        return [skewed(list(pair)) for pair in zip(own, halo)]
+        return [norm, rest]
 
     def second(i):
         slot = i % 2
@@ -656,13 +692,14 @@
 
         def window(j):
             rows = slice((j - base) * half, (j - base + 1) * half)
+            own = slice(j * half, (j + 1) * half)
 
             def read():
                 k, v = (
-                    jnp.concatenate([kv_ref[slot, m, 0, rows], kv_ref[slot, m, 1, rows]], axis=0)
+                    jnp.concatenate([qkv_in[1 + m, own], kv_ref[slot, m, rows]], axis=0)
                     for m in range(2)
                 )
-                return q_ref[slot, rows], k, v
+                return qkv_in[0, own], k, v
 
             def allowed():
                 same = jnp.broadcast_to(query_ids[:, j : j + 1], (half, 128)) == key_ids[j : j + 1, :]
@@ -673,7 +710,7 @@
 
             return window_pieces(read, lambda: bias_ref[...], allowed, write, masks, ones)
 
-        return [skewed([window(j) for j in range(*chunks[i])])]
+        return [skewed(grouped([window(j) for j in range(*chunks[i])], 99))]
 
     def third(i):
         base, stop = chunks[i]
@@ -704,10 +741,16 @@
                 copies[-1].start()
 
         return w.finish_pieces(
-            lambda: gather(own_ref, i), lambda: att_ref[i % 2, 0 : (stop - base) * half], store
+            lambda: gather(own_ref, chunks[i]), lambda: att_ref[i % 2, 0 : (stop - base) * half], store
         )
 
-    pipeline(len(chunks), [w.load_qkv, pick_bias, w.load_rest], first, second, third)
+    extra = {0: [w.load_qkv, pick_bias, w.load_rest]}
+    if near:
+        spread_message(next_in, next_ref)
+        last = len(chunks) + 4
+        for n, span in enumerate(chunks):
+            extra[last - len(chunks) + n] = own_pieces(w, next_ref, next_qkv, span, scale)
+    pipeline(len(chunks), extra, first, second, third)
     for copy in copies:
         copy.wait()
 
@@ -807,38 +850,43 @@
         [
             bias_scratch, half_wide,
             pltpu.VMEM(labels.shape, jnp.int32), pltpu.SemaphoreType.DMA((2,)),
-            pltpu.VMEM((2, 3, 4 * tokens, c), BF), pltpu.VMEM((2, 2 * tokens, c), BF),
+            pltpu.VMEM((2, 3, 16 * tokens, c), BF), pltpu.VMEM((2, 8 * tokens, c), BF),
         ] + weights_scratch,
         in_hbm(image_tokens), in_hbm(labels), left, right, rel2, normed, *packs0,
         in_specs=[pl.BlockSpec(memory_space=pltpu.HBM)] * 2 + [in_vmem] * (4 + groups),
     )
     near_halo = swapped(near, 0)
-    far = call(
-        lambda *refs: rest_kernel(*refs, **sizes),
-        strip,
-        [half_wide, pltpu.SemaphoreType.DMA((1,))] + weights_scratch,
-        in_hbm(image_tokens), left, right, rest, ids, *packs0,
-        in_specs=[pl.BlockSpec(memory_space=pltpu.HBM)] + [in_vmem] * (4 + groups),
+    chunks = even_split(tile_cols // WIN + 1, 17)
+    own_qkv = jax.ShapeDtypeStruct((3, (tile_cols // WIN + 1) * SHIFT * WIN, c), BF)
+    strip_wide = pltpu.VMEM((SHIFT, tile_cols + 2 * WIN, c), F32)
+    far, near_qkv = call(
+        lambda *refs: rest_kernel(*refs, chunks=chunks, **sizes),
+        (strip, own_qkv),
+        [
+            half_wide, strip_wide, weights_scratch[0], weights_scratch[-1],
+            pltpu.SemaphoreType.DMA((1,)),
+        ] + weights_scratch,
+        in_hbm(image_tokens), left, right, rest, ids, near, *packs0, *packs1,
+        in_specs=[pl.BlockSpec(memory_space=pltpu.HBM)] + [in_vmem] * (5 + 2 * groups),
     )
     far_halo = swapped(far, 1)
-    chunks = even_split(tile_cols // WIN + 1, 11)
     most = max(stop - base for base, stop in chunks) * SHIFT * WIN
-    strip_wide = pltpu.VMEM((SHIFT, tile_cols + 2 * WIN, c), F32)
     scratch = [
         pltpu.VMEM((SHIFT * WIN, own_heads * groups * tokens), F32), strip_wide, strip_wide,
         pltpu.VMEM((SHIFT, tile_cols + WIN, c), F32),
-        pltpu.VMEM((2, most, c), BF), pltpu.VMEM((2, 2, 2, most, c), BF), pltpu.VMEM((2, most, c), BF),
+        pltpu.VMEM((2, 2, most, c), BF), pltpu.VMEM((2, most, c), BF),
     ] + weights_scratch
-    near_out = call(
+    near_out, far_qkv = call(
         lambda *refs: shifted_kernel(*refs, chunks=chunks, near=True, **sizes),
-        jax.ShapeDtypeStruct((SHIFT, tile_cols, c), BF),
-        scratch, near, near_halo, rel2, *packs1,
+        (jax.ShapeDtypeStruct((SHIFT, tile_cols, c), BF), own_qkv),
+        [strip_wide] + scratch,
+        near, near_halo, near_qkv, rel2, *packs1, far,
     )
     return call(
         lambda *refs: shifted_kernel(*refs, chunks=chunks, near=False, **sizes),
         jax.ShapeDtypeStruct(image_tokens.shape, BF),
         [pltpu.VMEM((SHIFT, tile_cols, c), BF), pltpu.SemaphoreType.DMA((1 + len(chunks),))] + scratch,
-        far, far_halo, rel2, *packs1, near_out,
+        far, far_halo, far_qkv, rel2, *packs1, near_out,
         out_specs=pl.BlockSpec(memory_space=pltpu.HBM),
     )
 

time: 49.6 us -> 36.2 us (0.73)
  waiting for transfers between devices: 11.4 us -> 4.24 us
  Pallas kernels: 25.6 us -> 20.2 us
  starting transfers between devices: 12.1 us -> 11.2 us
    ppermute x2, waiting for transfers between devices: 10.3 us -> 0.01 us  [others(): found.append(lax.ppermute(found[-1], 'ch', swap))]
    pallas_call x6, Pallas kernels: 25.6 us -> 20.2 us  [call(): pl.pallas_call(kernel, out_shape=out_shapes, scratch_shapes=scratch, comp...]
    ppermute x2, waiting for transfers between devices: 0.01 us -> 2.8 us  [swapped(): lax.ppermute(value, ('row', 'ch'), pairs + [(j, i) for i, j in pairs])]
    ppermute x2, starting transfers between devices: 2.72 us -> 1.53 us  [others(): found.append(lax.ppermute(found[-1], 'ch', swap))]
  transfers between devices with their start and end apart: 6 -> 6, of which waited for: 2 -> 3; matrix products, arithmetic and copies ran while one was open for 0% -> 0% of each run, Pallas kernels for 21% -> 39%
where the time goes in v9:
time: 36.2 us; the launch traced here: 35.9 us
  Pallas kernels  20.2 us (56%)
  starting transfers between devices  11.2 us (31%)
  waiting for transfers between devices  4.24 us (12%)
    pallas_call x6, Pallas kernels, call(): pl.pallas_call(kernel, out_shape=out_shapes, scratch_shapes=scratch, comp...  20.2 us
    ppermute x1, starting transfers between devices, both_blocks(): left = lax.ppermute(right_edge, 'col', neighbours('col', 1))  4.23 us
    ppermute x2, starting transfers between devices, swapped(): lax.ppermute(value, ('row', 'ch'), pairs + [(j, i) for i, j in pairs])  3.51 us
    ppermute x2, waiting for transfers between devices, swapped(): lax.ppermute(value, ('row', 'ch'), pairs + [(j, i) for i, j in pairs])  2.8 us
    ppermute x1, starting transfers between devices, both_blocks(): right = lax.ppermute(left_edge, 'col', neighbours('col', -1))  1.92 us
    ppermute x2, starting transfers between devices, others(): found.append(lax.ppermute(found[-1], 'ch', swap))  1.53 us
    ppermute x1, waiting for transfers between devices, both_blocks(): right = lax.ppermute(left_edge, 'col', neighbours('col', -1))  1.43 us
  transfers between devices with their start and end apart: 6, of which 3 were waited for; matrix products, arithmetic and copies ran while one was open for 0% of the time, Pallas kernels for 39%

profile of v9, /device:TPU:9, one launch (start us, length us, event | category | flops | bytes accessed | tf_op | source)
XLA Modules:
  0.0 35.9 jit_solution(1295017762076020530)
XLA Ops:
  0.0 1.4 %shard_map.136 = (bf16[816,128]{1,0:T(8,128)(2,1)S(1)}, bf16[816,128]{1,0:T(8,128)(2,1)S(1)}, bf16[9,8,128]{2,1,0:T(8,128)(2,1)S(1)}, bf16[9,8,128]{2,1,0:T(8,128)(2,1)S(1)}, s32[64,128]{1,0:T(8,128)S(1)}) custom-call(bf16[8,256,128]{2,1,0:T(8,128)(2,1)} %refs_0_.7, s32[8,256]{1,0:T(8,128)} %refs_1_.3, s32[64,64]{1,0:T(8,128)} %refs_2_.1, ...), custom_call_target="tpu_custom_call" | custom-call | tf_op jit(solution)/shard_map/pallas_call | solution.py:759
  1.4 1.3 %collective-permute-start.2 = (bf16[816,128]{1,0:T(8,128)(2,1)S(1)}, bf16[816,128]{1,0:T(8,128)(2,1)S(1)}, u32[]{:S(2)}, u32[]{:S(2)}) collective-permute-start(bf16[816,128]{1,0:T(8,128)(2,1)S(1)} %get-tuple-element.20.refs_1_.refs_6_), channel_id=1, source_target_pairs={{0,1},{1,0},{2,3},{3,2},{4,5},{5,4},{6,7},{7,6},{8,9},{9,8},{10,11... | collective-permute-start | bytes 626696 | tf_op jit(solution)/shard_map/ppermute | solution.py:792
  2.7 0.2 collective-permute-start.3
  3.0 4.2 %collective-permute-start = (bf16[9,8,128]{2,1,0:T(8,128)(2,1)S(1)}, bf16[9,8,128]{2,1,0:T(8,128)(2,1)S(1)}, u32[]{:S(2)}, u32[]{:S(2)}) collective-permute-start(bf16[9,8,128]{2,1,0:T(8,128)(2,1)S(1)} %get-tuple-element.17), channel_id=1, source_target_pairs={{0,2},{2,4},{4,6},{1,3},{3,5},{5,7},{8,10},{10,12},{12,14},{9,11},... | collective-permute-start | bytes 55304 | tf_op jit(solution)/shard_map/ppermute | solution.py:811
  7.2 1.9 %collective-permute-start.1 = (bf16[9,8,128]{2,1,0:T(8,128)(2,1)S(1)}, bf16[9,8,128]{2,1,0:T(8,128)(2,1)S(1)}, u32[]{:S(2)}, u32[]{:S(2)}) collective-permute-start(bf16[9,8,128]{2,1,0:T(8,128)(2,1)S(1)} %get-tuple-element.18), channel_id=1, source_target_pairs={{2,0},{4,2},{6,4},{3,1},{5,3},{7,5},{10,8},{12,10},{14,12},{11,9},... | collective-permute-start | bytes 55304 | tf_op jit(solution)/shard_map/ppermute | solution.py:812
  9.1 2.0 %shard_map.137.refs_5_ = bf16[2048,128]{1,0:T(8,128)(2,1)S(1)} custom-call(bf16[8,256,128]{2,1,0:T(8,128)(2,1)} %refs_0_.7, bf16[816,128]{1,0:T(8,128)(2,1)S(1)} %get-tuple-element.20.refs_1_.refs_6_), custom_call_target="tpu_custom_call" | custom-call | tf_op jit(solution)/shard_map/pallas_call | solution.py:759
  11.1 0.0 collective-permute-done.refs_2_.refs_1_
  11.2 1.4 %collective-permute-done.1.refs_3_.refs_2_ = bf16[9,8,128]{2,1,0:T(8,128)(2,1)S(1)} collective-permute-done((bf16[9,8,128]{2,1,0:T(8,128)(2,1)S(1)}, bf16[9,8,128]{2,1,0:T(8,128)(2,1)S(1)}, u32[]{:S(2)}, u32[]{:S(2)}) %collective-permute-start.1) | collective-permute-done | bytes 18464 | tf_op jit(solution)/shard_map/ppermute | solution.py:812
  12.6 0.0 collective-permute-done.2.refs_7_
  12.6 4.5 %shard_map.138 = (bf16[4,272,128]{2,1,0:T(8,128)(2,1)S(1)}, bf16[1088,128]{1,0:T(8,128)(2,1)S(1)}, bf16[8,8,128]{2,1,0:T(8,128)(2,1)S(1)}) custom-call(bf16[8,256,128]{2,1,0:T(8,128)(2,1)} %refs_0_.7, s32[8,256]{1,0:T(8,128)} %refs_1_.3, bf16[9,8,128]{2,1,0:T(8,128)(2,1)S(1)} %collective-permute-done.refs_2_.refs_1_, ...), custom_call_target="tpu_custom_call" | custom-call | tf_op jit(solution)/shard_map/pallas_call | solution.py:759
  17.1 1.3 %collective-permute-start.5 = (bf16[4,272,128]{2,1,0:T(8,128)(2,1)S(1)}, bf16[4,272,128]{2,1,0:T(8,128)(2,1)S(1)}, u32[]{:S(2)}, u32[]{:S(2)}) collective-permute-start(bf16[4,272,128]{2,1,0:T(8,128)(2,1)S(1)} %get-tuple-element.23.refs_5_.refs_0_), channel_id=1, source_target_pairs={{0,1},{8,9},{16,17},{24,25},{1,0},{9,8},{17,16},{25,24},{2,3},{10,... | collective-permute-start | bytes 835592 | tf_op jit(solution)/shard_map/ppermute | solution.py:830
  18.4 0.0 collective-permute-done.3.refs_9_.refs_5_
  18.4 3.0 %shard_map.139 = (bf16[4,272,128]{2,1,0:T(8,128)(2,1)S(1)}, bf16[3,1056,128]{2,1,0:T(8,128)(2,1)S(1)}) custom-call(bf16[8,256,128]{2,1,0:T(8,128)(2,1)} %refs_0_.7, bf16[9,8,128]{2,1,0:T(8,128)(2,1)S(1)} %collective-permute-done.refs_2_.refs_1_, bf16[9,8,128]{2,1,0:T(8,128)(2,1)S(1)} %collective-permute-done.1.refs_3_.refs_2_, ...), custom_call_target="tpu_custom_call" | custom-call | tf_op jit(solution)/shard_map/pallas_call | solution.py:759
  21.4 2.2 %collective-permute-start.4 = (bf16[4,272,128]{2,1,0:T(8,128)(2,1)S(1)}, bf16[4,272,128]{2,1,0:T(8,128)(2,1)S(1)}, u32[]{:S(2)}, u32[]{:S(2)}) collective-permute-start(bf16[4,272,128]{2,1,0:T(8,128)(2,1)S(1)} %get-tuple-element.25.refs_6_.refs_0_), channel_id=1, source_target_pairs={{1,8},{9,16},{17,24},{8,1},{16,9},{24,17},{3,10},{11,18},{19,26},{... | collective-permute-start | bytes 835592 | tf_op jit(solution)/shard_map/ppermute | solution.py:830
  23.6 0.1 collective-permute-done.5.refs_1_
  23.7 4.6 %shard_map.140 = (bf16[4,256,128]{2,1,0:T(8,128)(2,1)S(1)}, bf16[3,1056,128]{2,1,0:T(8,128)(2,1)S(1)}) custom-call(bf16[4,272,128]{2,1,0:T(8,128)(2,1)S(1)} %get-tuple-element.23.refs_5_.refs_0_, bf16[4,272,128]{2,1,0:T(8,128)(2,1)S(1)} %collective-permute-done.5.refs_1_, bf16[3,1056,128]{2,1,0:T(8,128)(2,1)S(1)} %get-tuple-element.26.refs_2_, ...), custom_call_target="tpu_custom_call" | custom-call | tf_op jit(solution)/shard_map/pallas_call | solution.py:759
  28.3 2.7 %collective-permute-done.4.refs_1_ = bf16[4,272,128]{2,1,0:T(8,128)(2,1)S(1)} collective-permute-done((bf16[4,272,128]{2,1,0:T(8,128)(2,1)S(1)}, bf16[4,272,128]{2,1,0:T(8,128)(2,1)S(1)}, u32[]{:S(2)}, u32[]{:S(2)}) %collective-permute-start.4) | collective-permute-done | bytes 278560 | tf_op jit(solution)/shard_map/ppermute | solution.py:830
  31.0 4.7 %shard_map.141 = bf16[8,256,128]{2,1,0:T(8,128)(2,1)} custom-call(bf16[4,272,128]{2,1,0:T(8,128)(2,1)S(1)} %get-tuple-element.25.refs_6_.refs_0_, bf16[4,272,128]{2,1,0:T(8,128)(2,1)S(1)} %collective-permute-done.4.refs_1_, bf16[3,1056,128]{2,1,0:T(8,128)(2,1)S(1)} %get-tuple-element.27.refs_2_, s32[64,128]{1,0:T(8,128)S(1)} %get-tuple-element.19.refs_4_.refs_3_, ...), custom_call_target="tpu_custom_call" | custom-call | tf_op jit(solution)/shard_map/pallas_call | solution.py:759
Async XLA Ops:
  1.4 11.1 %collective-permute-start.2 = (bf16[816,128]{1,0:T(8,128)(2,1)S(1)}, bf16[816,128]{1,0:T(8,128)(2,1)S(1)}, u32[]{:S(2)}, u32[]{:S(2)}) collective-permute-start(bf16[816,128]{1,0:T(8,128)(2,1)S(1)} %get-tuple-element.20.refs_1_.refs_6_), channel_id=1, source_target_pairs={{0,1},{1,0},{2,3},{3,2},{4,5},{5,4},{6,7},{7,6},{8,9},{9,8},{10,11... | collective-permute-start | bytes 626696 | tf_op jit(solution)/shard_map/ppermute | solution.py:792
  2.7 15.6 %collective-permute-start.3 = (bf16[816,128]{1,0:T(8,128)(2,1)S(1)}, bf16[816,128]{1,0:T(8,128)(2,1)S(1)}, u32[]{:S(2)}, u32[]{:S(2)}) collective-permute-start(bf16[816,128]{1,0:T(8,128)(2,1)S(1)} %get-tuple-element.24.refs_8_.refs_4_), channel_id=1, source_target_pairs={{0,1},{1,0},{2,3},{3,2},{4,5},{5,4},{6,7},{7,6},{8,9},{9,8},{10,11... | collective-permute-start | bytes 626696 | tf_op jit(solution)/shard_map/ppermute | solution.py:792
  3.0 8.2 %collective-permute-start = (bf16[9,8,128]{2,1,0:T(8,128)(2,1)S(1)}, bf16[9,8,128]{2,1,0:T(8,128)(2,1)S(1)}, u32[]{:S(2)}, u32[]{:S(2)}) collective-permute-start(bf16[9,8,128]{2,1,0:T(8,128)(2,1)S(1)} %get-tuple-element.17), channel_id=1, source_target_pairs={{0,2},{2,4},{4,6},{1,3},{3,5},{5,7},{8,10},{10,12},{12,14},{9,11},... | collective-permute-start | bytes 55304 | tf_op jit(solution)/shard_map/ppermute | solution.py:811
  7.2 5.4 %collective-permute-start.1 = (bf16[9,8,128]{2,1,0:T(8,128)(2,1)S(1)}, bf16[9,8,128]{2,1,0:T(8,128)(2,1)S(1)}, u32[]{:S(2)}, u32[]{:S(2)}) collective-permute-start(bf16[9,8,128]{2,1,0:T(8,128)(2,1)S(1)} %get-tuple-element.18), channel_id=1, source_target_pairs={{2,0},{4,2},{6,4},{3,1},{5,3},{7,5},{10,8},{12,10},{14,12},{11,9},... | collective-permute-start | bytes 55304 | tf_op jit(solution)/shard_map/ppermute | solution.py:812
  17.1 6.6 %collective-permute-start.5 = (bf16[4,272,128]{2,1,0:T(8,128)(2,1)S(1)}, bf16[4,272,128]{2,1,0:T(8,128)(2,1)S(1)}, u32[]{:S(2)}, u32[]{:S(2)}) collective-permute-start(bf16[4,272,128]{2,1,0:T(8,128)(2,1)S(1)} %get-tuple-element.23.refs_5_.refs_0_), channel_id=1, source_target_pairs={{0,1},{8,9},{16,17},{24,25},{1,0},{9,8},{17,16},{25,24},{2,3},{10,... | collective-permute-start | bytes 835592 | tf_op jit(solution)/shard_map/ppermute | solution.py:830
  21.4 9.6 %collective-permute-start.4 = (bf16[4,272,128]{2,1,0:T(8,128)(2,1)S(1)}, bf16[4,272,128]{2,1,0:T(8,128)(2,1)S(1)}, u32[]{:S(2)}, u32[]{:S(2)}) collective-permute-start(bf16[4,272,128]{2,1,0:T(8,128)(2,1)S(1)} %get-tuple-element.25.refs_6_.refs_0_), channel_id=1, source_target_pairs={{1,8},{9,16},{17,24},{8,1},{16,9},{24,17},{3,10},{11,18},{19,26},{... | collective-permute-start | bytes 835592 | tf_op jit(solution)/shard_map/ppermute | solution.py:830

commit v10 on v9

--- a/solution.py
+++ b/solution.py
@@ -384,14 +384,16 @@
 
 class Rows:
 
-    def __init__(self, weights, x_ref, out_ref, cols):
-        self.w, self.x, self.out, self.cols = weights, x_ref, out_ref, cols
+    def __init__(self, weights, x_ref, edge_ref, out_ref):
+        self.w, self.x, self.edge, self.out = weights, x_ref, edge_ref, out_ref
+        self.cols = x_ref.shape[1]
 
     def pieces(self, start, count, attended):
         span = slice(start * WIN, (start + count) * WIN)
 
         def load():
-            block = self.x[:, span, :].astype(F32)
+            inside = start * WIN < self.cols
+            block = (self.x[:, span, :] if inside else self.edge[...]).astype(F32)
             return jnp.concatenate(
                 [block[r, n * WIN : (n + 1) * WIN] for n in range(count) for r in range(SHIFT)], axis=0
             )
@@ -417,17 +419,27 @@
     return [(n, min(size, wins - n)) for n in range(0, wins, size)] + [(wins, 2)]
 
 
-def put_edges(x_ref, left_ref, right_ref, cols, base=0):
-    for r in range(x_ref.shape[0]):
-        x_ref[r, cols : cols + 2 * WIN, :] = jnp.concatenate(
-            [left_ref[base + r], right_ref[base + r]], axis=0
+def put_edges(edge_ref, left_ref, right_ref, side):
+    for r in range(SHIFT):
+        edge_ref[r] = jnp.concatenate(
+            [left_ref[side * SHIFT + r], right_ref[side * SHIFT + r]], axis=0
         )
 
 
-def norm_kernel(x_hbm, pack_ref, normed_ref, x_ref, rows_ref, sem, *, part, hidden):
+def norm_kernel(
+    x_hbm, labels_hbm, pack_ref, normed_ref, near_ref, far_ref, labels_ref, x_ref, rows_ref, sem,
+    *, part, hidden,
+):
+    sides = [
+        pltpu.make_async_copy(x_hbm.at[pl.ds(side * SHIFT, SHIFT)], target, sem.at[k])
+        for k, side, target in ((1, 1 - parity(), near_ref), (2, parity(), far_ref))
+    ]
+    sides.append(pltpu.make_async_copy(labels_hbm, labels_ref, sem.at[3]))
     cols = x_hbm.shape[1]
     x_copy = pltpu.make_async_copy(x_hbm, x_ref, sem.at[0])
     x_copy.start()
+    for copy in sides:
+        copy.start()
     w = Weights([pack_ref], (None, None, None, None, rows_ref), x_ref.shape[2], part, hidden)
     for k in range(2):
         rows_ref[k : k + 1, :] = w.small(GAIN + k)[0]
@@ -453,24 +465,20 @@
     wins = cols // WIN
     for piece in offset([chunk(n, min(4, wins - n)) for n in range(0, wins, 4)], 1):
         piece()
+    for copy in sides:
+        copy.wait()
 
 
 def regular_kernel(
-    x_hbm, labels_hbm, left_ref, right_ref, rel_ref, normed_ref, *refs,
+    x_ref, labels_ref, left_ref, right_ref, rel_ref, normed_ref, *refs,
     groups, own_heads, entries, part, hidden,
 ):
     packs, refs = refs[:groups], refs[groups:]
-    (near_ref, rest_ref, ids_ref, bias_ref, side_ref), refs = refs[:5], refs[5:]
-    (labels_ref, sems, qkv_ref, att_ref), scratch = refs[:4], refs[4:]
+    (near_ref, rest_ref, ids_ref, bias_ref, edge_ref), refs = refs[:5], refs[5:]
+    (qkv_ref, att_ref), scratch = refs[:2], refs[2:]
     side = 1 - parity()
-    cols = x_hbm.shape[1]
-    labels_copy = pltpu.make_async_copy(labels_hbm, labels_ref, sems.at[0])
-    side_copy = pltpu.make_async_copy(
-        x_hbm.at[pl.ds(side * SHIFT, SHIFT)], side_ref.at[:, 0:cols], sems.at[1]
-    )
-    labels_copy.start()
-    side_copy.start()
-    c = side_ref.shape[2]
+    cols = x_ref.shape[1]
+    c = x_ref.shape[2]
     heads = own_heads * groups
     depth = c // heads
     tokens = WIN * WIN
@@ -488,12 +496,10 @@
     def put_ids():
         ids_ref[...] = edge_ids(left_ref, right_ref, labels_ref[...])
 
-    labels_copy.wait()
-    side_copy.wait()
-    put_edges(side_ref, left_ref, right_ref, cols, side * SHIFT)
-    extra = [pick_bias, put_ids, w.load_rest]
+    put_edges(edge_ref, left_ref, right_ref, side)
+    extra = {0: [pick_bias, put_ids, w.load_rest]}
     chunks = block0_chunks(cols)
-    finish = Rows(w, side_ref, near_ref, cols)
+    finish = Rows(w, x_ref, edge_ref, near_ref)
 
     def first(i):
         start, count = chunks[i]
@@ -541,32 +547,27 @@
         start, count = chunks[i]
         return finish.pieces(start, count, lambda: att_ref[i % 2, 0 : count * half])
 
-    pipeline(len(chunks), {0: extra}, first, second, third)
+    pipeline(len(chunks), extra, first, second, third)
     for r in range(SHIFT):
         near_ref[r, cols + WIN :, :] = ids_ref[side * SHIFT + r]
 
 
 def rest_kernel(
-    x_hbm, left_ref, right_ref, att_ref, ids_ref, near_ref, *refs,
+    x_ref, left_ref, right_ref, att_ref, ids_ref, near_ref, *refs,
     chunks, groups, own_heads, entries, part, hidden,
 ):
     packs, next_packs, refs = refs[:groups], refs[groups : 2 * groups], refs[2 * groups :]
-    (far_ref, qkv_ref, x_ref, strip_ref, next_qkv, next_rows, sems), scratch = refs[:7], refs[7:]
-    cols = x_hbm.shape[1]
+    (far_ref, qkv_ref, edge_ref, strip_ref, next_qkv, next_rows), scratch = refs[:6], refs[6:]
+    cols = x_ref.shape[1]
     side = parity()
-    x_copy = pltpu.make_async_copy(
-        x_hbm.at[pl.ds(side * SHIFT, SHIFT)], x_ref.at[:, 0:cols], sems.at[0]
-    )
-    x_copy.start()
     w = Weights(packs, scratch, x_ref.shape[2], part, hidden)
     w.load_rows()
     w.load_rest()
-    put_edges(x_ref, left_ref, right_ref, cols, side * SHIFT)
-    finish = Rows(w, x_ref, far_ref, cols)
+    put_edges(edge_ref, left_ref, right_ref, side)
+    finish = Rows(w, x_ref, edge_ref, far_ref)
     half = SHIFT * WIN
     for r in range(SHIFT):
         far_ref[r, cols + WIN :, :] = ids_ref[side * SHIFT + r]
-    x_copy.wait()
     threads = []
     for start, count in block0_chunks(cols, 8):
         rows = slice(start * half, (start + count) * half)
@@ -822,7 +823,8 @@
     ]
     strip = jax.ShapeDtypeStruct((SHIFT, tile_cols + 2 * WIN, c), BF)
     bias_scratch = pltpu.VMEM((tokens, own_heads * groups * tokens), F32)
-    half_wide = pltpu.VMEM((SHIFT, tile_cols + 2 * WIN, c), BF)
+    beside = pltpu.VMEM((SHIFT, 2 * WIN, c), BF)
+    half_tile = jax.ShapeDtypeStruct((SHIFT, tile_cols, c), BF)
     bands = lax.axis_size(("row", "ch"))
 
     def swapped(value, first):
@@ -830,15 +832,18 @@
         return lax.ppermute(value, ("row", "ch"), pairs + [(j, i) for i, j in pairs])
 
     in_vmem = pl.BlockSpec(memory_space=pltpu.VMEM)
-    normed = call(
+    normed, x_near, x_far, own_labels = call(
         lambda *refs: norm_kernel(*refs, part=part, hidden=hidden),
-        jax.ShapeDtypeStruct((tokens * (tile_cols // WIN), c), BF),
+        (
+            jax.ShapeDtypeStruct((tokens * (tile_cols // WIN), c), BF), half_tile, half_tile,
+            jax.ShapeDtypeStruct(labels.shape, labels.dtype),
+        ),
         [
             pltpu.VMEM(image_tokens.shape, BF), pltpu.VMEM((4, c), F32),
-            pltpu.SemaphoreType.DMA((1,)),
+            pltpu.SemaphoreType.DMA((4,)),
         ],
-        in_hbm(image_tokens), own0,
-        in_specs=[pl.BlockSpec(memory_space=pltpu.HBM), in_vmem],
+        in_hbm(image_tokens), in_hbm(labels), own0,
+        in_specs=[pl.BlockSpec(memory_space=pltpu.HBM)] * 2 + [in_vmem],
     )
     near, rest, ids = call(
         lambda *refs: regular_kernel(*refs, **sizes),
@@ -848,12 +853,10 @@
             jax.ShapeDtypeStruct((WIN, WIN, 128), BF),
         ),
         [
-            bias_scratch, half_wide,
-            pltpu.VMEM(labels.shape, jnp.int32), pltpu.SemaphoreType.DMA((2,)),
+            bias_scratch, beside,
             pltpu.VMEM((2, 3, 16 * tokens, c), BF), pltpu.VMEM((2, 8 * tokens, c), BF),
         ] + weights_scratch,
-        in_hbm(image_tokens), in_hbm(labels), left, right, rel2, normed, *packs0,
-        in_specs=[pl.BlockSpec(memory_space=pltpu.HBM)] * 2 + [in_vmem] * (4 + groups),
+        x_near, own_labels, left, right, rel2, normed, *packs0,
     )
     near_halo = swapped(near, 0)
     chunks = even_split(tile_cols // WIN + 1, 17)
@@ -862,12 +865,8 @@
     far, near_qkv = call(
         lambda *refs: rest_kernel(*refs, chunks=chunks, **sizes),
         (strip, own_qkv),
-        [
-            half_wide, strip_wide, weights_scratch[0], weights_scratch[-1],
-            pltpu.SemaphoreType.DMA((1,)),
-        ] + weights_scratch,
-        in_hbm(image_tokens), left, right, rest, ids, near, *packs0, *packs1,
-        in_specs=[pl.BlockSpec(memory_space=pltpu.HBM)] + [in_vmem] * (5 + 2 * groups),
+        [beside, strip_wide, weights_scratch[0], weights_scratch[-1]] + weights_scratch,
+        x_far, left, right, rest, ids, near, *packs0, *packs1,
     )
     far_halo = swapped(far, 1)
     most = max(stop - base for base, stop in chunks) * SHIFT * WIN

time: 36.2 us -> 38.6 us (1.066)
  the two profiles are of different devices: /device:TPU:9 before, /device:TPU:1 now
where the time goes in v10:
time: 38.6 us; the launch traced here: 38.4 us
  Pallas kernels  18.4 us (48%)
  starting transfers between devices  10.7 us (28%)
  waiting for transfers between devices  9.09 us (24%)
    pallas_call x6, Pallas kernels, call(): pl.pallas_call(kernel, out_shape=out_shapes, scratch_shapes=scratch, comp...  18.4 us
    ppermute x2, waiting for transfers between devices, swapped(): lax.ppermute(value, ('row', 'ch'), pairs + [(j, i) for i, j in pairs])  7.68 us
    ppermute x1, starting transfers between devices, both_blocks(): left = lax.ppermute(right_edge, 'col', neighbours('col', 1))  4.38 us
    ppermute x2, starting transfers between devices, others(): found.append(lax.ppermute(found[-1], 'ch', swap))  2.2 us
    ppermute x2, starting transfers between devices, swapped(): lax.ppermute(value, ('row', 'ch'), pairs + [(j, i) for i, j in pairs])  2.17 us
    ppermute x1, starting transfers between devices, both_blocks(): right = lax.ppermute(left_edge, 'col', neighbours('col', -1))  1.92 us
    ppermute x1, waiting for transfers between devices, both_blocks(): right = lax.ppermute(left_edge, 'col', neighbours('col', -1))  1.4 us
  transfers between devices with their start and end apart: 6, of which 2 were waited for; matrix products, arithmetic and copies ran while one was open for 0% of the time, Pallas kernels for 32%

profile of v10, /device:TPU:1, one launch (start us, length us, event | category | flops | bytes accessed | tf_op | source)
XLA Modules:
  0.0 38.4 jit_solution(6091031919813674436)
XLA Ops:
  0.0 1.4 %shard_map.136 = (bf16[816,128]{1,0:T(8,128)(2,1)S(1)}, bf16[816,128]{1,0:T(8,128)(2,1)S(1)}, bf16[9,8,128]{2,1,0:T(8,128)(2,1)S(1)}, bf16[9,8,128]{2,1,0:T(8,128)(2,1)S(1)}, s32[64,128]{1,0:T(8,128)S(1)}) custom-call(bf16[8,256,128]{2,1,0:T(8,128)(2,1)} %refs_0_.3, s32[8,256]{1,0:T(8,128)} %refs_1_.3, s32[64,64]{1,0:T(8,128)} %refs_2_.1, ...), custom_call_target="tpu_custom_call" | custom-call | tf_op jit(solution)/shard_map/pallas_call | solution.py:760
  1.4 2.1 %collective-permute-start.2 = (bf16[816,128]{1,0:T(8,128)(2,1)S(1)}, bf16[816,128]{1,0:T(8,128)(2,1)S(1)}, u32[]{:S(2)}, u32[]{:S(2)}) collective-permute-start(bf16[816,128]{1,0:T(8,128)(2,1)S(1)} %get-tuple-element.21.refs_2_.refs_6_), channel_id=1, source_target_pairs={{0,1},{1,0},{2,3},{3,2},{4,5},{5,4},{6,7},{7,6},{8,9},{9,8},{10,11... | collective-permute-start | bytes 626696 | tf_op jit(solution)/shard_map/ppermute | solution.py:793
  3.6 0.1 collective-permute-start.3
  3.6 4.4 %collective-permute-start = (bf16[9,8,128]{2,1,0:T(8,128)(2,1)S(1)}, bf16[9,8,128]{2,1,0:T(8,128)(2,1)S(1)}, u32[]{:S(2)}, u32[]{:S(2)}) collective-permute-start(bf16[9,8,128]{2,1,0:T(8,128)(2,1)S(1)} %get-tuple-element.23), channel_id=1, source_target_pairs={{0,2},{2,4},{4,6},{1,3},{3,5},{5,7},{8,10},{10,12},{12,14},{9,11},... | collective-permute-start | bytes 55304 | tf_op jit(solution)/shard_map/ppermute | solution.py:812
  8.0 1.9 %collective-permute-start.1 = (bf16[9,8,128]{2,1,0:T(8,128)(2,1)S(1)}, bf16[9,8,128]{2,1,0:T(8,128)(2,1)S(1)}, u32[]{:S(2)}, u32[]{:S(2)}) collective-permute-start(bf16[9,8,128]{2,1,0:T(8,128)(2,1)S(1)} %get-tuple-element.24), channel_id=1, source_target_pairs={{2,0},{4,2},{6,4},{3,1},{5,3},{7,5},{10,8},{12,10},{14,12},{11,9},... | collective-permute-start | bytes 55304 | tf_op jit(solution)/shard_map/ppermute | solution.py:813
  10.0 2.0 %shard_map.137 = (bf16[2048,128]{1,0:T(8,128)(2,1)S(1)}, bf16[4,256,128]{2,1,0:T(8,128)(2,1)S(1)}, bf16[4,256,128]{2,1,0:T(8,128)(2,1)S(1)}, s32[8,256]{1,0:T(8,128)S(1)}) custom-call(bf16[8,256,128]{2,1,0:T(8,128)(2,1)} %refs_0_.3, s32[8,256]{1,0:T(8,128)} %refs_1_.3, bf16[816,128]{1,0:T(8,128)(2,1)S(1)} %get-tuple-element.21.refs_2_.refs_6_), custom_call_target="tpu_custom_call" | custom-call | tf_op jit(solution)/shard_map/pallas_call | solution.py:760
  12.0 0.0 collective-permute-done.refs_2_.refs_1_
  12.0 1.4 %collective-permute-done.1.refs_3_.refs_2_ = bf16[9,8,128]{2,1,0:T(8,128)(2,1)S(1)} collective-permute-done((bf16[9,8,128]{2,1,0:T(8,128)(2,1)S(1)}, bf16[9,8,128]{2,1,0:T(8,128)(2,1)S(1)}, u32[]{:S(2)}, u32[]{:S(2)}) %collective-permute-start.1) | collective-permute-done | bytes 18464 | tf_op jit(solution)/shard_map/ppermute | solution.py:813
  13.4 0.0 collective-permute-done.2.refs_7_
  13.4 3.5 %shard_map.138 = (bf16[4,272,128]{2,1,0:T(8,128)(2,1)S(1)}, bf16[1088,128]{1,0:T(8,128)(2,1)S(1)}, bf16[8,8,128]{2,1,0:T(8,128)(2,1)S(1)}) custom-call(bf16[4,256,128]{2,1,0:T(8,128)(2,1)S(1)} %get-tuple-element.25.refs_0_, s32[8,256]{1,0:T(8,128)S(1)} %get-tuple-element.26.refs_1_, bf16[9,8,128]{2,1,0:T(8,128)(2,1)S(1)} %collective-permute-done.refs_2_.refs_1_, ...), custom_call_target="tpu_custom_call" | custom-call | tf_op jit(solution)/shard_map/pallas_call | solution.py:760
  17.0 1.3 %collective-permute-start.5 = (bf16[4,272,128]{2,1,0:T(8,128)(2,1)S(1)}, bf16[4,272,128]{2,1,0:T(8,128)(2,1)S(1)}, u32[]{:S(2)}, u32[]{:S(2)}) collective-permute-start(bf16[4,272,128]{2,1,0:T(8,128)(2,1)S(1)} %get-tuple-element.31.refs_5_.refs_0_), channel_id=1, source_target_pairs={{0,1},{8,9},{16,17},{24,25},{1,0},{9,8},{17,16},{25,24},{2,3},{10,... | collective-permute-start | bytes 835592 | tf_op jit(solution)/shard_map/ppermute | solution.py:832
  18.3 0.0 collective-permute-done.3.refs_9_.refs_5_
  18.3 2.1 %shard_map.139 = (bf16[4,272,128]{2,1,0:T(8,128)(2,1)S(1)}, bf16[3,1056,128]{2,1,0:T(8,128)(2,1)S(1)}) custom-call(bf16[4,256,128]{2,1,0:T(8,128)(2,1)S(1)} %get-tuple-element.22.refs_0_, bf16[9,8,128]{2,1,0:T(8,128)(2,1)S(1)} %collective-permute-done.refs_2_.refs_1_, bf16[9,8,128]{2,1,0:T(8,128)(2,1)S(1)} %collective-permute-done.1.refs_3_.refs_2_, ...), custom_call_target="tpu_custom_call" | custom-call | tf_op jit(solution)/shard_map/pallas_call | solution.py:760
  20.3 0.9 %collective-permute-start.4 = (bf16[4,272,128]{2,1,0:T(8,128)(2,1)S(1)}, bf16[4,272,128]{2,1,0:T(8,128)(2,1)S(1)}, u32[]{:S(2)}, u32[]{:S(2)}) collective-permute-start(bf16[4,272,128]{2,1,0:T(8,128)(2,1)S(1)} %get-tuple-element.33.refs_6_.refs_0_), channel_id=1, source_target_pairs={{1,8},{9,16},{17,24},{8,1},{16,9},{24,17},{3,10},{11,18},{19,26},{... | collective-permute-start | bytes 835592 | tf_op jit(solution)/shard_map/ppermute | solution.py:832
  21.2 7.7 %collective-permute-done.5.refs_1_ = bf16[4,272,128]{2,1,0:T(8,128)(2,1)S(1)} collective-permute-done((bf16[4,272,128]{2,1,0:T(8,128)(2,1)S(1)}, bf16[4,272,128]{2,1,0:T(8,128)(2,1)S(1)}, u32[]{:S(2)}, u32[]{:S(2)}) %collective-permute-start.5) | collective-permute-done | bytes 278560 | tf_op jit(solution)/shard_map/ppermute | solution.py:832
  28.9 4.6 %shard_map.140 = (bf16[4,256,128]{2,1,0:T(8,128)(2,1)S(1)}, bf16[3,1056,128]{2,1,0:T(8,128)(2,1)S(1)}) custom-call(bf16[4,272,128]{2,1,0:T(8,128)(2,1)S(1)} %get-tuple-element.31.refs_5_.refs_0_, bf16[4,272,128]{2,1,0:T(8,128)(2,1)S(1)} %collective-permute-done.5.refs_1_, bf16[3,1056,128]{2,1,0:T(8,128)(2,1)S(1)} %get-tuple-element.34.refs_2_, ...), custom_call_target="tpu_custom_call" | custom-call | tf_op jit(solution)/shard_map/pallas_call | solution.py:760
  33.5 0.0 collective-permute-done.4.refs_1_
  33.5 4.7 %shard_map.141 = bf16[8,256,128]{2,1,0:T(8,128)(2,1)} custom-call(bf16[4,272,128]{2,1,0:T(8,128)(2,1)S(1)} %get-tuple-element.33.refs_6_.refs_0_, bf16[4,272,128]{2,1,0:T(8,128)(2,1)S(1)} %collective-permute-done.4.refs_1_, bf16[3,1056,128]{2,1,0:T(8,128)(2,1)S(1)} %get-tuple-element.35.refs_2_, s32[64,128]{1,0:T(8,128)S(1)} %get-tuple-element.27.refs_4_.refs_3_, ...), custom_call_target="tpu_custom_call" | custom-call | tf_op jit(solution)/shard_map/pallas_call | solution.py:760
Async XLA Ops:
  1.4 12.0 %collective-permute-start.2 = (bf16[816,128]{1,0:T(8,128)(2,1)S(1)}, bf16[816,128]{1,0:T(8,128)(2,1)S(1)}, u32[]{:S(2)}, u32[]{:S(2)}) collective-permute-start(bf16[816,128]{1,0:T(8,128)(2,1)S(1)} %get-tuple-element.21.refs_2_.refs_6_), channel_id=1, source_target_pairs={{0,1},{1,0},{2,3},{3,2},{4,5},{5,4},{6,7},{7,6},{8,9},{9,8},{10,11... | collective-permute-start | bytes 626696 | tf_op jit(solution)/shard_map/ppermute | solution.py:793
  3.6 14.7 %collective-permute-start.3 = (bf16[816,128]{1,0:T(8,128)(2,1)S(1)}, bf16[816,128]{1,0:T(8,128)(2,1)S(1)}, u32[]{:S(2)}, u32[]{:S(2)}) collective-permute-start(bf16[816,128]{1,0:T(8,128)(2,1)S(1)} %get-tuple-element.32.refs_8_.refs_4_), channel_id=1, source_target_pairs={{0,1},{1,0},{2,3},{3,2},{4,5},{5,4},{6,7},{7,6},{8,9},{9,8},{10,11... | collective-permute-start | bytes 626696 | tf_op jit(solution)/shard_map/ppermute | solution.py:793
  3.6 8.3 %collective-permute-start = (bf16[9,8,128]{2,1,0:T(8,128)(2,1)S(1)}, bf16[9,8,128]{2,1,0:T(8,128)(2,1)S(1)}, u32[]{:S(2)}, u32[]{:S(2)}) collective-permute-start(bf16[9,8,128]{2,1,0:T(8,128)(2,1)S(1)} %get-tuple-element.23), channel_id=1, source_target_pairs={{0,2},{2,4},{4,6},{1,3},{3,5},{5,7},{8,10},{10,12},{12,14},{9,11},... | collective-permute-start | bytes 55304 | tf_op jit(solution)/shard_map/ppermute | solution.py:812
  8.0 5.4 %collective-permute-start.1 = (bf16[9,8,128]{2,1,0:T(8,128)(2,1)S(1)}, bf16[9,8,128]{2,1,0:T(8,128)(2,1)S(1)}, u32[]{:S(2)}, u32[]{:S(2)}) collective-permute-start(bf16[9,8,128]{2,1,0:T(8,128)(2,1)S(1)} %get-tuple-element.24), channel_id=1, source_target_pairs={{2,0},{4,2},{6,4},{3,1},{5,3},{7,5},{10,8},{12,10},{14,12},{11,9},... | collective-permute-start | bytes 55304 | tf_op jit(solution)/shard_map/ppermute | solution.py:813
  17.0 11.9 %collective-permute-start.5 = (bf16[4,272,128]{2,1,0:T(8,128)(2,1)S(1)}, bf16[4,272,128]{2,1,0:T(8,128)(2,1)S(1)}, u32[]{:S(2)}, u32[]{:S(2)}) collective-permute-start(bf16[4,272,128]{2,1,0:T(8,128)(2,1)S(1)} %get-tuple-element.31.refs_5_.refs_0_), channel_id=1, source_target_pairs={{0,1},{8,9},{16,17},{24,25},{1,0},{9,8},{17,16},{25,24},{2,3},{10,... | collective-permute-start | bytes 835592 | tf_op jit(solution)/shard_map/ppermute | solution.py:832
  20.3 13.2 %collective-permute-start.4 = (bf16[4,272,128]{2,1,0:T(8,128)(2,1)S(1)}, bf16[4,272,128]{2,1,0:T(8,128)(2,1)S(1)}, u32[]{:S(2)}, u32[]{:S(2)}) collective-permute-start(bf16[4,272,128]{2,1,0:T(8,128)(2,1)S(1)} %get-tuple-element.33.refs_6_.refs_0_), channel_id=1, source_target_pairs={{1,8},{9,16},{17,24},{8,1},{16,9},{24,17},{3,10},{11,18},{19,26},{... | collective-permute-start | bytes 835592 | tf_op jit(solution)/shard_map/ppermute | solution.py:832

commit v11 on v10

--- a/solution.py
+++ b/solution.py
@@ -557,7 +557,7 @@
     chunks, groups, own_heads, entries, part, hidden,
 ):
     packs, next_packs, refs = refs[:groups], refs[groups : 2 * groups], refs[2 * groups :]
-    (far_ref, qkv_ref, edge_ref, strip_ref, next_qkv, next_rows), scratch = refs[:6], refs[6:]
+    (far_ref, qkv_ref, far_qkv_ref, edge_ref, strip_ref, next_qkv, next_rows), scratch = refs[:7], refs[7:]
     cols = x_ref.shape[1]
     side = parity()
     w = Weights(packs, scratch, x_ref.shape[2], part, hidden)
@@ -580,6 +580,9 @@
     spread_message(near_ref, strip_ref)
     owns = [own_pieces(following, strip_ref, qkv_ref, span, scale) for span in chunks]
     weave(offset(threads, 3), offset(owns, 5))
+    spread_message(far_ref, strip_ref)
+    for piece in offset([own_pieces(following, strip_ref, far_qkv_ref, span, scale) for span in chunks], 1):
+        piece()
 
 
 def even_split(count, most):
@@ -630,8 +633,7 @@
     side = 1 - parity() if near else parity()
     copies = []
     if near:
-        next_in, out_ref, next_qkv, next_ref = refs[:4]
-        refs = refs[4:]
+        out_ref, refs = refs[0], refs[1:]
     else:
         done_ref, out_hbm, out_ref, sems = refs[:4]
         refs = refs[4:]
@@ -647,7 +649,6 @@
     depth = c // heads
     half = SHIFT * WIN
     tokens = WIN * WIN
-    scale = depth ** (-0.5) * LOG2E
     w = Weights(packs, scratch, c, part, hidden)
     w.load_rows()
     masks = head_masks(heads, depth, c)
@@ -746,11 +747,6 @@
         )
 
     extra = {0: [w.load_qkv, pick_bias, w.load_rest]}
-    if near:
-        spread_message(next_in, next_ref)
-        last = len(chunks) + 4
-        for n, span in enumerate(chunks):
-            extra[last - len(chunks) + n] = own_pieces(w, next_ref, next_qkv, span, scale)
     pipeline(len(chunks), extra, first, second, third)
     for copy in copies:
         copy.wait()
@@ -862,9 +858,9 @@
     chunks = even_split(tile_cols // WIN + 1, 17)
     own_qkv = jax.ShapeDtypeStruct((3, (tile_cols // WIN + 1) * SHIFT * WIN, c), BF)
     strip_wide = pltpu.VMEM((SHIFT, tile_cols + 2 * WIN, c), F32)
-    far, near_qkv = call(
+    far, near_qkv, far_qkv = call(
         lambda *refs: rest_kernel(*refs, chunks=chunks, **sizes),
-        (strip, own_qkv),
+        (strip, own_qkv, own_qkv),
         [beside, strip_wide, weights_scratch[0], weights_scratch[-1]] + weights_scratch,
         x_far, left, right, rest, ids, near, *packs0, *packs1,
     )
@@ -875,11 +871,9 @@
         pltpu.VMEM((SHIFT, tile_cols + WIN, c), F32),
         pltpu.VMEM((2, 2, most, c), BF), pltpu.VMEM((2, most, c), BF),
     ] + weights_scratch
-    near_out, far_qkv = call(
+    near_out = call(
         lambda *refs: shifted_kernel(*refs, chunks=chunks, near=True, **sizes),
-        (jax.ShapeDtypeStruct((SHIFT, tile_cols, c), BF), own_qkv),
-        [strip_wide] + scratch,
-        near, near_halo, near_qkv, rel2, *packs1, far,
+        half_tile, scratch, near, near_halo, near_qkv, rel2, *packs1,
     )
     return call(
         lambda *refs: shifted_kernel(*refs, chunks=chunks, near=False, **sizes),

time: 38.6 us -> 37.2 us (0.964)
  the two profiles are of different devices: /device:TPU:1 before, /device:TPU:14 now
where the time goes in v11:
time: 37.2 us; the launch traced here: 37 us
  Pallas kernels  18.5 us (50%)
  starting transfers between devices  12.8 us (34%)
  waiting for transfers between devices  5.4 us (15%)
    pallas_call x6, Pallas kernels, call(): pl.pallas_call(kernel, out_shape=out_shapes, scratch_shapes=scratch, comp...  18.5 us
    ppermute x2, waiting for transfers between devices, swapped(): lax.ppermute(value, ('row', 'ch'), pairs + [(j, i) for i, j in pairs])  5.39 us
    ppermute x2, starting transfers between devices, swapped(): lax.ppermute(value, ('row', 'ch'), pairs + [(j, i) for i, j in pairs])  5.2 us
    ppermute x1, starting transfers between devices, both_blocks(): right = lax.ppermute(left_edge, 'col', neighbours('col', -1))  3.64 us
    ppermute x2, starting transfers between devices, others(): found.append(lax.ppermute(found[-1], 'ch', swap))  2.09 us
    ppermute x1, starting transfers between devices, both_blocks(): left = lax.ppermute(right_edge, 'col', neighbours('col', 1))  1.91 us
  transfers between devices with their start and end apart: 6, of which 1 were waited for; matrix products, arithmetic and copies ran while one was open for 0% of the time, Pallas kernels for 33%

profile of v11, /device:TPU:14, one launch (start us, length us, event | category | flops | bytes accessed | tf_op | source)
XLA Modules:
  0.0 37.0 jit_solution(81103621128674106)
XLA Ops:
  0.0 1.4 %shard_map.136 = (bf16[816,128]{1,0:T(8,128)(2,1)S(1)}, bf16[816,128]{1,0:T(8,128)(2,1)S(1)}, bf16[9,8,128]{2,1,0:T(8,128)(2,1)S(1)}, bf16[9,8,128]{2,1,0:T(8,128)(2,1)S(1)}, s32[64,128]{1,0:T(8,128)S(1)}) custom-call(bf16[8,256,128]{2,1,0:T(8,128)(2,1)} %refs_0_.3, s32[8,256]{1,0:T(8,128)} %refs_1_.3, s32[64,64]{1,0:T(8,128)} %refs_2_.1, ...), custom_call_target="tpu_custom_call" | custom-call | tf_op jit(solution)/shard_map/pallas_call | solution.py:756
  1.4 0.6 %collective-permute-start.2 = (bf16[816,128]{1,0:T(8,128)(2,1)S(1)}, bf16[816,128]{1,0:T(8,128)(2,1)S(1)}, u32[]{:S(2)}, u32[]{:S(2)}) collective-permute-start(bf16[816,128]{1,0:T(8,128)(2,1)S(1)} %get-tuple-element.20.refs_2_.refs_6_), channel_id=1, source_target_pairs={{0,1},{1,0},{2,3},{3,2},{4,5},{5,4},{6,7},{7,6},{8,9},{9,8},{10,11... | collective-permute-start | bytes 626696 | tf_op jit(solution)/shard_map/ppermute | solution.py:789
  2.0 1.5 %collective-permute-start.3 = (bf16[816,128]{1,0:T(8,128)(2,1)S(1)}, bf16[816,128]{1,0:T(8,128)(2,1)S(1)}, u32[]{:S(2)}, u32[]{:S(2)}) collective-permute-start(bf16[816,128]{1,0:T(8,128)(2,1)S(1)} %get-tuple-element.31.refs_8_.refs_4_), channel_id=1, source_target_pairs={{0,1},{1,0},{2,3},{3,2},{4,5},{5,4},{6,7},{7,6},{8,9},{9,8},{10,11... | collective-permute-start | bytes 626696 | tf_op jit(solution)/shard_map/ppermute | solution.py:789
  3.5 1.9 %collective-permute-start = (bf16[9,8,128]{2,1,0:T(8,128)(2,1)S(1)}, bf16[9,8,128]{2,1,0:T(8,128)(2,1)S(1)}, u32[]{:S(2)}, u32[]{:S(2)}) collective-permute-start(bf16[9,8,128]{2,1,0:T(8,128)(2,1)S(1)} %get-tuple-element.22), channel_id=1, source_target_pairs={{0,2},{2,4},{4,6},{1,3},{3,5},{5,7},{8,10},{10,12},{12,14},{9,11},... | collective-permute-start | bytes 55304 | tf_op jit(solution)/shard_map/ppermute | solution.py:808
  5.5 3.6 %collective-permute-start.1 = (bf16[9,8,128]{2,1,0:T(8,128)(2,1)S(1)}, bf16[9,8,128]{2,1,0:T(8,128)(2,1)S(1)}, u32[]{:S(2)}, u32[]{:S(2)}) collective-permute-start(bf16[9,8,128]{2,1,0:T(8,128)(2,1)S(1)} %get-tuple-element.23), channel_id=1, source_target_pairs={{2,0},{4,2},{6,4},{3,1},{5,3},{7,5},{10,8},{12,10},{14,12},{11,9},... | collective-permute-start | bytes 55304 | tf_op jit(solution)/shard_map/ppermute | solution.py:809
  9.1 2.0 %shard_map.137 = (bf16[2048,128]{1,0:T(8,128)(2,1)S(1)}, bf16[4,256,128]{2,1,0:T(8,128)(2,1)S(1)}, bf16[4,256,128]{2,1,0:T(8,128)(2,1)S(1)}, s32[8,256]{1,0:T(8,128)S(1)}) custom-call(bf16[8,256,128]{2,1,0:T(8,128)(2,1)} %refs_0_.3, s32[8,256]{1,0:T(8,128)} %refs_1_.3, bf16[816,128]{1,0:T(8,128)(2,1)S(1)} %get-tuple-element.20.refs_2_.refs_6_), custom_call_target="tpu_custom_call" | custom-call | tf_op jit(solution)/shard_map/pallas_call | solution.py:756
  11.1 0.0 collective-permute-done.refs_2_.refs_1_
  11.1 0.0 collective-permute-done.1.refs_3_.refs_2_
  11.2 0.0 collective-permute-done.2.refs_7_
  11.2 3.5 %shard_map.138 = (bf16[4,272,128]{2,1,0:T(8,128)(2,1)S(1)}, bf16[1088,128]{1,0:T(8,128)(2,1)S(1)}, bf16[8,8,128]{2,1,0:T(8,128)(2,1)S(1)}) custom-call(bf16[4,256,128]{2,1,0:T(8,128)(2,1)S(1)} %get-tuple-element.24.refs_0_, s32[8,256]{1,0:T(8,128)S(1)} %get-tuple-element.25.refs_1_, bf16[9,8,128]{2,1,0:T(8,128)(2,1)S(1)} %collective-permute-done.refs_2_.refs_1_, ...), custom_call_target="tpu_custom_call" | custom-call | tf_op jit(solution)/shard_map/pallas_call | solution.py:756
  14.7 0.6 %collective-permute-start.5 = (bf16[4,272,128]{2,1,0:T(8,128)(2,1)S(1)}, bf16[4,272,128]{2,1,0:T(8,128)(2,1)S(1)}, u32[]{:S(2)}, u32[]{:S(2)}) collective-permute-start(bf16[4,272,128]{2,1,0:T(8,128)(2,1)S(1)} %get-tuple-element.30.refs_5_.refs_0_), channel_id=1, source_target_pairs={{0,1},{8,9},{16,17},{24,25},{1,0},{9,8},{17,16},{25,24},{2,3},{10,... | collective-permute-start | bytes 835592 | tf_op jit(solution)/shard_map/ppermute | solution.py:828
  15.3 0.0 collective-permute-done.3.refs_9_.refs_5_
  15.3 2.8 %shard_map.139 = (bf16[4,272,128]{2,1,0:T(8,128)(2,1)S(1)}, bf16[3,1056,128]{2,1,0:T(8,128)(2,1)S(1)}, bf16[3,1056,128]{2,1,0:T(8,128)(2,1)S(1)}) custom-call(bf16[4,256,128]{2,1,0:T(8,128)(2,1)S(1)} %get-tuple-element.21.refs_0_, bf16[9,8,128]{2,1,0:T(8,128)(2,1)S(1)} %collective-permute-done.refs_2_.refs_1_, ...), custom_call_target="tpu_custom_call" | custom-call | tf_op jit(solution)/shard_map/pallas_call | solution.py:756
  18.1 4.6 %collective-permute-start.4 = (bf16[4,272,128]{2,1,0:T(8,128)(2,1)S(1)}, bf16[4,272,128]{2,1,0:T(8,128)(2,1)S(1)}, u32[]{:S(2)}, u32[]{:S(2)}) collective-permute-start(bf16[4,272,128]{2,1,0:T(8,128)(2,1)S(1)} %get-tuple-element.32.refs_0_), channel_id=1, source_target_pairs={{1,8},{9,16},{17,24},{8,1},{16,9},{24,17},{3,10},{11,18},{19,26},{... | collective-permute-start | bytes 835592 | tf_op jit(solution)/shard_map/ppermute | solution.py:828
  22.7 5.4 %collective-permute-done.5.refs_1_ = bf16[4,272,128]{2,1,0:T(8,128)(2,1)S(1)} collective-permute-done((bf16[4,272,128]{2,1,0:T(8,128)(2,1)S(1)}, bf16[4,272,128]{2,1,0:T(8,128)(2,1)S(1)}, u32[]{:S(2)}, u32[]{:S(2)}) %collective-permute-start.5) | collective-permute-done | bytes 278560 | tf_op jit(solution)/shard_map/ppermute | solution.py:828
  28.1 4.0 %shard_map.140.refs_6_ = bf16[4,256,128]{2,1,0:T(8,128)(2,1)S(1)} custom-call(bf16[4,272,128]{2,1,0:T(8,128)(2,1)S(1)} %get-tuple-element.30.refs_5_.refs_0_, bf16[4,272,128]{2,1,0:T(8,128)(2,1)S(1)} %collective-permute-done.5.refs_1_, bf16[3,1056,128]{2,1,0:T(8,128)(2,1)S(1)} %get-tuple-element.34.refs_2_, s32[64,128]{1,0:T(8,128)S(1)} %get-tuple-element.26.refs_4_.refs_3_, ...), custom_call_target="tpu_custom_call" | custom-call | tf_op jit(solution)/shard_map/pallas_call | solution.py:756
  32.1 0.0 collective-permute-done.4.refs_1_
  32.1 4.7 %shard_map.141 = bf16[8,256,128]{2,1,0:T(8,128)(2,1)} custom-call(bf16[4,272,128]{2,1,0:T(8,128)(2,1)S(1)} %get-tuple-element.32.refs_0_, bf16[4,272,128]{2,1,0:T(8,128)(2,1)S(1)} %collective-permute-done.4.refs_1_, bf16[3,1056,128]{2,1,0:T(8,128)(2,1)S(1)} %get-tuple-element.33.refs_2_, s32[64,128]{1,0:T(8,128)S(1)} %get-tuple-element.26.refs_4_.refs_3_, ...), custom_call_target="tpu_custom_call" | custom-call | tf_op jit(solution)/shard_map/pallas_call | solution.py:756
Async XLA Ops:
  1.4 9.7 %collective-permute-start.2 = (bf16[816,128]{1,0:T(8,128)(2,1)S(1)}, bf16[816,128]{1,0:T(8,128)(2,1)S(1)}, u32[]{:S(2)}, u32[]{:S(2)}) collective-permute-start(bf16[816,128]{1,0:T(8,128)(2,1)S(1)} %get-tuple-element.20.refs_2_.refs_6_), channel_id=1, source_target_pairs={{0,1},{1,0},{2,3},{3,2},{4,5},{5,4},{6,7},{7,6},{8,9},{9,8},{10,11... | collective-permute-start | bytes 626696 | tf_op jit(solution)/shard_map/ppermute | solution.py:789
  2.0 13.3 %collective-permute-start.3 = (bf16[816,128]{1,0:T(8,128)(2,1)S(1)}, bf16[816,128]{1,0:T(8,128)(2,1)S(1)}, u32[]{:S(2)}, u32[]{:S(2)}) collective-permute-start(bf16[816,128]{1,0:T(8,128)(2,1)S(1)} %get-tuple-element.31.refs_8_.refs_4_), channel_id=1, source_target_pairs={{0,1},{1,0},{2,3},{3,2},{4,5},{5,4},{6,7},{7,6},{8,9},{9,8},{10,11... | collective-permute-start | bytes 626696 | tf_op jit(solution)/shard_map/ppermute | solution.py:789
  3.5 7.6 %collective-permute-start = (bf16[9,8,128]{2,1,0:T(8,128)(2,1)S(1)}, bf16[9,8,128]{2,1,0:T(8,128)(2,1)S(1)}, u32[]{:S(2)}, u32[]{:S(2)}) collective-permute-start(bf16[9,8,128]{2,1,0:T(8,128)(2,1)S(1)} %get-tuple-element.22), channel_id=1, source_target_pairs={{0,2},{2,4},{4,6},{1,3},{3,5},{5,7},{8,10},{10,12},{12,14},{9,11},... | collective-permute-start | bytes 55304 | tf_op jit(solution)/shard_map/ppermute | solution.py:808
  5.5 5.7 %collective-permute-start.1 = (bf16[9,8,128]{2,1,0:T(8,128)(2,1)S(1)}, bf16[9,8,128]{2,1,0:T(8,128)(2,1)S(1)}, u32[]{:S(2)}, u32[]{:S(2)}) collective-permute-start(bf16[9,8,128]{2,1,0:T(8,128)(2,1)S(1)} %get-tuple-element.23), channel_id=1, source_target_pairs={{2,0},{4,2},{6,4},{3,1},{5,3},{7,5},{10,8},{12,10},{14,12},{11,9},... | collective-permute-start | bytes 55304 | tf_op jit(solution)/shard_map/ppermute | solution.py:809
  14.7 13.4 %collective-permute-start.5 = (bf16[4,272,128]{2,1,0:T(8,128)(2,1)S(1)}, bf16[4,272,128]{2,1,0:T(8,128)(2,1)S(1)}, u32[]{:S(2)}, u32[]{:S(2)}) collective-permute-start(bf16[4,272,128]{2,1,0:T(8,128)(2,1)S(1)} %get-tuple-element.30.refs_5_.refs_0_), channel_id=1, source_target_pairs={{0,1},{8,9},{16,17},{24,25},{1,0},{9,8},{17,16},{25,24},{2,3},{10,... | collective-permute-start | bytes 835592 | tf_op jit(solution)/shard_map/ppermute | solution.py:828
  18.1 14.0 %collective-permute-start.4 = (bf16[4,272,128]{2,1,0:T(8,128)(2,1)S(1)}, bf16[4,272,128]{2,1,0:T(8,128)(2,1)S(1)}, u32[]{:S(2)}, u32[]{:S(2)}) collective-permute-start(bf16[4,272,128]{2,1,0:T(8,128)(2,1)S(1)} %get-tuple-element.32.refs_0_), channel_id=1, source_target_pairs={{1,8},{9,16},{17,24},{8,1},{16,9},{24,17},{3,10},{11,18},{19,26},{... | collective-permute-start | bytes 835592 | tf_op jit(solution)/shard_map/ppermute | solution.py:828
